TPU v7x, 512 devices: a whole 4x4x16 slice. The times are simulated.
512 devices in a mesh: dp: 64 (over z, y_lo, core), mp: 8 (over x, y_hi).
Axes of the slice: x: 4, y: 4 (y_hi: 2, y_lo: 2; y = y_hi * 2 + y_lo), z: 16, core: 2. Of those that a mesh axis runs over, the one named last changes fastest.
Arguments:
- picture_tower_vectors: bfloat16 [12288, 1152], P('dp'), may hold values from -6 to 6
- caption_tower_vectors: bfloat16 [12288, 1152], P('dp', 'mp'), may hold values from -6 to 6
- picture_standardize_factor: float32 [1152], replicated, may hold values from 0.1 to 1.9
- picture_entry_matrix: bfloat16 [1152, 4304], P(None, 'mp'), may hold values from -0.1875 to 0.1875
- picture_exit_matrix: bfloat16 [4304, 1152], P('mp'), may hold values from -0.09375 to 0.09375
- caption_mapping_matrix: bfloat16 [1152, 1152], P('mp'), may hold values from -1 to 1
- energy_multiplier: float32 [], replicated, may hold values from 4 to 16
- energy_offset_term: float32 [], replicated, may hold values from -2 to -0.5
Outputs:
- grad_image: float32 [12288, 1152], P('dp', 'mp')
- grad_text: float32 [12288, 1152], P('dp', 'mp')
All inputs are finite; a program needn't handle non-finite values.
Results may differ from a plain program's by a relative error of at most 0.0046.
Values may be sent and summed in bfloat16 or wider, within the bound.
No kernel may reach another device: no remote copies, remote signals or barrier semaphores. Data moves between devices by JAX's collectives and lax.ppermute only.
A program may use at most 64 MiB of HBM per device.

v0:
```python
import jax
import jax.numpy as jnp
from jax import lax
from jax.sharding import Mesh
from jax.sharding import PartitionSpec as P


DP = ("zh", "zl", "yl", "c")
MP = ("x", "yh")
Z = ("zh", "zl")
XY = ("yl", "x", "yh")
NEAR = (-2, -1, 1, 2)
FAR = 5
F32 = jnp.float32
BF16 = jnp.bfloat16


def swap(array, axes):
    return lax.all_to_all(array, axes, 0, 0, tiled=True)


def exchange(array, axes, k):
    n = lax.axis_size(axes)
    return lax.ppermute(array, axes, [(i, i ^ k) for i in range(n)])


def spread(array, axes):
    n = lax.axis_size(axes)
    copies = jnp.broadcast_to(array[None], (n, *array.shape))
    return swap(copies, axes).reshape(n * array.shape[0], *array.shape[1:])


def summed_at(array, axes):
    n = lax.axis_size(axes)
    parts = array.reshape(n, array.shape[0] // n, *array.shape[1:])
    return jnp.sum(swap(parts, axes).astype(F32), axis=0)


def shift(array, axes, k):
    n = lax.axis_size(axes)
    return lax.ppermute(array, axes, [(i, (i + k) % n) for i in range(n)])


def gather(array, axes):
    return lax.all_gather(array, axes, axis=0, tiled=True)


def gathered_from_own(array):
    high, low = (lax.axis_size(a) for a in Z)
    rows = array.shape[0]
    spaced = gather(array, "zh")
    parts = gather(spaced, "zl").reshape(low, high, rows, -1)
    in_line = parts.transpose(1, 0, 2, 3).reshape(high * low * rows, -1)
    twice = jnp.concatenate([in_line, in_line], axis=0)
    return lax.dynamic_slice_in_dim(twice, lax.axis_index(Z) * rows, in_line.shape[0], 0)


def sum_over_line(array, share):
    n = lax.axis_size(Z)
    half = n // 2

    def block(k):
        first = (k % n) * share
        return array[first : first + share]

    own = [block(0), block(FAR), block(-FAR)]
    arrived = []
    for b in NEAR:
        parts = [block(b), block(b + FAR), block(b - FAR)]
        arrived.append(shift(jnp.concatenate(parts, axis=0).astype(BF16), Z, b))
    last = shift(block(half).astype(BF16), Z, half - FAR).astype(F32)
    sums = []
    for place in range(3):
        total = own[place]
        for piece in arrived:
            total = total + piece[place * share : (place + 1) * share].astype(F32)
        sums.append(total)
    up = shift((sums[1] + last).astype(BF16), Z, FAR)
    down = shift(sums[2].astype(BF16), Z, -FAR)
    return sums[0] + up.astype(F32) + down.astype(F32)


def gelu_tanh(values):
    return jax.nn.gelu(values, approximate=True)


def norm_back(upstream, unit_rows, inverse):
    unit_float = unit_rows.astype(F32)
    along = jnp.sum(unit_float * upstream, axis=-1, keepdims=True)
    return inverse * (upstream - unit_float * along)


def dot(a, b, dims):
    return lax.dot_general(a, b, (dims, ((), ())), preferred_element_type=F32)


def per_device(picture, caption, gain, entry, exit_matrix, mapping, scale, offset):
    rows = picture.shape[0]
    width = picture.shape[1]
    heads = lax.axis_size(MP)
    head_pos = lax.axis_index(MP)
    share = rows // heads
    cols = caption.shape[1]
    first_row = head_pos * share
    first_col = head_pos * cols
    text_part = dot(caption, mapping, ((1,), (0,))).astype(BF16)
    text_out = summed_at(text_part, MP)
    inv_text = lax.rsqrt(jnp.sum(text_out * text_out, axis=-1, keepdims=True) + 1e-06)
    unit_text = (text_out * inv_text).astype(BF16)

    image_float = picture.astype(F32)
    mean_row = jnp.mean(image_float, axis=-1, keepdims=True)
    variance = jnp.mean((image_float - mean_row) ** 2, axis=-1, keepdims=True)
    inv_std = lax.rsqrt(variance + 1e-06)
    centred = (image_float - mean_row) * inv_std
    normed = (centred * gain).astype(BF16)
    preact = dot(normed, entry, ((1,), (0,)))
    hidden = gelu_tanh(preact).astype(BF16)
    partial_out = dot(hidden, exit_matrix, ((1,), (0,))).astype(BF16)
    own_rows = lax.dynamic_slice_in_dim(picture, first_row, share, 0).astype(F32)
    image_out = own_rows + summed_at(partial_out, MP)
    inv_image = lax.rsqrt(jnp.sum(image_out * image_out, axis=-1, keepdims=True) + 1e-06)
    unit_image = (image_out * inv_image).astype(BF16)

    line = gathered_from_own(unit_text)
    texts = jnp.concatenate([line, exchange(line, "c", 1)], axis=0)
    images = spread(unit_image, XY)

    own_start = lax.axis_index(XY) * share
    text_ids = jnp.arange(texts.shape[0], dtype=jnp.int32)[:, None]
    image_ids = jnp.arange(images.shape[0], dtype=jnp.int32)[None, :] - own_start
    same = (text_ids == image_ids) & (text_ids < share)
    energies = scale * dot(texts, images, ((1,), (1,))) + offset
    polarity = jnp.where(same, 1.0, -1.0).astype(F32)
    weighted = (scale * -polarity * jax.nn.sigmoid(-polarity * energies)).astype(BF16)
    text_add = dot(weighted, images, ((1,), (0,)))
    image_add = dot(weighted, texts, ((0,), (0,)))

    image_parts = swap(image_add.astype(BF16).reshape(-1, share, width), XY)
    image_dir = jnp.sum(image_parts.astype(F32), axis=0)
    grad_share = norm_back(image_dir, unit_image, inv_image).astype(BF16)
    grad_out_b = spread(grad_share, MP)

    middle = text_add.shape[0] // 2
    swapped = exchange(text_add[middle:].astype(BF16), "c", 1)
    text_half = text_add[:middle] + swapped.astype(F32)
    text_dir = sum_over_line(text_half, share)
    grad_text_share = norm_back(text_dir, unit_text, inv_text).astype(BF16)

    grad_hidden = dot(grad_out_b, exit_matrix, ((1,), (1,)))
    _, pull_back = jax.vjp(gelu_tanh, preact)
    grad_pre = pull_back(grad_hidden)[0].astype(BF16)
    partial_normed = dot(grad_pre, entry, ((1,), (1,)))
    scaled_part = partial_normed * gain
    sums = jnp.stack(
        [jnp.sum(scaled_part, axis=-1), jnp.sum(scaled_part * centred, axis=-1)], axis=-1
    )
    sums_high = lax.reduce_precision(sums, 8, 7)
    sums_low = sums - sums_high
    sums_both = jnp.concatenate([sums_high, sums_low], axis=-1).astype(BF16)
    blocks = partial_normed.astype(BF16).reshape(rows, heads, cols).transpose(1, 0, 2)
    packed = jnp.concatenate(
        [blocks, jnp.broadcast_to(sums_both[None], (heads, *sums_both.shape))], axis=2
    )
    arrived = jnp.sum(swap(packed, MP).astype(F32), axis=0)
    means = (arrived[:, cols : cols + 2] + arrived[:, cols + 2 :]) / width
    gain_here = lax.dynamic_slice_in_dim(gain, first_col, cols, 0)
    feature = jnp.arange(width, dtype=jnp.int32)[:, None] - first_col
    chosen = (feature == jnp.arange(cols, dtype=jnp.int32)[None, :]).astype(BF16)
    picture_here = dot(picture, chosen, ((1,), (0,)))
    centred_here = (picture_here - mean_row) * inv_std
    grad_out_here = dot(grad_out_b, chosen, ((1,), (0,)))
    scaled = arrived[:, :cols] * gain_here
    grad_image = grad_out_here + inv_std * (
        scaled - means[:, :1] - centred_here * means[:, 1:]
    )
    grad_text = dot(spread(grad_text_share, MP), mapping, ((1,), (1,)))
    return (grad_image, grad_text)


def solution(mesh):
    split = Mesh(mesh.devices.reshape(4, 4, 2, 2, 4, 2), (*DP, *MP))
    in_specs = (
        P(DP, None),
        P(DP, MP),
        P(),
        P(None, MP),
        P(MP, None),
        P(MP, None),
        P(),
        P(),
    )
    out_specs = (P(DP, MP), P(DP, MP))
    return jax.shard_map(
        per_device, mesh=split, in_specs=in_specs, out_specs=out_specs, check_vma=False
    )
```

profile of v0, /device:TPU:2, one launch (start us, length us, event | category | flops | bytes accessed | tf_op | source)
XLA Modules:
  0.0 200.9 jit_solution(10063359031724581272)
XLA Ops:
  0.6 0.0 copy-start
  0.7 2.2 %convolution_convert_fusion.1 = bf16[192,1152]{1,0:T(8,128)(2,1)} fusion(bf16[192,144]{0,1:T(8,128)(2,1)} %param.9, bf16[144,1152]{1,0:T(8,128)(2,1)} %param.13), kind=kOutput, calls=%fused_computation.1 | convolution fusion | flops 63922176 | bytes 829440 | tf_op jit(solution)/shard_map/dot_general | solution.py:94
  2.9 9.3 %all-to-all-start.1 = ((bf16[8,24,1152]{2,1,0:T(8,128)(2,1)}), bf16[8,24,1152]{2,1,0:T(8,128)(2,1)S(1)}, u32[]{:S(2)}, u32[]{:S(2)}) async-start(bf16[8,24,1152]{2,1,0:T(8,128)(2,1)} %bitcast.1), calls=%async_computation.1 | async-start | bytes 884736 | tf_op jit(solution)/shard_map/all_to_all | solution.py:19
  12.2 0.1 convert_reduce_fusion.2
  12.3 0.3 fusion.23
  12.6 2.0 fusion.35
  14.6 1.3 convolution_convert_fusion.2
  15.9 3.9 %all-to-all-done.1 = bf16[8,24,1152]{2,1,0:T(8,128)(2,1)S(1)} async-done(((bf16[8,24,1152]{2,1,0:T(8,128)(2,1)}), bf16[8,24,1152]{2,1,0:T(8,128)(2,1)S(1)}, u32[]{:S(2)}, u32[]{:S(2)}) %all-to-all-start.1) | async-done | bytes 442400 | tf_op jit(solution)/shard_map/all_to_all | solution.py:19
  19.8 4.9 %all-to-all-start = ((bf16[8,24,1152]{2,1,0:T(8,128)(2,1)}), bf16[8,24,1152]{2,1,0:T(8,128)(2,1)S(1)}, u32[]{:S(2)}, u32[]{:S(2)}) async-start(bf16[8,24,1152]{2,1,0:T(8,128)(2,1)} %bitcast), calls=%async_computation | async-start | bytes 884736 | tf_op jit(solution)/shard_map/all_to_all | solution.py:19
  24.7 0.1 convert_reduce_fusion.3
  24.8 0.1 multiply_reduce_fusion.1
  24.9 0.1 multiply_convert_fusion.3
  25.0 25.4 %all_gather.6 = bf16[96,1152]{1,0:T(8,128)(2,1)S(1)} all-gather(bf16[24,1152]{1,0:T(8,128)(2,1)S(1)} %multiply_convert_fusion.3), channel_id=1, replica_groups=mesh['zh'=4,'zl'=4,'yl'=2,'c'=2,'x'=4,'yh'=2] {'zh'}, dimensions={0}, use_global_device_ids=true | all-gather | bytes 276480 | tf_op jit(solution)/shard_map/all_gather | solution.py:45
  50.4 0.1 convert_reduce_fusion.4
  50.4 0.1 multiply_reduce_fusion.2
  50.6 18.7 %all_gather.7 = bf16[384,1152]{1,0:T(8,128)(2,1)S(1)} all-gather(bf16[96,1152]{1,0:T(8,128)(2,1)S(1)} %all_gather.6), channel_id=1, replica_groups=mesh['zh'=4,'zl'=4,'yl'=2,'c'=2,'x'=4,'yh'=2] {'zl'}, dimensions={0}, use_global_device_ids=true | all-gather | bytes 1105920 | tf_op jit(solution)/shard_map/all_gather | solution.py:45
  69.3 0.1 copy.10
  69.4 1.9 fusion.24
  71.3 1.9 collective-permute-start
  73.2 0.1 multiply_convert_fusion.2
  73.3 1.0 broadcast_in_dim.18
  74.3 7.2 %all-to-all-start.2 = ((bf16[16,24,1152]{2,1,0:T(8,128)(2,1)}), bf16[16,24,1152]{2,1,0:T(8,128)(2,1)S(1)}, u32[]{:S(2)}, u32[]{:S(2)}) async-start(bf16[16,24,1152]{2,1,0:T(8,128)(2,1)} %broadcast_in_dim.18), calls=%async_computation.2 | async-start | bytes 1769472 | tf_op jit(solution)/shard_map/all_to_all | solution.py:19
  82.7 14.8 %all-to-all-done.2 = bf16[16,24,1152]{2,1,0:T(8,128)(2,1)S(1)} async-done(((bf16[16,24,1152]{2,1,0:T(8,128)(2,1)}), bf16[16,24,1152]{2,1,0:T(8,128)(2,1)S(1)}, u32[]{:S(2)}, u32[]{:S(2)}) %all-to-all-start.2) | async-done | bytes 884768 | tf_op jit(solution)/shard_map/all_to_all | solution.py:19
  97.5 0.0 collective-permute-done
  97.5 2.9 %fusion.7 = bf16[768,384]{1,0:T(8,128)(2,1)S(1)} fusion(bf16[384,1152]{1,0:T(8,128)(2,1)S(1)} %bitcast.42, bf16[384,1152]{1,0:T(8,128)(2,1)} %collective-permute-done, bf16[384,1152]{1,0:T(8,128)(2,1)} %fusion.24, f32[]{:T(128)S(6)} %copy.13, s32[384]{0:T(512)S(1)} %iota_subtract_fusion.1, f32[]{:T(128)S(6)} %copy.12, pred[768]{0:T(1024)(128)(4,1)S(1)} %iota_compare_fusion.3), kind=kOutput, calls=%fused_computation.17 | convolution fusion | flops 686850048 | bytes 3246344 | tf_op jit(solution)/shard_map/dot_general | solution.py:94
  100.4 1.1 fusion.95
  101.5 1.7 copy-done.1
  103.3 1.0 slice.243
  104.3 1.9 collective-permute-start.1
  106.2 0.1 dynamic_slice.11
  106.3 3.4 %convolution_convert_fusion = bf16[384,1152]{1,0:T(8,128)(2,1)} fusion(bf16[768,384]{1,0:T(8,128)(2,1)S(1)} %fusion.7, bf16[384,1152]{1,0:T(8,128)(2,1)} %collective-permute-done, bf16[384,1152]{1,0:T(8,128)(2,1)} %fusion.24), kind=kOutput, calls=%fused_computation | convolution fusion | flops 683458560 | bytes 3244032 | tf_op jit(solution)/shard_map/dot_general | solution.py:94
  109.7 5.4 %all-to-all-start.3 = ((bf16[16,24,1152]{2,1,0:T(8,128)(2,1)}), bf16[16,24,1152]{2,1,0:T(8,128)(2,1)S(1)}, u32[]{:S(2)}, u32[]{:S(2)}) async-start(bf16[16,24,1152]{2,1,0:T(8,128)(2,1)} %bitcast.46), calls=%async_computation.3 | async-start | bytes 1769472 | tf_op jit(solution)/shard_map/all_to_all | solution.py:19
  115.1 3.2 %fusion.90 = (bf16[384,1152]{1,0:T(8,128)(2,1)S(1)}, f32[384,1152]{1,0:T(8,128)}) fusion(bf16[384,1152]{1,0:T(8,128)(2,1)} %collective-permute-done.1, f32[768,1152]{1,0:T(8,128)} %copy-done.1), kind=kLoop, calls=%fused_computation.138 | loop fusion | flops 1327104 | bytes 5308416 | tf_op jit(solution)/shard_map/convert.24
  118.3 0.1 fusion.91
  118.3 2.9 %collective-permute-start.2 = (bf16[72,1152]{1,0:T(8,128)(2,1)S(1)}, bf16[72,1152]{1,0:T(8,128)(2,1)}, u32[]{:S(2)}, u32[]{:S(2)}) collective-permute-start(bf16[72,1152]{1,0:T(8,128)(2,1)S(1)} %pad_maximum_fusion.4), channel_id=1, source_target_pairs={{0,448},{32,480},{64,0},{96,32},{128,64},{160,96},{192,128},{224,1... | collective-permute-start | bytes 497672 | tf_op jit(solution)/shard_map/ppermute | solution.py:41
  121.3 2.8 %collective-permute-start.3 = (bf16[72,1152]{1,0:T(8,128)(2,1)S(1)}, bf16[72,1152]{1,0:T(8,128)(2,1)}, u32[]{:S(2)}, u32[]{:S(2)}) collective-permute-start(bf16[72,1152]{1,0:T(8,128)(2,1)S(1)} %pad_maximum_fusion.5), channel_id=1, source_target_pairs={{0,480},{32,0},{64,32},{96,64},{128,96},{160,128},{192,160},{224,1... | collective-permute-start | bytes 497672 | tf_op jit(solution)/shard_map/ppermute | solution.py:41
  124.1 3.1 %collective-permute-start.4 = (bf16[72,1152]{1,0:T(8,128)(2,1)S(1)}, bf16[72,1152]{1,0:T(8,128)(2,1)}, u32[]{:S(2)}, u32[]{:S(2)}) collective-permute-start(bf16[72,1152]{1,0:T(8,128)(2,1)S(1)} %pad_maximum_fusion.6), channel_id=1, source_target_pairs={{0,32},{32,64},{64,96},{96,128},{128,160},{160,192},{192,224},{224... | collective-permute-start | bytes 497672 | tf_op jit(solution)/shard_map/ppermute | solution.py:41
  127.3 3.7 %collective-permute-start.5 = (bf16[72,1152]{1,0:T(8,128)(2,1)S(1)}, bf16[72,1152]{1,0:T(8,128)(2,1)}, u32[]{:S(2)}, u32[]{:S(2)}) collective-permute-start(bf16[72,1152]{1,0:T(8,128)(2,1)S(1)} %pad_maximum_fusion.7), channel_id=1, source_target_pairs={{0,64},{32,96},{64,128},{96,160},{128,192},{160,224},{192,256},{22... | collective-permute-start | bytes 497672 | tf_op jit(solution)/shard_map/ppermute | solution.py:41
  131.0 0.1 all-to-all-done.3
  131.2 0.1 convert_reduce_fusion
  131.3 5.0 %collective-permute-start.6 = (bf16[24,1152]{1,0:T(8,128)(2,1)S(1)}, bf16[24,1152]{1,0:T(8,128)(2,1)S(1)}, u32[]{:S(2)}, u32[]{:S(2)}) collective-permute-start(bf16[24,1152]{1,0:T(8,128)(2,1)S(1)} %get-tuple-element.10), channel_id=1, source_target_pairs={{0,96},{32,128},{64,160},{96,192},{128,224},{160,256},{192,288},{2... | collective-permute-start | bytes 165896 | tf_op jit(solution)/shard_map/ppermute | solution.py:41
  136.3 0.1 fusion.53
  136.4 7.0 %collective-permute-done.6 = bf16[24,1152]{1,0:T(8,128)(2,1)S(1)} collective-permute-done((bf16[24,1152]{1,0:T(8,128)(2,1)S(1)}, bf16[24,1152]{1,0:T(8,128)(2,1)S(1)}, u32[]{:S(2)}, u32[]{:S(2)}) %collective-permute-start.6) | collective-permute-done | bytes 55328 | tf_op jit(solution)/shard_map/ppermute | solution.py:41
  143.4 1.2 fusion.69
  144.6 6.4 %collective-permute-start.7 = (bf16[24,1152]{1,0:T(8,128)(2,1)S(1)}, bf16[24,1152]{1,0:T(8,128)(2,1)S(1)}, u32[]{:S(2)}, u32[]{:S(2)}) collective-permute-start(bf16[24,1152]{1,0:T(8,128)(2,1)S(1)} %get-tuple-element.8), channel_id=1, source_target_pairs={{0,160},{32,192},{64,224},{96,256},{128,288},{160,320},{192,352},{... | collective-permute-start | bytes 165896 | tf_op jit(solution)/shard_map/ppermute | solution.py:41
  151.0 5.5 %collective-permute-start.8 = (bf16[24,1152]{1,0:T(8,128)(2,1)S(1)}, bf16[24,1152]{1,0:T(8,128)(2,1)S(1)}, u32[]{:S(2)}, u32[]{:S(2)}) collective-permute-start(bf16[24,1152]{1,0:T(8,128)(2,1)S(1)} %get-tuple-element.9), channel_id=1, source_target_pairs={{0,352},{32,384},{64,416},{96,448},{128,480},{160,0},{192,32},{224... | collective-permute-start | bytes 165896 | tf_op jit(solution)/shard_map/ppermute | solution.py:41
  156.5 0.1 fusion.56
  156.6 0.8 broadcast_in_dim.19
  157.4 7.2 %all-to-all-start.4 = ((bf16[8,24,1152]{2,1,0:T(8,128)(2,1)}), bf16[8,24,1152]{2,1,0:T(8,128)(2,1)S(1)}, u32[]{:S(2)}, u32[]{:S(2)}) async-start(bf16[8,24,1152]{2,1,0:T(8,128)(2,1)} %broadcast_in_dim.19), calls=%async_computation.4 | async-start | bytes 884736 | tf_op jit(solution)/shard_map/all_to_all | solution.py:19
  164.6 1.2 fusion.57
  165.8 0.1 fusion.60
  165.9 6.4 %all-to-all-done.4 = bf16[8,24,1152]{2,1,0:T(8,128)(2,1)S(1)} async-done(((bf16[8,24,1152]{2,1,0:T(8,128)(2,1)}), bf16[8,24,1152]{2,1,0:T(8,128)(2,1)S(1)}, u32[]{:S(2)}, u32[]{:S(2)}) %all-to-all-start.4) | async-done | bytes 442400 | tf_op jit(solution)/shard_map/all_to_all | solution.py:19
  172.2 0.9 broadcast_in_dim.21
  173.1 4.9 %all-to-all-start.6 = ((bf16[8,24,1152]{2,1,0:T(8,128)(2,1)}), bf16[8,24,1152]{2,1,0:T(8,128)(2,1)S(1)}, u32[]{:S(2)}, u32[]{:S(2)}) async-start(bf16[8,24,1152]{2,1,0:T(8,128)(2,1)} %broadcast_in_dim.21), calls=%async_computation.6 | async-start | bytes 884736 | tf_op jit(solution)/shard_map/all_to_all | solution.py:19
  178.0 2.9 %multiply_reduce_fusion = (f32[192]{0:T(256)S(1)}, f32[192]{0:T(256)S(1)}, bf16[192,1152]{1,0:T(8,128)(2,1)S(1)}) fusion(f32[1152]{0:T(1024)S(1)} %copy-done.5, f32[192]{0:T(256)S(1)} %add_rsqrt_fusion, f32[192]{0:T(256)S(1)} %broadcast_multiply_fusion, bf16[192,1152]{1,0:T(8,128)(2,1)S(1)} %copy-done.2, bf16[1152,538]{0,1:T(8,128)(2,1)} %param.11, ...), kind=kOutput, calls=%fused_computation.43 | convolution fusion | flops 479822976 | bytes 4227072 | tf_op jit(solution)/shard_map/dot_general | solution.py:94
  180.8 0.2 copy.11
  181.2 0.9 pad_maximum_fusion.3
  182.1 3.5 %all-to-all-done.6 = bf16[8,24,1152]{2,1,0:T(8,128)(2,1)S(1)} async-done(((bf16[8,24,1152]{2,1,0:T(8,128)(2,1)}), bf16[8,24,1152]{2,1,0:T(8,128)(2,1)S(1)}, u32[]{:S(2)}, u32[]{:S(2)}) %all-to-all-start.6) | async-done | bytes 442400 | tf_op jit(solution)/shard_map/all_to_all | solution.py:19
  185.6 5.0 %all-to-all-start.5 = ((bf16[8,192,148]{1,2,0:T(8,128)(2,1)}), bf16[8,192,148]{1,2,0:T(8,128)(2,1)S(1)}, u32[]{:S(2)}, u32[]{:S(2)}) async-start(bf16[8,192,148]{1,2,0:T(8,128)(2,1)} %pad_maximum_fusion.3), calls=%async_computation.5 | async-start | bytes 1245184 | tf_op jit(solution)/shard_map/all_to_all | solution.py:19
  190.6 1.7 fusion.9
  192.3 1.0 fusion.96
  193.3 6.2 %all-to-all-done.5 = bf16[8,192,148]{1,2,0:T(8,128)(2,1)S(1)} async-done(((bf16[8,192,148]{1,2,0:T(8,128)(2,1)}), bf16[8,192,148]{1,2,0:T(8,128)(2,1)S(1)}, u32[]{:S(2)}, u32[]{:S(2)}) %all-to-all-start.5) | async-done | bytes 454688 | tf_op jit(solution)/shard_map/all_to_all | solution.py:19
  199.5 0.1 convert_reduce_fusion.1
  199.6 1.3 fusion.16
  (36 shorter events, 0.2 us)
Async XLA Ops:
  0.6 14.0 %copy-start = (bf16[538,1152]{1,0:T(8,128)(2,1)S(1)}, bf16[538,1152]{1,0:T(8,128)(2,1)}, u32[]{:S(2)}) copy-start(bf16[538,1152]{1,0:T(8,128)(2,1)} %param.12) | copy-start | bytes 3718660
  0.6 11.5 %copy-start.2 = (bf16[192,1152]{1,0:T(8,128)(2,1)S(1)}, bf16[192,1152]{1,0:T(8,128)(2,1)}, u32[]{:S(2)}) copy-start(bf16[192,1152]{1,0:T(8,128)(2,1)} %param.8) | copy-start | bytes 1327108
  0.7 11.9 %copy-start.5 = (f32[1152]{0:T(1024)S(1)}, f32[1152]{0:T(1024)}, u32[]{:S(2)}) copy-start(f32[1152]{0:T(1024)} %param.10) | copy-start | bytes 13828
  2.9 16.9 %all-to-all-start.1 = ((bf16[8,24,1152]{2,1,0:T(8,128)(2,1)}), bf16[8,24,1152]{2,1,0:T(8,128)(2,1)S(1)}, u32[]{:S(2)}, u32[]{:S(2)}) async-start(bf16[8,24,1152]{2,1,0:T(8,128)(2,1)} %bitcast.1), calls=%async_computation.1 | async-start | bytes 884736 | tf_op jit(solution)/shard_map/all_to_all | solution.py:19
  14.6 1.4 copy-start.6
  19.8 30.5 %all-to-all-start = ((bf16[8,24,1152]{2,1,0:T(8,128)(2,1)}), bf16[8,24,1152]{2,1,0:T(8,128)(2,1)S(1)}, u32[]{:S(2)}, u32[]{:S(2)}) async-start(bf16[8,24,1152]{2,1,0:T(8,128)(2,1)} %bitcast), calls=%async_computation | async-start | bytes 884736 | tf_op jit(solution)/shard_map/all_to_all | solution.py:19
  71.3 26.2 %collective-permute-start = (bf16[384,1152]{1,0:T(8,128)(2,1)}, bf16[384,1152]{1,0:T(8,128)(2,1)}, u32[]{:S(2)}, u32[]{:S(2)}) collective-permute-start(bf16[384,1152]{1,0:T(8,128)(2,1)} %fusion.24), channel_id=1, source_target_pairs={{0,8},{8,0},{1,9},{9,1},{2,10},{10,2},{3,11},{11,3},{4,12},{12,4},... | collective-permute-start | bytes 2654216 | tf_op jit(solution)/shard_map/ppermute | solution.py:24
  74.3 23.2 %all-to-all-start.2 = ((bf16[16,24,1152]{2,1,0:T(8,128)(2,1)}), bf16[16,24,1152]{2,1,0:T(8,128)(2,1)S(1)}, u32[]{:S(2)}, u32[]{:S(2)}) async-start(bf16[16,24,1152]{2,1,0:T(8,128)(2,1)} %broadcast_in_dim.18), calls=%async_computation.2 | async-start | bytes 1769472 | tf_op jit(solution)/shard_map/all_to_all | solution.py:19
  101.5 1.7 copy-start.1
  104.3 10.8 %collective-permute-start.1 = (bf16[384,1152]{1,0:T(8,128)(2,1)}, bf16[384,1152]{1,0:T(8,128)(2,1)}, u32[]{:S(2)}, u32[]{:S(2)}) collective-permute-start(bf16[384,1152]{1,0:T(8,128)(2,1)} %slice.243), channel_id=1, source_target_pairs={{0,8},{8,0},{1,9},{9,1},{2,10},{10,2},{3,11},{11,3},{4,12},{12,4},... | collective-permute-start | bytes 2654216 | tf_op jit(solution)/shard_map/ppermute | solution.py:24
  109.7 21.5 %all-to-all-start.3 = ((bf16[16,24,1152]{2,1,0:T(8,128)(2,1)}), bf16[16,24,1152]{2,1,0:T(8,128)(2,1)S(1)}, u32[]{:S(2)}, u32[]{:S(2)}) async-start(bf16[16,24,1152]{2,1,0:T(8,128)(2,1)} %bitcast.46), calls=%async_computation.3 | async-start | bytes 1769472 | tf_op jit(solution)/shard_map/all_to_all | solution.py:19
  118.3 25.1 %collective-permute-start.2 = (bf16[72,1152]{1,0:T(8,128)(2,1)S(1)}, bf16[72,1152]{1,0:T(8,128)(2,1)}, u32[]{:S(2)}, u32[]{:S(2)}) collective-permute-start(bf16[72,1152]{1,0:T(8,128)(2,1)S(1)} %pad_maximum_fusion.4), channel_id=1, source_target_pairs={{0,448},{32,480},{64,0},{96,32},{128,64},{160,96},{192,128},{224,1... | collective-permute-start | bytes 497672 | tf_op jit(solution)/shard_map/ppermute | solution.py:41
  121.3 22.1 %collective-permute-start.3 = (bf16[72,1152]{1,0:T(8,128)(2,1)S(1)}, bf16[72,1152]{1,0:T(8,128)(2,1)}, u32[]{:S(2)}, u32[]{:S(2)}) collective-permute-start(bf16[72,1152]{1,0:T(8,128)(2,1)S(1)} %pad_maximum_fusion.5), channel_id=1, source_target_pairs={{0,480},{32,0},{64,32},{96,64},{128,96},{160,128},{192,160},{224,1... | collective-permute-start | bytes 497672 | tf_op jit(solution)/shard_map/ppermute | solution.py:41
  124.1 19.3 %collective-permute-start.4 = (bf16[72,1152]{1,0:T(8,128)(2,1)S(1)}, bf16[72,1152]{1,0:T(8,128)(2,1)}, u32[]{:S(2)}, u32[]{:S(2)}) collective-permute-start(bf16[72,1152]{1,0:T(8,128)(2,1)S(1)} %pad_maximum_fusion.6), channel_id=1, source_target_pairs={{0,32},{32,64},{64,96},{96,128},{128,160},{160,192},{192,224},{224... | collective-permute-start | bytes 497672 | tf_op jit(solution)/shard_map/ppermute | solution.py:41
  127.3 16.1 %collective-permute-start.5 = (bf16[72,1152]{1,0:T(8,128)(2,1)S(1)}, bf16[72,1152]{1,0:T(8,128)(2,1)}, u32[]{:S(2)}, u32[]{:S(2)}) collective-permute-start(bf16[72,1152]{1,0:T(8,128)(2,1)S(1)} %pad_maximum_fusion.7), channel_id=1, source_target_pairs={{0,64},{32,96},{64,128},{96,160},{128,192},{160,224},{192,256},{22... | collective-permute-start | bytes 497672 | tf_op jit(solution)/shard_map/ppermute | solution.py:41
  131.3 12.1 %collective-permute-start.6 = (bf16[24,1152]{1,0:T(8,128)(2,1)S(1)}, bf16[24,1152]{1,0:T(8,128)(2,1)S(1)}, u32[]{:S(2)}, u32[]{:S(2)}) collective-permute-start(bf16[24,1152]{1,0:T(8,128)(2,1)S(1)} %get-tuple-element.10), channel_id=1, source_target_pairs={{0,96},{32,128},{64,160},{96,192},{128,224},{160,256},{192,288},{2... | collective-permute-start | bytes 165896 | tf_op jit(solution)/shard_map/ppermute | solution.py:41
  144.6 20.0 %collective-permute-start.7 = (bf16[24,1152]{1,0:T(8,128)(2,1)S(1)}, bf16[24,1152]{1,0:T(8,128)(2,1)S(1)}, u32[]{:S(2)}, u32[]{:S(2)}) collective-permute-start(bf16[24,1152]{1,0:T(8,128)(2,1)S(1)} %get-tuple-element.8), channel_id=1, source_target_pairs={{0,160},{32,192},{64,224},{96,256},{128,288},{160,320},{192,352},{... | collective-permute-start | bytes 165896 | tf_op jit(solution)/shard_map/ppermute | solution.py:41
  151.0 13.6 %collective-permute-start.8 = (bf16[24,1152]{1,0:T(8,128)(2,1)S(1)}, bf16[24,1152]{1,0:T(8,128)(2,1)S(1)}, u32[]{:S(2)}, u32[]{:S(2)}) collective-permute-start(bf16[24,1152]{1,0:T(8,128)(2,1)S(1)} %get-tuple-element.9), channel_id=1, source_target_pairs={{0,352},{32,384},{64,416},{96,448},{128,480},{160,0},{192,32},{224... | collective-permute-start | bytes 165896 | tf_op jit(solution)/shard_map/ppermute | solution.py:41
  157.4 14.9 %all-to-all-start.4 = ((bf16[8,24,1152]{2,1,0:T(8,128)(2,1)}), bf16[8,24,1152]{2,1,0:T(8,128)(2,1)S(1)}, u32[]{:S(2)}, u32[]{:S(2)}) async-start(bf16[8,24,1152]{2,1,0:T(8,128)(2,1)} %broadcast_in_dim.19), calls=%async_computation.4 | async-start | bytes 884736 | tf_op jit(solution)/shard_map/all_to_all | solution.py:19
  172.2 8.6 %copy-start.4 = (bf16[8,24,1152]{2,1,0:T(8,128)(2,1)}, bf16[8,24,1152]{2,1,0:T(8,128)(2,1)S(1)}, u32[]{:S(2)}) copy-start(bf16[8,24,1152]{2,1,0:T(8,128)(2,1)S(1)} %all-to-all-done.4) | copy-start | bytes 1327108
  173.1 12.5 %all-to-all-start.6 = ((bf16[8,24,1152]{2,1,0:T(8,128)(2,1)}), bf16[8,24,1152]{2,1,0:T(8,128)(2,1)S(1)}, u32[]{:S(2)}, u32[]{:S(2)}) async-start(bf16[8,24,1152]{2,1,0:T(8,128)(2,1)} %broadcast_in_dim.21), calls=%async_computation.6 | async-start | bytes 884736 | tf_op jit(solution)/shard_map/all_to_all | solution.py:19
  182.1 10.2 %copy-start.3 = (bf16[144,1152]{1,0:T(8,128)(2,1)S(1)}, bf16[144,1152]{1,0:T(8,128)(2,1)}, u32[]{:S(2)}) copy-start(bf16[144,1152]{1,0:T(8,128)(2,1)} %param.13) | copy-start | bytes 995332
  185.6 13.8 %all-to-all-start.5 = ((bf16[8,192,148]{1,2,0:T(8,128)(2,1)}), bf16[8,192,148]{1,2,0:T(8,128)(2,1)S(1)}, u32[]{:S(2)}, u32[]{:S(2)}) async-start(bf16[8,192,148]{1,2,0:T(8,128)(2,1)} %pad_maximum_fusion.3), calls=%async_computation.5 | async-start | bytes 1245184 | tf_op jit(solution)/shard_map/all_to_all | solution.py:19
where the time goes:
time: 202 us; the launch traced here: 201 us
  starting transfers between devices  77.1 us (38%)
  blocking collectives  44.1 us (22%)
  waiting for transfers between devices  41.8 us (21%)
  matrix products  19.7 us (10%)
  other arithmetic  10 us (5%)
  local copies, waits for them, and re-layouts  5.88 us (3%)
  between operations  2.27 us (1%)
    all_gather x2, blocking collectives, gather(): return lax.all_gather(array, axes, axis=0, tiled=True)  44.1 us
    all_to_all x7, starting transfers between devices, swap(): return lax.all_to_all(array, axes, 0, 0, tiled=True)  43.8 us
    all_to_all x7, waiting for transfers between devices, swap(): return lax.all_to_all(array, axes, 0, 0, tiled=True)  34.8 us
    ppermute x7, starting transfers between devices, shift(): return lax.ppermute(array, axes, [(i, (i + k) % n) for i in range(n)])  29.4 us
    dot_general x10, matrix products, dot(): return lax.dot_general(a, b, (dims, ((), ())), preferred_element_type=F32)  19.7 us
    ppermute x7, waiting for transfers between devices, shift(): return lax.ppermute(array, axes, [(i, (i + k) % n) for i in range(n)])  6.99 us
  transfers between devices with their start and end apart: 16, of which 7 were waited for; matrix products, arithmetic and copies ran while one was open for 10% of the time, Pallas kernels for 0%

commit v1 on v0

--- a/solution.py
+++ b/solution.py
@@ -30,12 +30,6 @@
     return swap(copies, axes).reshape(n * array.shape[0], *array.shape[1:])
 
 
-def summed_at(array, axes):
-    n = lax.axis_size(axes)
-    parts = array.reshape(n, array.shape[0] // n, *array.shape[1:])
-    return jnp.sum(swap(parts, axes).astype(F32), axis=0)
-
-
 def shift(array, axes, k):
     n = lax.axis_size(axes)
     return lax.ppermute(array, axes, [(i, (i + k) % n) for i in range(n)])
@@ -46,13 +40,10 @@
 
 
 def gathered_from_own(array):
-    high, low = (lax.axis_size(a) for a in Z)
-    rows = array.shape[0]
-    spaced = gather(array, "zh")
-    parts = gather(spaced, "zl").reshape(low, high, rows, -1)
-    in_line = parts.transpose(1, 0, 2, 3).reshape(high * low * rows, -1)
+    in_line = gather(array, Z)
     twice = jnp.concatenate([in_line, in_line], axis=0)
-    return lax.dynamic_slice_in_dim(twice, lax.axis_index(Z) * rows, in_line.shape[0], 0)
+    first = lax.axis_index(Z) * array.shape[0]
+    return lax.dynamic_slice_in_dim(twice, first, in_line.shape[0], 0)
 
 
 def sum_over_line(array, share):
@@ -104,10 +95,6 @@
     first_row = head_pos * share
     first_col = head_pos * cols
     text_part = dot(caption, mapping, ((1,), (0,))).astype(BF16)
-    text_out = summed_at(text_part, MP)
-    inv_text = lax.rsqrt(jnp.sum(text_out * text_out, axis=-1, keepdims=True) + 1e-06)
-    unit_text = (text_out * inv_text).astype(BF16)
-
     image_float = picture.astype(F32)
     mean_row = jnp.mean(image_float, axis=-1, keepdims=True)
     variance = jnp.mean((image_float - mean_row) ** 2, axis=-1, keepdims=True)
@@ -118,7 +105,12 @@
     hidden = gelu_tanh(preact).astype(BF16)
     partial_out = dot(hidden, exit_matrix, ((1,), (0,))).astype(BF16)
     own_rows = lax.dynamic_slice_in_dim(picture, first_row, share, 0).astype(F32)
-    image_out = own_rows + summed_at(partial_out, MP)
+    parts = [p.reshape(heads, share, width) for p in (text_part, partial_out)]
+    sums = jnp.sum(swap(jnp.concatenate(parts, axis=1), MP).astype(F32), axis=0)
+    text_out = sums[:share]
+    inv_text = lax.rsqrt(jnp.sum(text_out * text_out, axis=-1, keepdims=True) + 1e-06)
+    unit_text = (text_out * inv_text).astype(BF16)
+    image_out = own_rows + sums[share:]
     inv_image = lax.rsqrt(jnp.sum(image_out * image_out, axis=-1, keepdims=True) + 1e-06)
     unit_image = (image_out * inv_image).astype(BF16)
 
@@ -133,7 +125,9 @@
     energies = scale * dot(texts, images, ((1,), (1,))) + offset
     polarity = jnp.where(same, 1.0, -1.0).astype(F32)
     weighted = (scale * -polarity * jax.nn.sigmoid(-polarity * energies)).astype(BF16)
-    text_add = dot(weighted, images, ((1,), (0,)))
+    middle = weighted.shape[0] // 2
+    text_sent = dot(weighted[middle:], images, ((1,), (0,))).astype(BF16)
+    text_kept = dot(weighted[:middle], images, ((1,), (0,)))
     image_add = dot(weighted, texts, ((0,), (0,)))
 
     image_parts = swap(image_add.astype(BF16).reshape(-1, share, width), XY)
@@ -141,9 +135,8 @@
     grad_share = norm_back(image_dir, unit_image, inv_image).astype(BF16)
     grad_out_b = spread(grad_share, MP)
 
-    middle = text_add.shape[0] // 2
-    swapped = exchange(text_add[middle:].astype(BF16), "c", 1)
-    text_half = text_add[:middle] + swapped.astype(F32)
+    swapped = exchange(text_sent, "c", 1)
+    text_half = text_kept + swapped.astype(F32)
     text_dir = sum_over_line(text_half, share)
     grad_text_share = norm_back(text_dir, unit_text, inv_text).astype(BF16)
 
@@ -152,11 +145,11 @@
     grad_pre = pull_back(grad_hidden)[0].astype(BF16)
     partial_normed = dot(grad_pre, entry, ((1,), (1,)))
     scaled_part = partial_normed * gain
-    sums = jnp.stack(
+    row_sums = jnp.stack(
         [jnp.sum(scaled_part, axis=-1), jnp.sum(scaled_part * centred, axis=-1)], axis=-1
     )
-    sums_high = lax.reduce_precision(sums, 8, 7)
-    sums_low = sums - sums_high
+    sums_high = lax.reduce_precision(row_sums, 8, 7)
+    sums_low = row_sums - sums_high
     sums_both = jnp.concatenate([sums_high, sums_low], axis=-1).astype(BF16)
     blocks = partial_normed.astype(BF16).reshape(rows, heads, cols).transpose(1, 0, 2)
     packed = jnp.concatenate(

time: 202 us -> 201 us (level)
  waiting for transfers between devices: 41.8 us -> 50.9 us
  starting transfers between devices: 77.1 us -> 69.2 us
  blocking collectives: 44.1 us -> 40.5 us
    all_to_all x7 -> x6, waiting for transfers between devices: 34.8 us -> 40.9 us  [swap(): return lax.all_to_all(array, axes, 0, 0, tiled=True)]
    all_to_all x7 -> x6, starting transfers between devices: 43.8 us -> 37.9 us  [swap(): return lax.all_to_all(array, axes, 0, 0, tiled=True)]
    all_gather x2 -> x1, blocking collectives: 44.1 us -> 40.5 us  [gather(): return lax.all_gather(array, axes, axis=0, tiled=True)]
    another operation x2 -> x1, other arithmetic: 3.17 us -> 0.01 us
    ppermute x7, waiting for transfers between devices: 6.99 us -> 9.95 us  [shift(): return lax.ppermute(array, axes, [(i, (i + k) % n) for i in range(n)])]
    dot_general x10 -> x11, matrix products: 19.7 us -> 20.2 us  [dot(): return lax.dot_general(a, b, (dims, ((), ())), preferred_element_type=F32)]
  transfers between devices with their start and end apart: 16 -> 15, of which waited for: 7 -> 7; matrix products, arithmetic and copies ran while one was open for 10% -> 10% of each run, Pallas kernels for 0% -> 0%
where the time goes in v1:
time: 201 us; the launch traced here: 200 us
  starting transfers between devices  69.2 us (34%)
  waiting for transfers between devices  50.9 us (25%)
  blocking collectives  40.5 us (20%)
  matrix products  20.2 us (10%)
  other arithmetic  9.57 us (5%)
  local copies, waits for them, and re-layouts  7.05 us (4%)
  between operations  2.31 us (1%)
    all_to_all x6, waiting for transfers between devices, swap(): return lax.all_to_all(array, axes, 0, 0, tiled=True)  40.9 us
    all_gather x1, blocking collectives, gather(): return lax.all_gather(array, axes, axis=0, tiled=True)  40.5 us
    all_to_all x6, starting transfers between devices, swap(): return lax.all_to_all(array, axes, 0, 0, tiled=True)  37.9 us
    ppermute x7, starting transfers between devices, shift(): return lax.ppermute(array, axes, [(i, (i + k) % n) for i in range(n)])  27.4 us
    dot_general x11, matrix products, dot(): return lax.dot_general(a, b, (dims, ((), ())), preferred_element_type=F32)  20.2 us
    ppermute x7, waiting for transfers between devices, shift(): return lax.ppermute(array, axes, [(i, (i + k) % n) for i in range(n)])  9.95 us
  transfers between devices with their start and end apart: 15, of which 7 were waited for; matrix products, arithmetic and copies ran while one was open for 10% of the time, Pallas kernels for 0%

profile of v1, /device:TPU:2, one launch (start us, length us, event | category | flops | bytes accessed | tf_op | source)
XLA Modules:
  0.0 199.6 jit_solution(6028956407376201179)
XLA Ops:
  0.6 0.0 copy-start
  0.6 0.0 copy-start.1
  0.7 0.0 copy-start.7
  0.7 0.0 copy-start.9
  0.7 1.3 convert_reduce_fusion.3
  2.0 1.3 fusion.23
  3.3 1.4 convolution_convert_fusion.3
  4.7 0.7 fusion.35
  5.4 0.6 convolution_convert_fusion.2
  5.9 0.2 copy-done.10
  6.2 1.0 pad_maximum_fusion.3
  7.2 9.3 %all-to-all-start = ((bf16[8,48,1152]{2,1,0:T(8,128)(2,1)}), bf16[8,48,1152]{2,1,0:T(8,128)(2,1)S(1)}, u32[]{:S(2)}, u32[]{:S(2)}) async-start(bf16[8,48,1152]{2,1,0:T(8,128)(2,1)} %pad_maximum_fusion.3), calls=%async_computation | async-start | bytes 1769472 | tf_op jit(solution)/shard_map/all_to_all | solution.py:19
  16.5 11.3 %all-to-all-done = bf16[8,48,1152]{2,1,0:T(8,128)(2,1)S(1)} async-done(((bf16[8,48,1152]{2,1,0:T(8,128)(2,1)}), bf16[8,48,1152]{2,1,0:T(8,128)(2,1)S(1)}, u32[]{:S(2)}, u32[]{:S(2)}) %all-to-all-start) | async-done | bytes 884768 | tf_op jit(solution)/shard_map/all_to_all | solution.py:19
  27.8 0.1 convert_reduce_fusion.1
  27.9 0.1 multiply_reduce_fusion.1
  28.1 0.1 multiply_convert_fusion.3
  28.2 0.0 copy-start.3
  28.2 0.6 copy-done.3
  28.8 40.5 %all_gather.3 = bf16[384,1152]{1,0:T(8,128)(2,1)S(1)} all-gather(bf16[24,1152]{1,0:T(8,128)(2,1)S(1)} %get-tuple-element.24), channel_id=1, replica_groups=mesh['zh'=4,'zl'=4,'yl'=2,'c'=2,'x'=4,'yh'=2] {'zh','zl'}, dimensions={0}, use_global_device_ids=true | all-gather | bytes 940032 | tf_op jit(solution)/shard_map/all_gather | solution.py:39
  69.3 1.0 fusion.24
  70.3 1.9 collective-permute-start
  72.2 1.0 broadcast_in_dim.18
  73.2 5.8 %all-to-all-start.1 = ((bf16[16,24,1152]{2,1,0:T(8,128)(2,1)}), bf16[16,24,1152]{2,1,0:T(8,128)(2,1)S(1)}, u32[]{:S(2)}, u32[]{:S(2)}) async-start(bf16[16,24,1152]{2,1,0:T(8,128)(2,1)} %broadcast_in_dim.18), calls=%async_computation.1 | async-start | bytes 1769472 | tf_op jit(solution)/shard_map/all_to_all | solution.py:19
  80.3 14.8 %all-to-all-done.1 = bf16[16,24,1152]{2,1,0:T(8,128)(2,1)S(1)} async-done(((bf16[16,24,1152]{2,1,0:T(8,128)(2,1)}), bf16[16,24,1152]{2,1,0:T(8,128)(2,1)S(1)}, u32[]{:S(2)}, u32[]{:S(2)}) %all-to-all-start.1) | async-done | bytes 884768 | tf_op jit(solution)/shard_map/all_to_all | solution.py:19
  95.1 2.6 %fusion.7 = bf16[768,384]{1,0:T(8,128)(2,1)S(1)} fusion(bf16[384,1152]{1,0:T(8,128)(2,1)S(1)} %bitcast.36, bf16[384,1152]{1,0:T(8,128)(2,1)} %collective-permute-done, bf16[384,1152]{1,0:T(8,128)(2,1)S(1)} %fusion.24, f32[]{:T(128)S(6)} %copy.12, s32[384]{0:T(512)S(1)} %iota_subtract_fusion.1, f32[]{:T(128)S(6)} %copy.11, ...), kind=kOutput, calls=%fused_computation.18 | convolution fusion | flops 686850048 | bytes 3246344 | tf_op jit(solution)/shard_map/dot_general | solution.py:85
  97.7 0.8 copy-done.5
  98.5 1.6 convolution_convert_fusion
  100.1 1.9 collective-permute-start.1
  102.0 0.8 dynamic_slice.11
  102.8 3.2 %convolution_convert_fusion.1 = bf16[384,1152]{1,0:T(8,128)(2,1)} fusion(bf16[768,384]{1,0:T(8,128)(2,1)} %copy-done.5, bf16[384,1152]{1,0:T(8,128)(2,1)} %collective-permute-done, bf16[384,1152]{1,0:T(8,128)(2,1)S(1)} %fusion.24), kind=kOutput, calls=%fused_computation.1 | convolution fusion | flops 683458560 | bytes 3244032 | tf_op jit(solution)/shard_map/dot_general | solution.py:85
  106.1 5.4 %all-to-all-start.2 = ((bf16[16,24,1152]{2,1,0:T(8,128)(2,1)}), bf16[16,24,1152]{2,1,0:T(8,128)(2,1)S(1)}, u32[]{:S(2)}, u32[]{:S(2)}) async-start(bf16[16,24,1152]{2,1,0:T(8,128)(2,1)} %bitcast.42), calls=%async_computation.2 | async-start | bytes 1769472 | tf_op jit(solution)/shard_map/all_to_all | solution.py:19
  111.5 3.1 %fusion.97 = (bf16[384,1152]{1,0:T(8,128)(2,1)S(1)}, f32[384,1152]{1,0:T(8,128)}) fusion(bf16[384,1152]{1,0:T(8,128)(2,1)} %collective-permute-done.1, bf16[384,1152]{1,0:T(8,128)(2,1)S(1)} %bitcast.38, bf16[768,384]{1,0:T(8,128)(2,1)} %copy-done.5), kind=kOutput, calls=%fused_computation.143 | convolution fusion | flops 341065728 | bytes 4718592 | tf_op jit(solution)/shard_map/dot_general | solution.py:85
  114.6 0.7 fusion.95
  115.3 3.3 %collective-permute-start.2 = (bf16[72,1152]{1,0:T(8,128)(2,1)S(1)}, bf16[72,1152]{1,0:T(8,128)(2,1)}, u32[]{:S(2)}, u32[]{:S(2)}) collective-permute-start(bf16[72,1152]{1,0:T(8,128)(2,1)S(1)} %pad_maximum_fusion.5), channel_id=1, source_target_pairs={{0,448},{32,480},{64,0},{96,32},{128,64},{160,96},{192,128},{224,1... | collective-permute-start | bytes 497672 | tf_op jit(solution)/shard_map/ppermute | solution.py:35
  118.7 2.3 %collective-permute-start.3 = (bf16[72,1152]{1,0:T(8,128)(2,1)S(1)}, bf16[72,1152]{1,0:T(8,128)(2,1)}, u32[]{:S(2)}, u32[]{:S(2)}) collective-permute-start(bf16[72,1152]{1,0:T(8,128)(2,1)S(1)} %pad_maximum_fusion.6), channel_id=1, source_target_pairs={{0,480},{32,0},{64,32},{96,64},{128,96},{160,128},{192,160},{224,1... | collective-permute-start | bytes 497672 | tf_op jit(solution)/shard_map/ppermute | solution.py:35
  121.0 0.7 pad_maximum_fusion.7
  121.7 3.6 %collective-permute-start.4 = (bf16[72,1152]{1,0:T(8,128)(2,1)}, bf16[72,1152]{1,0:T(8,128)(2,1)}, u32[]{:S(2)}, u32[]{:S(2)}) collective-permute-start(bf16[72,1152]{1,0:T(8,128)(2,1)} %pad_maximum_fusion.7), channel_id=1, source_target_pairs={{0,32},{32,64},{64,96},{96,128},{128,160},{160,192},{192,224},{224... | collective-permute-start | bytes 497672 | tf_op jit(solution)/shard_map/ppermute | solution.py:35
  125.4 3.4 %collective-permute-start.5 = (bf16[72,1152]{1,0:T(8,128)(2,1)S(1)}, bf16[72,1152]{1,0:T(8,128)(2,1)}, u32[]{:S(2)}, u32[]{:S(2)}) collective-permute-start(bf16[72,1152]{1,0:T(8,128)(2,1)S(1)} %pad_maximum_fusion.8), channel_id=1, source_target_pairs={{0,64},{32,96},{64,128},{96,160},{128,192},{160,224},{192,256},{22... | collective-permute-start | bytes 497672 | tf_op jit(solution)/shard_map/ppermute | solution.py:35
  128.8 0.1 convert_reduce_fusion
  128.9 2.9 %collective-permute-start.6 = (bf16[24,1152]{1,0:T(8,128)(2,1)S(1)}, bf16[24,1152]{1,0:T(8,128)(2,1)S(1)}, u32[]{:S(2)}, u32[]{:S(2)}) collective-permute-start(bf16[24,1152]{1,0:T(8,128)(2,1)S(1)} %copy-done.6), channel_id=1, source_target_pairs={{0,96},{32,128},{64,160},{96,192},{128,224},{160,256},{192,288},{2... | collective-permute-start | bytes 165896 | tf_op jit(solution)/shard_map/ppermute | solution.py:35
  131.8 0.1 fusion.58
  131.9 9.2 %collective-permute-done.6 = bf16[24,1152]{1,0:T(8,128)(2,1)S(1)} collective-permute-done((bf16[24,1152]{1,0:T(8,128)(2,1)S(1)}, bf16[24,1152]{1,0:T(8,128)(2,1)S(1)}, u32[]{:S(2)}, u32[]{:S(2)}) %collective-permute-start.6) | collective-permute-done | bytes 55328 | tf_op jit(solution)/shard_map/ppermute | solution.py:35
  141.2 0.7 collective-permute-done.5
  141.9 1.2 fusion.74
  143.1 5.1 %collective-permute-start.7 = (bf16[24,1152]{1,0:T(8,128)(2,1)S(1)}, bf16[24,1152]{1,0:T(8,128)(2,1)S(1)}, u32[]{:S(2)}, u32[]{:S(2)}) collective-permute-start(bf16[24,1152]{1,0:T(8,128)(2,1)S(1)} %get-tuple-element.8), channel_id=1, source_target_pairs={{0,160},{32,192},{64,224},{96,256},{128,288},{160,320},{192,352},{... | collective-permute-start | bytes 165896 | tf_op jit(solution)/shard_map/ppermute | solution.py:35
  148.2 6.7 %collective-permute-start.8 = (bf16[24,1152]{1,0:T(8,128)(2,1)S(1)}, bf16[24,1152]{1,0:T(8,128)(2,1)S(1)}, u32[]{:S(2)}, u32[]{:S(2)}) collective-permute-start(bf16[24,1152]{1,0:T(8,128)(2,1)S(1)} %get-tuple-element.9), channel_id=1, source_target_pairs={{0,352},{32,384},{64,416},{96,448},{128,480},{160,0},{192,32},{224... | collective-permute-start | bytes 165896 | tf_op jit(solution)/shard_map/ppermute | solution.py:35
  154.9 0.1 fusion.61
  155.0 0.8 broadcast_in_dim.19
  155.9 7.2 %all-to-all-start.3 = ((bf16[8,24,1152]{2,1,0:T(8,128)(2,1)}), bf16[8,24,1152]{2,1,0:T(8,128)(2,1)S(1)}, u32[]{:S(2)}, u32[]{:S(2)}) async-start(bf16[8,24,1152]{2,1,0:T(8,128)(2,1)} %broadcast_in_dim.19), calls=%async_computation.3 | async-start | bytes 884736 | tf_op jit(solution)/shard_map/all_to_all | solution.py:19
  163.1 1.2 fusion.62
  164.3 0.1 fusion.65
  164.4 6.3 %all-to-all-done.3 = bf16[8,24,1152]{2,1,0:T(8,128)(2,1)S(1)} async-done(((bf16[8,24,1152]{2,1,0:T(8,128)(2,1)}), bf16[8,24,1152]{2,1,0:T(8,128)(2,1)S(1)}, u32[]{:S(2)}, u32[]{:S(2)}) %all-to-all-start.3) | async-done | bytes 442400 | tf_op jit(solution)/shard_map/all_to_all | solution.py:19
  170.7 0.8 broadcast_in_dim.21
  171.5 4.9 %all-to-all-start.5 = ((bf16[8,24,1152]{2,1,0:T(8,128)(2,1)}), bf16[8,24,1152]{2,1,0:T(8,128)(2,1)S(1)}, u32[]{:S(2)}, u32[]{:S(2)}) async-start(bf16[8,24,1152]{2,1,0:T(8,128)(2,1)} %broadcast_in_dim.21), calls=%async_computation.5 | async-start | bytes 884736 | tf_op jit(solution)/shard_map/all_to_all | solution.py:19
  176.4 3.4 %multiply_reduce_fusion = (f32[192]{0:T(256)S(1)}, f32[192]{0:T(256)S(1)}, bf16[192,1152]{1,0:T(8,128)(2,1)}) fusion(f32[1152]{0:T(1024)S(1)} %copy-done.8, f32[192]{0:T(256)S(1)} %add_rsqrt_fusion, f32[192]{0:T(256)S(1)} %broadcast_multiply_fusion, bf16[192,1152]{1,0:T(8,128)(2,1)S(1)} %copy-done.1, bf16[1152,538]{0,1:T(8,128)(2,1)} %param.11, ...), kind=kOutput, calls=%fused_computation.43 | convolution fusion | flops 479822976 | bytes 4227072 | tf_op jit(solution)/shard_map/dot_general | solution.py:85
  179.8 1.2 copy.10
  181.1 0.9 pad_maximum_fusion.4
  182.0 2.1 %all-to-all-done.5 = bf16[8,24,1152]{2,1,0:T(8,128)(2,1)S(1)} async-done(((bf16[8,24,1152]{2,1,0:T(8,128)(2,1)}), bf16[8,24,1152]{2,1,0:T(8,128)(2,1)S(1)}, u32[]{:S(2)}, u32[]{:S(2)}) %all-to-all-start.5) | async-done | bytes 442400 | tf_op jit(solution)/shard_map/all_to_all | solution.py:19
  184.1 5.3 %all-to-all-start.4 = ((bf16[8,192,148]{1,2,0:T(8,128)(2,1)}), bf16[8,192,148]{1,2,0:T(8,128)(2,1)S(1)}, u32[]{:S(2)}, u32[]{:S(2)}) async-start(bf16[8,192,148]{1,2,0:T(8,128)(2,1)} %pad_maximum_fusion.4), calls=%async_computation.4 | async-start | bytes 1245184 | tf_op jit(solution)/shard_map/all_to_all | solution.py:19
  189.4 1.3 fusion.9
  190.7 1.0 fusion.100
  191.7 6.5 %all-to-all-done.4 = bf16[8,192,148]{1,2,0:T(8,128)(2,1)S(1)} async-done(((bf16[8,192,148]{1,2,0:T(8,128)(2,1)}), bf16[8,192,148]{1,2,0:T(8,128)(2,1)S(1)}, u32[]{:S(2)}, u32[]{:S(2)}) %all-to-all-start.4) | async-done | bytes 454688 | tf_op jit(solution)/shard_map/all_to_all | solution.py:19
  198.2 0.1 convert_reduce_fusion.2
  198.3 1.3 fusion.16
  (40 shorter events, 0.2 us)
Async XLA Ops:
  0.6 4.7 %copy-start = (bf16[538,1152]{1,0:T(8,128)(2,1)S(1)}, bf16[538,1152]{1,0:T(8,128)(2,1)}, u32[]{:S(2)}) copy-start(bf16[538,1152]{1,0:T(8,128)(2,1)} %param.12) | copy-start | bytes 3718660
  0.6 4.0 %copy-start.1 = (bf16[192,1152]{1,0:T(8,128)(2,1)S(1)}, bf16[192,1152]{1,0:T(8,128)(2,1)}, u32[]{:S(2)}) copy-start(bf16[192,1152]{1,0:T(8,128)(2,1)} %param.8) | copy-start | bytes 1327108
  0.7 4.0 %copy-start.7 = (f32[1152]{0:T(1024)S(1)}, f32[1152]{0:T(1024)}, u32[]{:S(2)}) copy-start(f32[1152]{0:T(1024)} %param.10) | copy-start | bytes 13828
  0.7 4.0 %copy-start.9 = (bf16[1152,538]{0,1:T(8,128)(2,1)S(1)}, bf16[1152,538]{0,1:T(8,128)(2,1)}, u32[]{:S(2)}) copy-start(bf16[1152,538]{0,1:T(8,128)(2,1)} %param.11) | copy-start | bytes 3718660
  5.4 0.8 copy-start.10
  7.2 20.7 %all-to-all-start = ((bf16[8,48,1152]{2,1,0:T(8,128)(2,1)}), bf16[8,48,1152]{2,1,0:T(8,128)(2,1)S(1)}, u32[]{:S(2)}, u32[]{:S(2)}) async-start(bf16[8,48,1152]{2,1,0:T(8,128)(2,1)} %pad_maximum_fusion.3), calls=%async_computation | async-start | bytes 1769472 | tf_op jit(solution)/shard_map/all_to_all | solution.py:19
  28.2 0.6 copy-start.3
  70.3 24.8 %collective-permute-start = (bf16[384,1152]{1,0:T(8,128)(2,1)S(1)}, bf16[384,1152]{1,0:T(8,128)(2,1)}, u32[]{:S(2)}, u32[]{:S(2)}) collective-permute-start(bf16[384,1152]{1,0:T(8,128)(2,1)S(1)} %fusion.24), channel_id=1, source_target_pairs={{0,8},{8,0},{1,9},{9,1},{2,10},{10,2},{3,11},{11,3},{4,12},{12,4},... | collective-permute-start | bytes 2654216 | tf_op jit(solution)/shard_map/ppermute | solution.py:24
  73.2 21.9 %all-to-all-start.1 = ((bf16[16,24,1152]{2,1,0:T(8,128)(2,1)}), bf16[16,24,1152]{2,1,0:T(8,128)(2,1)S(1)}, u32[]{:S(2)}, u32[]{:S(2)}) async-start(bf16[16,24,1152]{2,1,0:T(8,128)(2,1)} %broadcast_in_dim.18), calls=%async_computation.1 | async-start | bytes 1769472 | tf_op jit(solution)/shard_map/all_to_all | solution.py:19
  97.7 0.8 copy-start.5
  100.1 11.4 %collective-permute-start.1 = (bf16[384,1152]{1,0:T(8,128)(2,1)}, bf16[384,1152]{1,0:T(8,128)(2,1)}, u32[]{:S(2)}, u32[]{:S(2)}) collective-permute-start(bf16[384,1152]{1,0:T(8,128)(2,1)} %convolution_convert_fusion), channel_id=1, source_target_pairs={{0,8},{8,0},{1,9},{9,1},{2,10},{10,2},{3,11},{11,3},{4,12},{12,4},... | collective-permute-start | bytes 2654216 | tf_op jit(solution)/shard_map/ppermute | solution.py:24
  106.1 22.7 %all-to-all-start.2 = ((bf16[16,24,1152]{2,1,0:T(8,128)(2,1)}), bf16[16,24,1152]{2,1,0:T(8,128)(2,1)S(1)}, u32[]{:S(2)}, u32[]{:S(2)}) async-start(bf16[16,24,1152]{2,1,0:T(8,128)(2,1)} %bitcast.42), calls=%async_computation.2 | async-start | bytes 1769472 | tf_op jit(solution)/shard_map/all_to_all | solution.py:19
  115.3 25.9 %collective-permute-start.2 = (bf16[72,1152]{1,0:T(8,128)(2,1)S(1)}, bf16[72,1152]{1,0:T(8,128)(2,1)}, u32[]{:S(2)}, u32[]{:S(2)}) collective-permute-start(bf16[72,1152]{1,0:T(8,128)(2,1)S(1)} %pad_maximum_fusion.5), channel_id=1, source_target_pairs={{0,448},{32,480},{64,0},{96,32},{128,64},{160,96},{192,128},{224,1... | collective-permute-start | bytes 497672 | tf_op jit(solution)/shard_map/ppermute | solution.py:35
  118.7 10.3 %copy-start.6 = (bf16[24,1152]{1,0:T(8,128)(2,1)S(1)}, bf16[24,1152]{1,0:T(8,128)(2,1)}, u32[]{:S(2)}) copy-start(bf16[24,1152]{1,0:T(8,128)(2,1)} %get-tuple-element.10) | copy-start | bytes 165892
  118.7 22.5 %collective-permute-start.3 = (bf16[72,1152]{1,0:T(8,128)(2,1)S(1)}, bf16[72,1152]{1,0:T(8,128)(2,1)}, u32[]{:S(2)}, u32[]{:S(2)}) collective-permute-start(bf16[72,1152]{1,0:T(8,128)(2,1)S(1)} %pad_maximum_fusion.6), channel_id=1, source_target_pairs={{0,480},{32,0},{64,32},{96,64},{128,96},{160,128},{192,160},{224,1... | collective-permute-start | bytes 497672 | tf_op jit(solution)/shard_map/ppermute | solution.py:35
  121.7 19.5 %collective-permute-start.4 = (bf16[72,1152]{1,0:T(8,128)(2,1)}, bf16[72,1152]{1,0:T(8,128)(2,1)}, u32[]{:S(2)}, u32[]{:S(2)}) collective-permute-start(bf16[72,1152]{1,0:T(8,128)(2,1)} %pad_maximum_fusion.7), channel_id=1, source_target_pairs={{0,32},{32,64},{64,96},{96,128},{128,160},{160,192},{192,224},{224... | collective-permute-start | bytes 497672 | tf_op jit(solution)/shard_map/ppermute | solution.py:35
  125.4 16.5 %collective-permute-start.5 = (bf16[72,1152]{1,0:T(8,128)(2,1)S(1)}, bf16[72,1152]{1,0:T(8,128)(2,1)}, u32[]{:S(2)}, u32[]{:S(2)}) collective-permute-start(bf16[72,1152]{1,0:T(8,128)(2,1)S(1)} %pad_maximum_fusion.8), channel_id=1, source_target_pairs={{0,64},{32,96},{64,128},{96,160},{128,192},{160,224},{192,256},{22... | collective-permute-start | bytes 497672 | tf_op jit(solution)/shard_map/ppermute | solution.py:35
  128.9 12.2 %collective-permute-start.6 = (bf16[24,1152]{1,0:T(8,128)(2,1)S(1)}, bf16[24,1152]{1,0:T(8,128)(2,1)S(1)}, u32[]{:S(2)}, u32[]{:S(2)}) collective-permute-start(bf16[24,1152]{1,0:T(8,128)(2,1)S(1)} %copy-done.6), channel_id=1, source_target_pairs={{0,96},{32,128},{64,160},{96,192},{128,224},{160,256},{192,288},{2... | collective-permute-start | bytes 165896 | tf_op jit(solution)/shard_map/ppermute | solution.py:35
  131.9 31.1 %copy-start.4 = (bf16[24,1152]{1,0:T(8,128)(2,1)S(1)}, bf16[24,1152]{1,0:T(8,128)(2,1)}, u32[]{:S(2)}) copy-start(bf16[24,1152]{1,0:T(8,128)(2,1)} %copy-done.3) | copy-start | bytes 165892
  143.1 20.0 %collective-permute-start.7 = (bf16[24,1152]{1,0:T(8,128)(2,1)S(1)}, bf16[24,1152]{1,0:T(8,128)(2,1)S(1)}, u32[]{:S(2)}, u32[]{:S(2)}) collective-permute-start(bf16[24,1152]{1,0:T(8,128)(2,1)S(1)} %get-tuple-element.8), channel_id=1, source_target_pairs={{0,160},{32,192},{64,224},{96,256},{128,288},{160,320},{192,352},{... | collective-permute-start | bytes 165896 | tf_op jit(solution)/shard_map/ppermute | solution.py:35
  148.2 14.9 %collective-permute-start.8 = (bf16[24,1152]{1,0:T(8,128)(2,1)S(1)}, bf16[24,1152]{1,0:T(8,128)(2,1)S(1)}, u32[]{:S(2)}, u32[]{:S(2)}) collective-permute-start(bf16[24,1152]{1,0:T(8,128)(2,1)S(1)} %get-tuple-element.9), channel_id=1, source_target_pairs={{0,352},{32,384},{64,416},{96,448},{128,480},{160,0},{192,32},{224... | collective-permute-start | bytes 165896 | tf_op jit(solution)/shard_map/ppermute | solution.py:35
  155.9 14.9 %all-to-all-start.3 = ((bf16[8,24,1152]{2,1,0:T(8,128)(2,1)}), bf16[8,24,1152]{2,1,0:T(8,128)(2,1)S(1)}, u32[]{:S(2)}, u32[]{:S(2)}) async-start(bf16[8,24,1152]{2,1,0:T(8,128)(2,1)} %broadcast_in_dim.19), calls=%async_computation.3 | async-start | bytes 884736 | tf_op jit(solution)/shard_map/all_to_all | solution.py:19
  163.1 13.3 %copy-start.8 = (f32[1152]{0:T(1024)S(1)}, f32[1152]{0:T(1024)}, u32[]{:S(2)}) copy-start(f32[1152]{0:T(1024)} %param.10) | copy-start | bytes 13828
  163.1 13.3 %copy-start.11 = (f32[192,538]{1,0:T(8,128)S(1)}, f32[192,538]{1,0:T(8,128)}, u32[]{:S(2)}) copy-start(f32[192,538]{1,0:T(8,128)} %copy-done.10) | copy-start | bytes 1239556
  171.5 12.5 %all-to-all-start.5 = ((bf16[8,24,1152]{2,1,0:T(8,128)(2,1)}), bf16[8,24,1152]{2,1,0:T(8,128)(2,1)S(1)}, u32[]{:S(2)}, u32[]{:S(2)}) async-start(bf16[8,24,1152]{2,1,0:T(8,128)(2,1)} %broadcast_in_dim.21), calls=%async_computation.5 | async-start | bytes 884736 | tf_op jit(solution)/shard_map/all_to_all | solution.py:19
  182.0 8.7 %copy-start.2 = (bf16[144,1152]{1,0:T(8,128)(2,1)S(1)}, bf16[144,1152]{1,0:T(8,128)(2,1)}, u32[]{:S(2)}) copy-start(bf16[144,1152]{1,0:T(8,128)(2,1)} %param.13) | copy-start | bytes 995332
  184.1 14.1 %all-to-all-start.4 = ((bf16[8,192,148]{1,2,0:T(8,128)(2,1)}), bf16[8,192,148]{1,2,0:T(8,128)(2,1)S(1)}, u32[]{:S(2)}, u32[]{:S(2)}) async-start(bf16[8,192,148]{1,2,0:T(8,128)(2,1)} %pad_maximum_fusion.4), calls=%async_computation.4 | async-start | bytes 1245184 | tf_op jit(solution)/shard_map/all_to_all | solution.py:19
  190.7 7.6 %copy-start.12 = (f32[192,144]{0,1:T(8,128)S(1)}, f32[192,144]{0,1:T(8,128)}, u32[]{:S(2)}) copy-start(f32[192,144]{0,1:T(8,128)} %fusion.9) | copy-start | bytes 331780

commit v2 on v1

--- a/solution.py
+++ b/solution.py
@@ -9,8 +9,9 @@
 MP = ("x", "yh")
 Z = ("zh", "zl")
 XY = ("yl", "x", "yh")
-NEAR = (-2, -1, 1, 2)
-FAR = 5
+LINE = ("zh", "zl", "c")
+NEAR = (1, 2)
+FAR = (3, 6)
 F32 = jnp.float32
 BF16 = jnp.bfloat16
 
@@ -30,45 +31,42 @@
     return swap(copies, axes).reshape(n * array.shape[0], *array.shape[1:])
 
 
-def shift(array, axes, k):
-    n = lax.axis_size(axes)
-    return lax.ppermute(array, axes, [(i, (i + k) % n) for i in range(n)])
+def along(array, k):
+    n = lax.axis_size(Z)
+    moves = []
+    for i in range(n):
+        moves.append((2 * i, 2 * ((i - k) % n)))
+        moves.append((2 * i + 1, 2 * ((i + k) % n) + 1))
+    return lax.ppermute(array, LINE, moves)
 
 
-def gather(array, axes):
-    return lax.all_gather(array, axes, axis=0, tiled=True)
+def gathered_line(array):
+    share = array.shape[0]
+    pair = jnp.concatenate([array, exchange(array, "c", 1)], axis=0)
+    far = [along(pair, -k) for k in FAR]
+    near = jnp.concatenate([pair, *far], axis=0)
+    cut = near.shape[0] - share
+    last = [along(near, -NEAR[0]), along(near[:cut], -NEAR[1])]
+    mine = jnp.concatenate([near, *last], axis=0)
+    other = exchange(mine[2 * share :], "c", 1)
+    return jnp.concatenate([mine, other], axis=0)
 
 
-def gathered_from_own(array):
-    in_line = gather(array, Z)
-    twice = jnp.concatenate([in_line, in_line], axis=0)
-    first = lax.axis_index(Z) * array.shape[0]
-    return lax.dynamic_slice_in_dim(twice, first, in_line.shape[0], 0)
-
-
-def sum_over_line(array, share):
-    n = lax.axis_size(Z)
-    half = n // 2
-
-    def block(k):
-        first = (k % n) * share
-        return array[first : first + share]
-
-    own = [block(0), block(FAR), block(-FAR)]
-    arrived = []
-    for b in NEAR:
-        parts = [block(b), block(b + FAR), block(b - FAR)]
-        arrived.append(shift(jnp.concatenate(parts, axis=0).astype(BF16), Z, b))
-    last = shift(block(half).astype(BF16), Z, half - FAR).astype(F32)
-    sums = []
-    for place in range(3):
-        total = own[place]
-        for piece in arrived:
-            total = total + piece[place * share : (place + 1) * share].astype(F32)
-        sums.append(total)
-    up = shift((sums[1] + last).astype(BF16), Z, FAR)
-    down = shift(sums[2].astype(BF16), Z, -FAR)
-    return sums[0] + up.astype(F32) + down.astype(F32)
+def summed_line(kept, swapped, share):
+    pair = 2 * share
+    rest = kept[pair:] + swapped.astype(F32)
+    cut = 5 * pair
+    one = along(rest[2 * pair : cut].astype(BF16), NEAR[0]).astype(F32)
+    two = along(rest[cut:].astype(BF16), NEAR[1]).astype(F32)
+    here = kept[:pair] + one[:pair] + two[:pair]
+    third = rest[:pair] + one[pair : 2 * pair] + two[pair : 2 * pair]
+    sixth = rest[pair : 2 * pair] + one[2 * pair :]
+    sixth = jnp.concatenate([sixth[:share] + two[2 * pair :], sixth[share:]], axis=0)
+    three = along(third.astype(BF16), FAR[0])
+    six = along(sixth.astype(BF16), FAR[1])
+    total = here + three.astype(F32) + six.astype(F32)
+    partner = exchange(total[share:].astype(BF16), "c", 1)
+    return total[:share] + partner.astype(F32)
 
 
 def gelu_tanh(values):
@@ -114,8 +112,7 @@
     inv_image = lax.rsqrt(jnp.sum(image_out * image_out, axis=-1, keepdims=True) + 1e-06)
     unit_image = (image_out * inv_image).astype(BF16)
 
-    line = gathered_from_own(unit_text)
-    texts = jnp.concatenate([line, exchange(line, "c", 1)], axis=0)
+    texts = gathered_line(unit_text)
     images = spread(unit_image, XY)
 
     own_start = lax.axis_index(XY) * share
@@ -125,7 +122,7 @@
     energies = scale * dot(texts, images, ((1,), (1,))) + offset
     polarity = jnp.where(same, 1.0, -1.0).astype(F32)
     weighted = (scale * -polarity * jax.nn.sigmoid(-polarity * energies)).astype(BF16)
-    middle = weighted.shape[0] // 2
+    middle = weighted.shape[0] // 2 + share
     text_sent = dot(weighted[middle:], images, ((1,), (0,))).astype(BF16)
     text_kept = dot(weighted[:middle], images, ((1,), (0,)))
     image_add = dot(weighted, texts, ((0,), (0,)))
@@ -136,8 +133,7 @@
     grad_out_b = spread(grad_share, MP)
 
     swapped = exchange(text_sent, "c", 1)
-    text_half = text_kept + swapped.astype(F32)
-    text_dir = sum_over_line(text_half, share)
+    text_dir = summed_line(text_kept, swapped, share)
     grad_text_share = norm_back(text_dir, unit_text, inv_text).astype(BF16)
 
     grad_hidden = dot(grad_out_b, exit_matrix, ((1,), (1,)))

time: 201 us -> 199 us (0.990)
  the two profiles are of different devices: /device:TPU:2 before, /device:TPU:64 now
where the time goes in v2:
time: 199 us; the launch traced here: 198 us
  waiting for transfers between devices  75.8 us (38%)
  starting transfers between devices  72.9 us (37%)
  matrix products  19.7 us (10%)
  other arithmetic  15.9 us (8%)
  local copies, waits for them, and re-layouts  11.4 us (6%)
  between operations  2.45 us (1%)
    all_to_all x6, waiting for transfers between devices, swap(): return lax.all_to_all(array, axes, 0, 0, tiled=True)  53.2 us
    ppermute x8, starting transfers between devices, along(): return lax.ppermute(array, LINE, moves)  38 us
    all_to_all x6, starting transfers between devices, swap(): return lax.all_to_all(array, axes, 0, 0, tiled=True)  27.1 us
    ppermute x8, waiting for transfers between devices, along(): return lax.ppermute(array, LINE, moves)  22.6 us
    dot_general x11, matrix products, dot(): return lax.dot_general(a, b, (dims, ((), ())), preferred_element_type=F32)  19.7 us
    ppermute x4, starting transfers between devices, exchange(): return lax.ppermute(array, axes, [(i, i ^ k) for i in range(n)])  7.79 us
    unnamed x47, local copies, waits for them, and re-layouts  5.64 us
  transfers between devices with their start and end apart: 18, of which 11 were waited for; matrix products, arithmetic and copies ran while one was open for 15% of the time, Pallas kernels for 0%

profile of v2, /device:TPU:64, one launch (start us, length us, event | category | flops | bytes accessed | tf_op | source)
XLA Modules:
  0.0 198.0 jit_solution(18228329554286060284)
XLA Ops:
  0.6 1.3 convert_reduce_fusion.3
  1.9 1.3 fusion.23
  3.2 2.1 %fusion.34 = f32[192,538]{1,0:T(8,128)S(1)} fusion(bf16[1152,538]{0,1:T(8,128)(2,1)} %param.11, bf16[192,1152]{1,0:T(8,128)(2,1)} %param.8, f32[1152]{0:T(1024)} %param.10, f32[192]{0:T(256)S(1)} %add_rsqrt_fusion, f32[192]{0:T(256)S(1)} %broadcast_multiply_fusion), kind=kOutput, calls=%fused_computation.54 | convolution fusion | flops 239099904 | bytes 2101248 | tf_op jit(solution)/shard_map/dot_general | solution.py:83
  5.4 0.6 convolution_convert_fusion.2
  5.9 0.6 copy-done.5
  6.9 1.0 pad_maximum_fusion
  7.9 7.1 %all-to-all-start = ((bf16[8,48,1152]{2,1,0:T(8,128)(2,1)}), bf16[8,48,1152]{2,1,0:T(8,128)(2,1)S(1)}, u32[]{:S(2)}, u32[]{:S(2)}) async-start(bf16[8,48,1152]{2,1,0:T(8,128)(2,1)} %pad_maximum_fusion), calls=%async_computation | async-start | bytes 1769472 | tf_op jit(solution)/shard_map/all_to_all | solution.py:20
  14.9 14.2 %all-to-all-done = bf16[8,48,1152]{2,1,0:T(8,128)(2,1)S(1)} async-done(((bf16[8,48,1152]{2,1,0:T(8,128)(2,1)}), bf16[8,48,1152]{2,1,0:T(8,128)(2,1)S(1)}, u32[]{:S(2)}, u32[]{:S(2)}) %all-to-all-start) | async-done | bytes 884768 | tf_op jit(solution)/shard_map/all_to_all | solution.py:20
  29.4 0.7 constant_dynamic-update-slice_fusion.6
  30.1 1.9 collective-permute-start
  33.3 7.7 %collective-permute-start.1 = (bf16[48,1152]{1,0:T(8,128)(2,1)S(1)}, bf16[48,1152]{1,0:T(8,128)(2,1)S(1)}, u32[]{:S(2)}, u32[]{:S(2)}) collective-permute-start(bf16[48,1152]{1,0:T(8,128)(2,1)S(1)} %pad_maximum_fusion.4), channel_id=1, source_target_pairs={{0,96},{8,424},{32,128},{40,456},{64,160},{72,488},{96,192},{104,8... | collective-permute-start | bytes 331784 | tf_op jit(solution)/shard_map/ppermute | solution.py:40
  41.1 9.1 %collective-permute-start.2 = (bf16[48,1152]{1,0:T(8,128)(2,1)S(1)}, bf16[48,1152]{1,0:T(8,128)(2,1)S(1)}, u32[]{:S(2)}, u32[]{:S(2)}) collective-permute-start(bf16[48,1152]{1,0:T(8,128)(2,1)S(1)} %pad_maximum_fusion.4), channel_id=1, source_target_pairs={{0,192},{8,328},{32,224},{40,360},{64,256},{72,392},{96,288},{104,... | collective-permute-start | bytes 331784 | tf_op jit(solution)/shard_map/ppermute | solution.py:40
  50.2 8.9 %collective-permute-done.2 = bf16[48,1152]{1,0:T(8,128)(2,1)S(1)} collective-permute-done((bf16[48,1152]{1,0:T(8,128)(2,1)S(1)}, bf16[48,1152]{1,0:T(8,128)(2,1)S(1)}, u32[]{:S(2)}, u32[]{:S(2)}) %collective-permute-start.2) | collective-permute-done | bytes 110624 | tf_op jit(solution)/shard_map/ppermute | solution.py:40
  59.2 1.9 collective-permute-start.3
  61.1 0.7 slice.112
  61.8 6.1 %collective-permute-start.4 = (bf16[120,1152]{1,0:T(8,128)(2,1)}, bf16[120,1152]{1,0:T(8,128)(2,1)S(1)}, u32[]{:S(2)}, u32[]{:S(2)}) collective-permute-start(bf16[120,1152]{1,0:T(8,128)(2,1)} %slice.112), channel_id=1, source_target_pairs={{0,64},{8,456},{32,96},{40,488},{64,128},{72,8},{96,160},{104,40},... | collective-permute-start | bytes 829448 | tf_op jit(solution)/shard_map/ppermute | solution.py:40
  68.0 1.0 broadcast_in_dim.18
  69.0 4.2 %all-to-all-start.1 = ((bf16[16,24,1152]{2,1,0:T(8,128)(2,1)}), bf16[16,24,1152]{2,1,0:T(8,128)(2,1)S(1)}, u32[]{:S(2)}, u32[]{:S(2)}) async-start(bf16[16,24,1152]{2,1,0:T(8,128)(2,1)} %broadcast_in_dim.18), calls=%async_computation.1 | async-start | bytes 1769472 | tf_op jit(solution)/shard_map/all_to_all | solution.py:20
  73.2 1.5 constant_dynamic-update-slice_fusion.5
  74.7 0.6 collective-permute-done.4
  75.3 1.0 pad_maximum_fusion.1
  76.3 1.9 collective-permute-start.5
  78.2 0.7 constant_dynamic-update-slice_fusion.4
  78.9 0.7 constant_dynamic-update-slice_fusion.3
  79.5 0.8 constant_dynamic-update-slice_fusion.2
  80.3 0.8 constant_dynamic-update-slice_fusion.1
  81.1 1.0 constant_dynamic-update-slice_fusion
  82.1 7.2 %all-to-all-done.1 = bf16[16,24,1152]{2,1,0:T(8,128)(2,1)S(1)} async-done(((bf16[16,24,1152]{2,1,0:T(8,128)(2,1)}), bf16[16,24,1152]{2,1,0:T(8,128)(2,1)S(1)}, u32[]{:S(2)}, u32[]{:S(2)}) %all-to-all-start.1) | async-done | bytes 884768 | tf_op jit(solution)/shard_map/all_to_all | solution.py:20
  89.3 2.9 %fusion.7 = bf16[768,384]{1,0:T(8,128)(2,1)S(1)} fusion(bf16[768,1152]{1,0:T(8,128)(2,1)} %constant_dynamic-update-slice_fusion, bf16[384,1152]{1,0:T(8,128)(2,1)S(1)} %bitcast.38, f32[]{:T(128)S(6)} %copy.18, s32[384]{0:T(512)S(1)} %iota_subtract_fusion.1, f32[]{:T(128)S(6)} %copy.17, pred[768]{0:T(1024)(128)(4,1)S(1)} %iota_compare_fusion.3), kind=kOutput, calls=%fused_computation.15 | convolution fusion | flops 683311104 | bytes 3246344 | tf_op jit(solution)/shard_map/dot_general | solution.py:83
  92.2 1.5 convolution_convert_fusion.1
  93.8 1.9 collective-permute-start.6
  95.8 3.4 %convolution_convert_fusion = bf16[384,1152]{1,0:T(8,128)(2,1)} fusion(bf16[768,384]{1,0:T(8,128)(2,1)S(1)} %fusion.7, bf16[768,1152]{1,0:T(8,128)(2,1)} %constant_dynamic-update-slice_fusion), kind=kOutput, calls=%fused_computation | convolution fusion | flops 679919616 | bytes 3244032 | tf_op jit(solution)/shard_map/dot_general | solution.py:83
  99.2 4.1 %all-to-all-start.2 = ((bf16[16,24,1152]{2,1,0:T(8,128)(2,1)}), bf16[16,24,1152]{2,1,0:T(8,128)(2,1)S(1)}, u32[]{:S(2)}, u32[]{:S(2)}) async-start(bf16[16,24,1152]{2,1,0:T(8,128)(2,1)} %bitcast.44), calls=%async_computation.2 | async-start | bytes 1769472 | tf_op jit(solution)/shard_map/all_to_all | solution.py:20
  103.3 1.7 fusion.39
  105.0 3.1 %fusion.79 = (bf16[360,1152]{1,0:T(8,128)(2,1)S(1)}, f32[360,1152]{1,0:T(8,128)}) fusion(bf16[360,1152]{1,0:T(8,128)(2,1)} %collective-permute-done.6, f32[408,1152]{1,0:T(8,128)S(1)} %fusion.39), kind=kLoop, calls=%fused_computation.138 | loop fusion | flops 1244160 | bytes 4976640 | tf_op jit(solution)/shard_map/convert.5
  108.2 12.4 %all-to-all-done.2 = bf16[16,24,1152]{2,1,0:T(8,128)(2,1)S(1)} async-done(((bf16[16,24,1152]{2,1,0:T(8,128)(2,1)}), bf16[16,24,1152]{2,1,0:T(8,128)(2,1)S(1)}, u32[]{:S(2)}, u32[]{:S(2)}) %all-to-all-start.2) | async-done | bytes 884768 | tf_op jit(solution)/shard_map/all_to_all | solution.py:20
  120.9 2.5 %collective-permute-start.8 = (bf16[120,1152]{1,0:T(8,128)(2,1)S(1)}, bf16[120,1152]{1,0:T(8,128)(2,1)S(1)}, u32[]{:S(2)}, u32[]{:S(2)}) collective-permute-start(bf16[120,1152]{1,0:T(8,128)(2,1)S(1)} %slice.124), channel_id=1, source_target_pairs={{0,448},{8,72},{32,480},{40,104},{64,0},{72,136},{96,32},{104,168}... | collective-permute-start | bytes 829448 | tf_op jit(solution)/shard_map/ppermute | solution.py:40
  123.3 3.7 %collective-permute-start.7 = (bf16[144,1152]{1,0:T(8,128)(2,1)S(1)}, bf16[144,1152]{1,0:T(8,128)(2,1)}, u32[]{:S(2)}, u32[]{:S(2)}) collective-permute-start(bf16[144,1152]{1,0:T(8,128)(2,1)S(1)} %slice.122), channel_id=1, source_target_pairs={{0,480},{8,40},{32,0},{40,72},{64,32},{72,104},{96,64},{104,136},{... | collective-permute-start | bytes 995336 | tf_op jit(solution)/shard_map/ppermute | solution.py:40
  127.2 0.8 broadcast_in_dim.19
  128.0 4.0 %all-to-all-start.3 = ((bf16[8,24,1152]{2,1,0:T(8,128)(2,1)}), bf16[8,24,1152]{2,1,0:T(8,128)(2,1)S(1)}, u32[]{:S(2)}, u32[]{:S(2)}) async-start(bf16[8,24,1152]{2,1,0:T(8,128)(2,1)} %broadcast_in_dim.19), calls=%async_computation.3 | async-start | bytes 884736 | tf_op jit(solution)/shard_map/all_to_all | solution.py:20
  131.9 2.1 %collective-permute-done.8 = bf16[120,1152]{1,0:T(8,128)(2,1)S(1)} collective-permute-done((bf16[120,1152]{1,0:T(8,128)(2,1)S(1)}, bf16[120,1152]{1,0:T(8,128)(2,1)S(1)}, u32[]{:S(2)}, u32[]{:S(2)}) %collective-permute-start.8) | collective-permute-done | bytes 276512 | tf_op jit(solution)/shard_map/ppermute | solution.py:40
  134.1 3.6 %collective-permute-done.7 = bf16[144,1152]{1,0:T(8,128)(2,1)} collective-permute-done((bf16[144,1152]{1,0:T(8,128)(2,1)S(1)}, bf16[144,1152]{1,0:T(8,128)(2,1)}, u32[]{:S(2)}, u32[]{:S(2)}) %collective-permute-start.7) | collective-permute-done | bytes 331808 | tf_op jit(solution)/shard_map/ppermute | solution.py:40
  137.6 1.0 convert_element_type.110
  138.7 1.8 fusion.54
  140.5 0.6 pad_maximum_fusion.5
  141.1 2.8 %collective-permute-start.10 = (bf16[48,1152]{1,0:T(8,128)(2,1)}, bf16[48,1152]{1,0:T(8,128)(2,1)}, u32[]{:S(2)}, u32[]{:S(2)}) collective-permute-start(bf16[48,1152]{1,0:T(8,128)(2,1)} %pad_maximum_fusion.5), channel_id=1, source_target_pairs={{0,320},{8,200},{32,352},{40,232},{64,384},{72,264},{96,416},{104,... | collective-permute-start | bytes 331784 | tf_op jit(solution)/shard_map/ppermute | solution.py:40
  143.9 4.2 %collective-permute-start.9 = (bf16[48,1152]{1,0:T(8,128)(2,1)}, bf16[48,1152]{1,0:T(8,128)(2,1)}, u32[]{:S(2)}, u32[]{:S(2)}) collective-permute-start(bf16[48,1152]{1,0:T(8,128)(2,1)} %get-tuple-element.10), channel_id=1, source_target_pairs={{0,416},{8,104},{32,448},{40,136},{64,480},{72,168},{96,0},{104,20... | collective-permute-start | bytes 331784 | tf_op jit(solution)/shard_map/ppermute | solution.py:40
  148.1 3.5 %multiply_reduce_fusion = (f32[192]{0:T(256)S(1)}, f32[192]{0:T(256)S(1)}, bf16[192,1152]{1,0:T(8,128)(2,1)}) fusion(f32[1152]{0:T(1024)S(1)} %copy-done.18, f32[192]{0:T(256)S(1)} %add_rsqrt_fusion, f32[192]{0:T(256)S(1)} %broadcast_multiply_fusion, bf16[192,1152]{1,0:T(8,128)(2,1)S(1)} %copy-done.2, bf16[1152,538]{0,1:T(8,128)(2,1)} %param.11, ...), kind=kOutput, calls=%fused_computation.39 | convolution fusion | flops 479822976 | bytes 4227072 | tf_op jit(solution)/shard_map/dot_general | solution.py:83
  151.6 1.3 fusion.9
  152.9 1.2 copy.10
  154.2 5.9 %collective-permute-done.10 = bf16[48,1152]{1,0:T(8,128)(2,1)} collective-permute-done((bf16[48,1152]{1,0:T(8,128)(2,1)}, bf16[48,1152]{1,0:T(8,128)(2,1)}, u32[]{:S(2)}, u32[]{:S(2)}) %collective-permute-start.10) | collective-permute-done | bytes 110624 | tf_op jit(solution)/shard_map/ppermute | solution.py:40
  160.1 1.6 collective-permute-done.9
  161.7 1.1 fusion.56
  162.8 0.7 copy-done.7
  163.5 2.1 %collective-permute-start.11 = (bf16[24,1152]{1,0:T(8,128)(2,1)S(1)}, bf16[24,1152]{1,0:T(8,128)(2,1)S(1)}, u32[]{:S(2)}, u32[]{:S(2)}) collective-permute-start(bf16[24,1152]{1,0:T(8,128)(2,1)S(1)} %slice.186), channel_id=1, source_target_pairs={{0,8},{8,0},{1,9},{9,1},{2,10},{10,2},{3,11},{11,3},{4,12},{12,4},... | collective-permute-start | bytes 165896 | tf_op jit(solution)/shard_map/ppermute | solution.py:25
  165.6 0.9 pad_maximum_fusion.2
  166.5 3.8 %all-to-all-start.4 = ((bf16[8,192,148]{1,2,0:T(8,128)(2,1)}), bf16[8,192,148]{1,2,0:T(8,128)(2,1)S(1)}, u32[]{:S(2)}, u32[]{:S(2)}) async-start(bf16[8,192,148]{1,2,0:T(8,128)(2,1)} %pad_maximum_fusion.2), calls=%async_computation.4 | async-start | bytes 1245184 | tf_op jit(solution)/shard_map/all_to_all | solution.py:20
  170.4 0.9 fusion.62
  171.4 11.1 %all-to-all-done.4 = bf16[8,192,148]{1,2,0:T(8,128)(2,1)S(1)} async-done(((bf16[8,192,148]{1,2,0:T(8,128)(2,1)}), bf16[8,192,148]{1,2,0:T(8,128)(2,1)S(1)}, u32[]{:S(2)}, u32[]{:S(2)}) %all-to-all-start.4) | async-done | bytes 454688 | tf_op jit(solution)/shard_map/all_to_all | solution.py:20
  182.5 0.8 broadcast_in_dim.21
  183.3 3.9 %all-to-all-start.5 = ((bf16[8,24,1152]{2,1,0:T(8,128)(2,1)}), bf16[8,24,1152]{2,1,0:T(8,128)(2,1)S(1)}, u32[]{:S(2)}, u32[]{:S(2)}) async-start(bf16[8,24,1152]{2,1,0:T(8,128)(2,1)} %broadcast_in_dim.21), calls=%async_computation.5 | async-start | bytes 884736 | tf_op jit(solution)/shard_map/all_to_all | solution.py:20
  187.4 1.3 fusion.16
  188.7 8.3 %all-to-all-done.5 = bf16[8,24,1152]{2,1,0:T(8,128)(2,1)S(1)} async-done(((bf16[8,24,1152]{2,1,0:T(8,128)(2,1)}), bf16[8,24,1152]{2,1,0:T(8,128)(2,1)S(1)}, u32[]{:S(2)}, u32[]{:S(2)}) %all-to-all-start.5) | async-done | bytes 442400 | tf_op jit(solution)/shard_map/all_to_all | solution.py:20
  197.0 1.0 fusion.83
  (76 shorter events, 1.6 us)
Async XLA Ops:
  0.6 4.7 %copy-start = (bf16[538,1152]{1,0:T(8,128)(2,1)S(1)}, bf16[538,1152]{1,0:T(8,128)(2,1)}, u32[]{:S(2)}) copy-start(bf16[538,1152]{1,0:T(8,128)(2,1)} %param.12) | copy-start | bytes 3718660
  5.3 1.5 copy-start.19
  5.3 1.2 copy-start.5
  5.4 1.2 copy-start.17
  7.9 21.4 %copy-start.2 = (bf16[192,1152]{1,0:T(8,128)(2,1)S(1)}, bf16[192,1152]{1,0:T(8,128)(2,1)}, u32[]{:S(2)}) copy-start(bf16[192,1152]{1,0:T(8,128)(2,1)} %param.8) | copy-start | bytes 1327108
  7.9 21.2 %all-to-all-start = ((bf16[8,48,1152]{2,1,0:T(8,128)(2,1)}), bf16[8,48,1152]{2,1,0:T(8,128)(2,1)S(1)}, u32[]{:S(2)}, u32[]{:S(2)}) async-start(bf16[8,48,1152]{2,1,0:T(8,128)(2,1)} %pad_maximum_fusion), calls=%async_computation | async-start | bytes 1769472 | tf_op jit(solution)/shard_map/all_to_all | solution.py:20
  30.1 38.9 %copy-start.3 = (bf16[24,1152]{1,0:T(8,128)(2,1)}, bf16[24,1152]{1,0:T(8,128)(2,1)S(1)}, u32[]{:S(2)}) copy-start(bf16[24,1152]{1,0:T(8,128)(2,1)S(1)} %get-tuple-element.9) | copy-start | bytes 165892
  30.1 3.2 %collective-permute-start = (bf16[24,1152]{1,0:T(8,128)(2,1)S(1)}, bf16[24,1152]{1,0:T(8,128)(2,1)S(1)}, u32[]{:S(2)}, u32[]{:S(2)}) collective-permute-start(bf16[24,1152]{1,0:T(8,128)(2,1)S(1)} %get-tuple-element.9), channel_id=1, source_target_pairs={{0,8},{8,0},{1,9},{9,1},{2,10},{10,2},{3,11},{11,3},{4,12},{12,4},... | collective-permute-start | bytes 165896 | tf_op jit(solution)/shard_map/ppermute | solution.py:25
  33.3 34.6 %copy-start.16 = (bf16[24,1152]{1,0:T(8,128)(2,1)}, bf16[24,1152]{1,0:T(8,128)(2,1)S(1)}, u32[]{:S(2)}) copy-start(bf16[24,1152]{1,0:T(8,128)(2,1)S(1)} %collective-permute-done) | copy-start | bytes 165892
  33.3 16.9 %collective-permute-start.1 = (bf16[48,1152]{1,0:T(8,128)(2,1)S(1)}, bf16[48,1152]{1,0:T(8,128)(2,1)S(1)}, u32[]{:S(2)}, u32[]{:S(2)}) collective-permute-start(bf16[48,1152]{1,0:T(8,128)(2,1)S(1)} %pad_maximum_fusion.4), channel_id=1, source_target_pairs={{0,96},{8,424},{32,128},{40,456},{64,160},{72,488},{96,192},{104,8... | collective-permute-start | bytes 331784 | tf_op jit(solution)/shard_map/ppermute | solution.py:40
  41.1 18.1 %collective-permute-start.2 = (bf16[48,1152]{1,0:T(8,128)(2,1)S(1)}, bf16[48,1152]{1,0:T(8,128)(2,1)S(1)}, u32[]{:S(2)}, u32[]{:S(2)}) collective-permute-start(bf16[48,1152]{1,0:T(8,128)(2,1)S(1)} %pad_maximum_fusion.4), channel_id=1, source_target_pairs={{0,192},{8,328},{32,224},{40,360},{64,256},{72,392},{96,288},{104,... | collective-permute-start | bytes 331784 | tf_op jit(solution)/shard_map/ppermute | solution.py:40
  50.2 18.8 %copy-start.9 = (bf16[48,1152]{1,0:T(8,128)(2,1)}, bf16[48,1152]{1,0:T(8,128)(2,1)S(1)}, u32[]{:S(2)}) copy-start(bf16[48,1152]{1,0:T(8,128)(2,1)S(1)} %collective-permute-done.1) | copy-start | bytes 331780
  59.1 9.9 %copy-start.11 = (bf16[48,1152]{1,0:T(8,128)(2,1)}, bf16[48,1152]{1,0:T(8,128)(2,1)S(1)}, u32[]{:S(2)}) copy-start(bf16[48,1152]{1,0:T(8,128)(2,1)S(1)} %collective-permute-done.2) | copy-start | bytes 331780
  59.2 16.1 %collective-permute-start.3 = (bf16[144,1152]{1,0:T(8,128)(2,1)S(1)}, bf16[144,1152]{1,0:T(8,128)(2,1)S(1)}, u32[]{:S(2)}, u32[]{:S(2)}) collective-permute-start(bf16[144,1152]{1,0:T(8,128)(2,1)S(1)} %pad_maximum_fusion.3), channel_id=1, source_target_pairs={{0,32},{8,488},{32,64},{40,8},{64,96},{72,40},{96,128},{104,72},{1... | collective-permute-start | bytes 995336 | tf_op jit(solution)/shard_map/ppermute | solution.py:40
  61.8 13.4 %collective-permute-start.4 = (bf16[120,1152]{1,0:T(8,128)(2,1)}, bf16[120,1152]{1,0:T(8,128)(2,1)S(1)}, u32[]{:S(2)}, u32[]{:S(2)}) collective-permute-start(bf16[120,1152]{1,0:T(8,128)(2,1)} %slice.112), channel_id=1, source_target_pairs={{0,64},{8,456},{32,96},{40,488},{64,128},{72,8},{96,160},{104,40},... | collective-permute-start | bytes 829448 | tf_op jit(solution)/shard_map/ppermute | solution.py:40
  68.0 1.0 copy-start.13
  69.0 20.3 %all-to-all-start.1 = ((bf16[16,24,1152]{2,1,0:T(8,128)(2,1)}), bf16[16,24,1152]{2,1,0:T(8,128)(2,1)S(1)}, u32[]{:S(2)}, u32[]{:S(2)}) async-start(bf16[16,24,1152]{2,1,0:T(8,128)(2,1)} %broadcast_in_dim.18), calls=%async_computation.1 | async-start | bytes 1769472 | tf_op jit(solution)/shard_map/all_to_all | solution.py:20
  73.2 5.0 %copy-start.10 = (bf16[48,1152]{1,0:T(8,128)(2,1)S(1)}, bf16[48,1152]{1,0:T(8,128)(2,1)}, u32[]{:S(2)}) copy-start(bf16[48,1152]{1,0:T(8,128)(2,1)} %copy-done.9) | copy-start | bytes 331780
  73.2 5.7 %copy-start.12 = (bf16[48,1152]{1,0:T(8,128)(2,1)S(1)}, bf16[48,1152]{1,0:T(8,128)(2,1)}, u32[]{:S(2)}) copy-start(bf16[48,1152]{1,0:T(8,128)(2,1)} %copy-done.11) | copy-start | bytes 331780
  76.3 4.8 %collective-permute-start.5 = (bf16[360,1152]{1,0:T(8,128)(2,1)S(1)}, bf16[360,1152]{1,0:T(8,128)(2,1)S(1)}, u32[]{:S(2)}, u32[]{:S(2)}) collective-permute-start(bf16[360,1152]{1,0:T(8,128)(2,1)S(1)} %pad_maximum_fusion.1), channel_id=1, source_target_pairs={{0,8},{8,0},{1,9},{9,1},{2,10},{10,2},{3,11},{11,3},{4,12},{12,4},... | collective-permute-start | bytes 2488328 | tf_op jit(solution)/shard_map/ppermute | solution.py:25
  92.2 7.0 %copy-start.15 = (bf16[768,384]{1,0:T(8,128)(2,1)}, bf16[768,384]{1,0:T(8,128)(2,1)S(1)}, u32[]{:S(2)}) copy-start(bf16[768,384]{1,0:T(8,128)(2,1)S(1)} %fusion.7) | copy-start | bytes 1769476
  92.2 3.5 %copy-start.18 = (f32[1152]{0:T(1024)S(1)}, f32[1152]{0:T(1024)}, u32[]{:S(2)}) copy-start(f32[1152]{0:T(1024)} %param.10) | copy-start | bytes 13828
  93.8 11.2 %collective-permute-start.6 = (bf16[360,1152]{1,0:T(8,128)(2,1)}, bf16[360,1152]{1,0:T(8,128)(2,1)}, u32[]{:S(2)}, u32[]{:S(2)}) collective-permute-start(bf16[360,1152]{1,0:T(8,128)(2,1)} %convolution_convert_fusion.1), channel_id=1, source_target_pairs={{0,8},{8,0},{1,9},{9,1},{2,10},{10,2},{3,11},{11,3},{4,12},{12,4},... | collective-permute-start | bytes 2488328 | tf_op jit(solution)/shard_map/ppermute | solution.py:25
  99.2 21.4 %all-to-all-start.2 = ((bf16[16,24,1152]{2,1,0:T(8,128)(2,1)}), bf16[16,24,1152]{2,1,0:T(8,128)(2,1)S(1)}, u32[]{:S(2)}, u32[]{:S(2)}) async-start(bf16[16,24,1152]{2,1,0:T(8,128)(2,1)} %bitcast.44), calls=%async_computation.2 | async-start | bytes 1769472 | tf_op jit(solution)/shard_map/all_to_all | solution.py:20
  105.0 3.2 %copy-start.1 = (f32[408,1152]{1,0:T(8,128)}, f32[408,1152]{1,0:T(8,128)S(1)}, u32[]{:S(2)}) copy-start(f32[408,1152]{1,0:T(8,128)S(1)} %fusion.39) | copy-start | bytes 5640196
  108.2 12.6 %copy-start.14 = (bf16[24,1152]{1,0:T(8,128)(2,1)S(1)}, bf16[24,1152]{1,0:T(8,128)(2,1)}, u32[]{:S(2)}) copy-start(bf16[24,1152]{1,0:T(8,128)(2,1)} %copy-done.13) | copy-start | bytes 165892
  120.9 13.2 %collective-permute-start.8 = (bf16[120,1152]{1,0:T(8,128)(2,1)S(1)}, bf16[120,1152]{1,0:T(8,128)(2,1)S(1)}, u32[]{:S(2)}, u32[]{:S(2)}) collective-permute-start(bf16[120,1152]{1,0:T(8,128)(2,1)S(1)} %slice.124), channel_id=1, source_target_pairs={{0,448},{8,72},{32,480},{40,104},{64,0},{72,136},{96,32},{104,168}... | collective-permute-start | bytes 829448 | tf_op jit(solution)/shard_map/ppermute | solution.py:40
  123.3 14.3 %collective-permute-start.7 = (bf16[144,1152]{1,0:T(8,128)(2,1)S(1)}, bf16[144,1152]{1,0:T(8,128)(2,1)}, u32[]{:S(2)}, u32[]{:S(2)}) collective-permute-start(bf16[144,1152]{1,0:T(8,128)(2,1)S(1)} %slice.122), channel_id=1, source_target_pairs={{0,480},{8,40},{32,0},{40,72},{64,32},{72,104},{96,64},{104,136},{... | collective-permute-start | bytes 995336 | tf_op jit(solution)/shard_map/ppermute | solution.py:40
  128.0 20.1 %all-to-all-start.3 = ((bf16[8,24,1152]{2,1,0:T(8,128)(2,1)}), bf16[8,24,1152]{2,1,0:T(8,128)(2,1)S(1)}, u32[]{:S(2)}, u32[]{:S(2)}) async-start(bf16[8,24,1152]{2,1,0:T(8,128)(2,1)} %broadcast_in_dim.19), calls=%async_computation.3 | async-start | bytes 884736 | tf_op jit(solution)/shard_map/all_to_all | solution.py:20
  141.1 19.0 %collective-permute-start.10 = (bf16[48,1152]{1,0:T(8,128)(2,1)}, bf16[48,1152]{1,0:T(8,128)(2,1)}, u32[]{:S(2)}, u32[]{:S(2)}) collective-permute-start(bf16[48,1152]{1,0:T(8,128)(2,1)} %pad_maximum_fusion.5), channel_id=1, source_target_pairs={{0,320},{8,200},{32,352},{40,232},{64,384},{72,264},{96,416},{104,... | collective-permute-start | bytes 331784 | tf_op jit(solution)/shard_map/ppermute | solution.py:40
  143.9 17.8 %collective-permute-start.9 = (bf16[48,1152]{1,0:T(8,128)(2,1)}, bf16[48,1152]{1,0:T(8,128)(2,1)}, u32[]{:S(2)}, u32[]{:S(2)}) collective-permute-start(bf16[48,1152]{1,0:T(8,128)(2,1)} %get-tuple-element.10), channel_id=1, source_target_pairs={{0,416},{8,104},{32,448},{40,136},{64,480},{72,168},{96,0},{104,20... | collective-permute-start | bytes 331784 | tf_op jit(solution)/shard_map/ppermute | solution.py:40
  162.8 0.7 copy-start.7
  163.5 7.8 %copy-start.4 = (bf16[24,1152]{1,0:T(8,128)(2,1)S(1)}, bf16[24,1152]{1,0:T(8,128)(2,1)}, u32[]{:S(2)}) copy-start(bf16[24,1152]{1,0:T(8,128)(2,1)} %copy-done.3) | copy-start | bytes 165892
  163.5 6.9 %copy-start.8 = (f32[48,1152]{1,0:T(8,128)S(1)}, f32[48,1152]{1,0:T(8,128)}, u32[]{:S(2)}) copy-start(f32[48,1152]{1,0:T(8,128)} %copy-done.7) | copy-start | bytes 663556
  163.5 6.8 %collective-permute-start.11 = (bf16[24,1152]{1,0:T(8,128)(2,1)S(1)}, bf16[24,1152]{1,0:T(8,128)(2,1)S(1)}, u32[]{:S(2)}, u32[]{:S(2)}) collective-permute-start(bf16[24,1152]{1,0:T(8,128)(2,1)S(1)} %slice.186), channel_id=1, source_target_pairs={{0,8},{8,0},{1,9},{9,1},{2,10},{10,2},{3,11},{11,3},{4,12},{12,4},... | collective-permute-start | bytes 165896 | tf_op jit(solution)/shard_map/ppermute | solution.py:25
  166.5 20.9 %copy-start.20 = (f32[192,144]{0,1:T(8,128)S(1)}, f32[192,144]{0,1:T(8,128)}, u32[]{:S(2)}) copy-start(f32[192,144]{0,1:T(8,128)} %fusion.9) | copy-start | bytes 331780
  166.5 16.0 %all-to-all-start.4 = ((bf16[8,192,148]{1,2,0:T(8,128)(2,1)}), bf16[8,192,148]{1,2,0:T(8,128)(2,1)S(1)}, u32[]{:S(2)}, u32[]{:S(2)}) async-start(bf16[8,192,148]{1,2,0:T(8,128)(2,1)} %pad_maximum_fusion.2), calls=%async_computation.4 | async-start | bytes 1245184 | tf_op jit(solution)/shard_map/all_to_all | solution.py:20
  171.4 25.6 %copy-start.6 = (bf16[144,1152]{1,0:T(8,128)(2,1)S(1)}, bf16[144,1152]{1,0:T(8,128)(2,1)}, u32[]{:S(2)}) copy-start(bf16[144,1152]{1,0:T(8,128)(2,1)} %param.13) | copy-start | bytes 995332
  183.3 13.7 %all-to-all-start.5 = ((bf16[8,24,1152]{2,1,0:T(8,128)(2,1)}), bf16[8,24,1152]{2,1,0:T(8,128)(2,1)S(1)}, u32[]{:S(2)}, u32[]{:S(2)}) async-start(bf16[8,24,1152]{2,1,0:T(8,128)(2,1)} %broadcast_in_dim.21), calls=%async_computation.5 | async-start | bytes 884736 | tf_op jit(solution)/shard_map/all_to_all | solution.py:20

commit v3 on v2

--- a/solution.py
+++ b/solution.py
@@ -1,6 +1,7 @@
 import jax
 import jax.numpy as jnp
 from jax import lax
+from jax.experimental import pallas as pl
 from jax.sharding import Mesh
 from jax.sharding import PartitionSpec as P
 
@@ -67,6 +68,60 @@
     total = here + three.astype(F32) + six.astype(F32)
     partner = exchange(total[share:].astype(BF16), "c", 1)
     return total[:share] + partner.astype(F32)
+
+
+LANES = 128
+SUM_ROWS = 16
+
+
+def pack_kernel(back_ref, sums_ref, text_ref, out_ref):
+    heads = out_ref.shape[0]
+    cols = back_ref.shape[0] // heads
+    rows = back_ref.shape[1]
+    share, width = text_ref.shape
+    for h in range(heads):
+        block = back_ref[h * cols : (h + 1) * cols, :]
+        out_ref[h, :cols, :] = block[:, :LANES]
+        out_ref[h, cols : 2 * cols, : rows - LANES] = block[:, LANES:]
+        out_ref[h, cols : 2 * cols, rows - LANES :] = jnp.zeros((cols, 2 * LANES - rows), BF16)
+        out_ref[h, 2 * cols : 2 * cols + SUM_ROWS, :] = sums_ref[...]
+        for k in range(width // LANES):
+            first = 2 * cols + SUM_ROWS + k * share
+            out_ref[h, first : first + share, :] = text_ref[:, k * LANES : (k + 1) * LANES]
+
+
+def finish_kernel(
+    packed_ref, direct_ref, centred_ref, inv_ref, gain_ref, mapping_ref, image_ref, text_ref, rows_ref
+):
+    heads = packed_ref.shape[0]
+    cols, rows = direct_ref.shape
+    width = mapping_ref.shape[1]
+    share = rows // heads
+    sums = packed_ref[0, 2 * cols : 2 * cols + SUM_ROWS, :].astype(F32)
+    for h in range(1, heads):
+        sums = sums + packed_ref[h, 2 * cols : 2 * cols + SUM_ROWS, :].astype(F32)
+    for half, span in enumerate((LANES, rows - LANES)):
+        here = slice(half * LANES, half * LANES + span)
+        total = packed_ref[0, half * cols : (half + 1) * cols, :span].astype(F32)
+        for h in range(1, heads):
+            total = total + packed_ref[h, half * cols : (half + 1) * cols, :span].astype(F32)
+        one = (sums[half : half + 1, :span] + sums[half + 4 : half + 5, :span]) / width
+        two = (sums[half + 2 : half + 3, :span] + sums[half + 6 : half + 7, :span]) / width
+        image_ref[:, here] = direct_ref[:, here] + inv_ref[:, here] * (
+            total * gain_ref[...] - one - centred_ref[:, here] * two
+        )
+    for h in range(heads):
+        for k in range(width // LANES):
+            first = 2 * cols + SUM_ROWS + k * share
+            rows_ref[h * share : (h + 1) * share, k * LANES : (k + 1) * LANES] = packed_ref[
+                h, first : first + share, :
+            ]
+    text_ref[...] = lax.dot_general(
+        mapping_ref[...],
+        rows_ref[...],
+        (((1,), (1,)), ((), ())),
+        preferred_element_type=F32,
+    )
 
 
 def gelu_tanh(values):
@@ -100,6 +155,7 @@
     centred = (image_float - mean_row) * inv_std
     normed = (centred * gain).astype(BF16)
     preact = dot(normed, entry, ((1,), (0,)))
+    entry_gain = jnp.sum(entry.astype(F32) * gain[:, None], axis=0)
     hidden = gelu_tanh(preact).astype(BF16)
     partial_out = dot(hidden, exit_matrix, ((1,), (0,))).astype(BF16)
     own_rows = lax.dynamic_slice_in_dim(picture, first_row, share, 0).astype(F32)
@@ -137,34 +193,34 @@
     grad_text_share = norm_back(text_dir, unit_text, inv_text).astype(BF16)
 
     grad_hidden = dot(grad_out_b, exit_matrix, ((1,), (1,)))
-    _, pull_back = jax.vjp(gelu_tanh, preact)
+    unused, pull_back = jax.vjp(gelu_tanh, preact)
     grad_pre = pull_back(grad_hidden)[0].astype(BF16)
-    partial_normed = dot(grad_pre, entry, ((1,), (1,)))
-    scaled_part = partial_normed * gain
+    back = dot(entry, grad_pre, ((1,), (1,))).astype(BF16)
+    pre_float = grad_pre.astype(F32)
     row_sums = jnp.stack(
-        [jnp.sum(scaled_part, axis=-1), jnp.sum(scaled_part * centred, axis=-1)], axis=-1
+        [jnp.sum(pre_float * entry_gain, axis=-1), jnp.sum(pre_float * preact, axis=-1)]
     )
     sums_high = lax.reduce_precision(row_sums, 8, 7)
     sums_low = row_sums - sums_high
-    sums_both = jnp.concatenate([sums_high, sums_low], axis=-1).astype(BF16)
-    blocks = partial_normed.astype(BF16).reshape(rows, heads, cols).transpose(1, 0, 2)
-    packed = jnp.concatenate(
-        [blocks, jnp.broadcast_to(sums_both[None], (heads, *sums_both.shape))], axis=2
-    )
-    arrived = jnp.sum(swap(packed, MP).astype(F32), axis=0)
-    means = (arrived[:, cols : cols + 2] + arrived[:, cols + 2 :]) / width
+    sums_both = jnp.concatenate([sums_high, sums_low], axis=0).astype(BF16)
+    sums_both = jnp.pad(sums_both, ((0, 0), (0, 2 * LANES - rows))).reshape(-1, LANES)
+    sums_both = jnp.pad(sums_both, ((0, SUM_ROWS - sums_both.shape[0]), (0, 0)))
+    length = 2 * cols + SUM_ROWS + share * width // LANES
+    packed = pl.pallas_call(
+        pack_kernel, out_shape=jax.ShapeDtypeStruct((heads, length, LANES), BF16)
+    )(back, sums_both, grad_text_share)
+    arrived = swap(packed, MP)
     gain_here = lax.dynamic_slice_in_dim(gain, first_col, cols, 0)
-    feature = jnp.arange(width, dtype=jnp.int32)[:, None] - first_col
-    chosen = (feature == jnp.arange(cols, dtype=jnp.int32)[None, :]).astype(BF16)
-    picture_here = dot(picture, chosen, ((1,), (0,)))
-    centred_here = (picture_here - mean_row) * inv_std
-    grad_out_here = dot(grad_out_b, chosen, ((1,), (0,)))
-    scaled = arrived[:, :cols] * gain_here
-    grad_image = grad_out_here + inv_std * (
-        scaled - means[:, :1] - centred_here * means[:, 1:]
-    )
-    grad_text = dot(spread(grad_text_share, MP), mapping, ((1,), (1,)))
-    return (grad_image, grad_text)
+    feature = jnp.arange(width, dtype=jnp.int32)[None, :] - first_col
+    chosen = (feature == jnp.arange(cols, dtype=jnp.int32)[:, None]).astype(BF16)
+    picture_here = dot(chosen, picture, ((1,), (1,)))
+    centred_here = (picture_here - mean_row.T) * inv_std.T
+    direct = dot(chosen, grad_out_b, ((1,), (1,)))
+    outs = jax.ShapeDtypeStruct((cols, rows), F32)
+    grad_image, grad_text, unused = pl.pallas_call(
+        finish_kernel, out_shape=(outs, outs, jax.ShapeDtypeStruct((rows, width), BF16))
+    )(arrived, direct, centred_here, inv_std.T, gain_here[:, None], mapping)
+    return (grad_image.T, grad_text.T)
 
 
 def solution(mesh):

time: 199 us -> 198 us (level)
  the two profiles are of different devices: /device:TPU:64 before, /device:TPU:1 now
where the time goes in v3:
time: 198 us; the launch traced here: 197 us
  starting transfers between devices  79 us (40%)
  waiting for transfers between devices  57.5 us (29%)
  other arithmetic  18.3 us (9%)
  local copies, waits for them, and re-layouts  17.5 us (9%)
  matrix products  17 us (9%)
  Pallas kernels  4.93 us (2%)
  between operations  2.37 us (1%)
    ppermute x8, starting transfers between devices, along(): return lax.ppermute(array, LINE, moves)  38.9 us
    all_to_all x5, waiting for transfers between devices, swap(): return lax.all_to_all(array, axes, 0, 0, tiled=True)  37.6 us
    all_to_all x5, starting transfers between devices, swap(): return lax.all_to_all(array, axes, 0, 0, tiled=True)  24.1 us
    ppermute x8, waiting for transfers between devices, along(): return lax.ppermute(array, LINE, moves)  19.9 us
    dot_general x11, matrix products, dot(): return lax.dot_general(a, b, (dims, ((), ())), preferred_element_type=F32)  17 us
    ppermute x4, starting transfers between devices, exchange(): return lax.ppermute(array, axes, [(i, i ^ k) for i in range(n)])  16 us
    unnamed x43, local copies, waits for them, and re-layouts  8.69 us
  transfers between devices with their start and end apart: 17, of which 10 were waited for; matrix products, arithmetic and copies ran while one was open for 16% of the time, Pallas kernels for 0%

profile of v3, /device:TPU:1, one launch (start us, length us, event | category | flops | bytes accessed | tf_op | source)
XLA Modules:
  0.0 196.6 jit_solution(3083543555211007340)
XLA Ops:
  0.7 1.3 convert_reduce_fusion.2
  2.0 1.3 fusion.12
  3.3 1.4 convolution_convert_fusion.4
  5.4 0.8 copy-done.18
  6.7 1.0 pad_maximum_fusion
  7.7 7.5 %all-to-all-start = ((bf16[8,48,1152]{2,1,0:T(8,128)(2,1)}), bf16[8,48,1152]{2,1,0:T(8,128)(2,1)S(1)}, u32[]{:S(2)}, u32[]{:S(2)}) async-start(bf16[8,48,1152]{2,1,0:T(8,128)(2,1)} %pad_maximum_fusion), calls=%async_computation | async-start | bytes 1769472 | tf_op jit(solution)/shard_map/all_to_all | solution.py:21
  15.2 11.1 %all-to-all-done = bf16[8,48,1152]{2,1,0:T(8,128)(2,1)S(1)} async-done(((bf16[8,48,1152]{2,1,0:T(8,128)(2,1)}), bf16[8,48,1152]{2,1,0:T(8,128)(2,1)S(1)}, u32[]{:S(2)}, u32[]{:S(2)}) %all-to-all-start) | async-done | bytes 884768 | tf_op jit(solution)/shard_map/all_to_all | solution.py:21
  26.4 1.0 multiply_reduce_fusion.2
  27.4 0.7 constant_dynamic-update-slice_fusion.6
  28.1 6.4 %collective-permute-start = (bf16[24,1152]{1,0:T(8,128)(2,1)S(1)}, bf16[24,1152]{1,0:T(8,128)(2,1)S(1)}, u32[]{:S(2)}, u32[]{:S(2)}) collective-permute-start(bf16[24,1152]{1,0:T(8,128)(2,1)S(1)} %get-tuple-element.14), channel_id=1, source_target_pairs={{0,8},{8,0},{1,9},{9,1},{2,10},{10,2},{3,11},{11,3},{4,12},{12,4},... | collective-permute-start | bytes 165896 | tf_op jit(solution)/shard_map/ppermute | solution.py:26
  35.9 14.1 %collective-permute-start.2 = (bf16[48,1152]{1,0:T(8,128)(2,1)S(1)}, bf16[48,1152]{1,0:T(8,128)(2,1)S(1)}, u32[]{:S(2)}, u32[]{:S(2)}) collective-permute-start(bf16[48,1152]{1,0:T(8,128)(2,1)S(1)} %pad_maximum_fusion.3), channel_id=1, source_target_pairs={{0,192},{8,328},{32,224},{40,360},{64,256},{72,392},{96,288},{104,... | collective-permute-start | bytes 331784 | tf_op jit(solution)/shard_map/ppermute | solution.py:41
  50.0 2.6 %collective-permute-start.1 = (bf16[48,1152]{1,0:T(8,128)(2,1)S(1)}, bf16[48,1152]{1,0:T(8,128)(2,1)S(1)}, u32[]{:S(2)}, u32[]{:S(2)}) collective-permute-start(bf16[48,1152]{1,0:T(8,128)(2,1)S(1)} %pad_maximum_fusion.3), channel_id=1, source_target_pairs={{0,96},{8,424},{32,128},{40,456},{64,160},{72,488},{96,192},{104,8... | collective-permute-start | bytes 331784 | tf_op jit(solution)/shard_map/ppermute | solution.py:41
  52.6 4.0 %collective-permute-done.2 = bf16[48,1152]{1,0:T(8,128)(2,1)S(1)} collective-permute-done((bf16[48,1152]{1,0:T(8,128)(2,1)S(1)}, bf16[48,1152]{1,0:T(8,128)(2,1)S(1)}, u32[]{:S(2)}, u32[]{:S(2)}) %collective-permute-start.2) | collective-permute-done | bytes 110624 | tf_op jit(solution)/shard_map/ppermute | solution.py:41
  56.7 4.2 %collective-permute-done.1 = bf16[48,1152]{1,0:T(8,128)(2,1)S(1)} collective-permute-done((bf16[48,1152]{1,0:T(8,128)(2,1)S(1)}, bf16[48,1152]{1,0:T(8,128)(2,1)S(1)}, u32[]{:S(2)}, u32[]{:S(2)}) %collective-permute-start.1) | collective-permute-done | bytes 110624 | tf_op jit(solution)/shard_map/ppermute | solution.py:41
  60.9 0.8 pad_maximum_fusion.2
  61.6 1.7 slice.92
  63.3 1.9 collective-permute-start.3
  65.2 7.1 %collective-permute-start.4 = (bf16[120,1152]{1,0:T(8,128)(2,1)}, bf16[120,1152]{1,0:T(8,128)(2,1)}, u32[]{:S(2)}, u32[]{:S(2)}) collective-permute-start(bf16[120,1152]{1,0:T(8,128)(2,1)} %slice.92), channel_id=1, source_target_pairs={{0,64},{8,456},{32,96},{40,488},{64,128},{72,8},{96,160},{104,40},... | collective-permute-start | bytes 829448 | tf_op jit(solution)/shard_map/ppermute | solution.py:41
  72.4 1.0 multiply_convert_fusion.2
  73.3 1.0 broadcast_in_dim.16
  74.3 3.9 %all-to-all-start.1 = ((bf16[16,24,1152]{2,1,0:T(8,128)(2,1)}), bf16[16,24,1152]{2,1,0:T(8,128)(2,1)S(1)}, u32[]{:S(2)}, u32[]{:S(2)}) async-start(bf16[16,24,1152]{2,1,0:T(8,128)(2,1)} %broadcast_in_dim.16), calls=%async_computation.1 | async-start | bytes 1769472 | tf_op jit(solution)/shard_map/all_to_all | solution.py:21
  78.3 1.5 constant_dynamic-update-slice_fusion.5
  79.7 1.2 pad_maximum_fusion.1
  80.9 1.9 collective-permute-start.5
  84.2 1.7 constant_dynamic-update-slice_fusion.2
  85.9 1.7 constant_dynamic-update-slice_fusion.1
  87.6 1.0 constant_dynamic-update-slice_fusion
  88.6 4.6 %all-to-all-done.1 = bf16[16,24,1152]{2,1,0:T(8,128)(2,1)S(1)} async-done(((bf16[16,24,1152]{2,1,0:T(8,128)(2,1)}), bf16[16,24,1152]{2,1,0:T(8,128)(2,1)S(1)}, u32[]{:S(2)}, u32[]{:S(2)}) %all-to-all-start.1) | async-done | bytes 884768 | tf_op jit(solution)/shard_map/all_to_all | solution.py:21
  93.2 2.9 %fusion.7 = bf16[768,384]{1,0:T(8,128)(2,1)S(1)} fusion(bf16[768,1152]{1,0:T(8,128)(2,1)} %constant_dynamic-update-slice_fusion, bf16[384,1152]{1,0:T(8,128)(2,1)S(1)} %bitcast.28, f32[]{:T(128)S(6)} %copy.22, s32[384]{0:T(512)S(1)} %iota_subtract_fusion.1, f32[]{:T(128)S(6)} %copy.21, pred[768]{0:T(1024)(128)(4,1)S(1)} %iota_compare_fusion.5), kind=kOutput, calls=%fused_computation.17 | convolution fusion | flops 683311104 | bytes 3246344 | tf_op jit(solution)/shard_map/dot_general | solution.py:138
  96.1 1.5 convolution_convert_fusion.1
  97.7 1.9 collective-permute-start.6
  99.9 1.9 convolution_convert_fusion
  101.8 4.3 %all-to-all-start.2 = ((bf16[16,24,1152]{2,1,0:T(8,128)(2,1)}), bf16[16,24,1152]{2,1,0:T(8,128)(2,1)}, u32[]{:S(2)}, u32[]{:S(2)}) async-start(bf16[16,24,1152]{2,1,0:T(8,128)(2,1)} %bitcast.33), calls=%async_computation.2 | async-start | bytes 1769472 | tf_op jit(solution)/shard_map/all_to_all | solution.py:21
  106.1 1.7 fusion.32
  107.8 3.2 %fusion.59 = (bf16[360,1152]{1,0:T(8,128)(2,1)S(1)}, f32[360,1152]{1,0:T(8,128)}) fusion(bf16[360,1152]{1,0:T(8,128)(2,1)} %collective-permute-done.6, f32[408,1152]{1,0:T(8,128)S(1)} %fusion.32), kind=kLoop, calls=%fused_computation.119 | loop fusion | flops 1244160 | bytes 4976640 | tf_op jit(solution)/shard_map/convert.5
  111.0 0.7 slice.99
  111.8 9.0 %all-to-all-done.2 = bf16[16,24,1152]{2,1,0:T(8,128)(2,1)} async-done(((bf16[16,24,1152]{2,1,0:T(8,128)(2,1)}), bf16[16,24,1152]{2,1,0:T(8,128)(2,1)}, u32[]{:S(2)}, u32[]{:S(2)}) %all-to-all-start.2) | async-done | bytes 884768 | tf_op jit(solution)/shard_map/all_to_all | solution.py:21
  120.8 1.3 convert_reduce_fusion
  122.2 2.5 %collective-permute-start.8 = (bf16[120,1152]{1,0:T(8,128)(2,1)}, bf16[120,1152]{1,0:T(8,128)(2,1)S(1)}, u32[]{:S(2)}, u32[]{:S(2)}) collective-permute-start(bf16[120,1152]{1,0:T(8,128)(2,1)} %slice.99), channel_id=1, source_target_pairs={{0,448},{8,72},{32,480},{40,104},{64,0},{72,136},{96,32},{104,168}... | collective-permute-start | bytes 829448 | tf_op jit(solution)/shard_map/ppermute | solution.py:41
  124.7 3.2 %collective-permute-start.7 = (bf16[144,1152]{1,0:T(8,128)(2,1)S(1)}, bf16[144,1152]{1,0:T(8,128)(2,1)}, u32[]{:S(2)}, u32[]{:S(2)}) collective-permute-start(bf16[144,1152]{1,0:T(8,128)(2,1)S(1)} %slice.97), channel_id=1, source_target_pairs={{0,480},{8,40},{32,0},{40,72},{64,32},{72,104},{96,64},{104,136},{... | collective-permute-start | bytes 995336 | tf_op jit(solution)/shard_map/ppermute | solution.py:41
  128.0 0.8 broadcast_in_dim.17
  128.9 4.5 %all-to-all-start.3 = ((bf16[8,24,1152]{2,1,0:T(8,128)(2,1)}), bf16[8,24,1152]{2,1,0:T(8,128)(2,1)}, u32[]{:S(2)}, u32[]{:S(2)}) async-start(bf16[8,24,1152]{2,1,0:T(8,128)(2,1)} %broadcast_in_dim.17), calls=%async_computation.3 | async-start | bytes 884736 | tf_op jit(solution)/shard_map/all_to_all | solution.py:21
  133.3 1.2 collective-permute-done.8
  134.6 3.8 %collective-permute-done.7 = bf16[144,1152]{1,0:T(8,128)(2,1)} collective-permute-done((bf16[144,1152]{1,0:T(8,128)(2,1)S(1)}, bf16[144,1152]{1,0:T(8,128)(2,1)}, u32[]{:S(2)}, u32[]{:S(2)}) %collective-permute-start.7) | collective-permute-done | bytes 331808 | tf_op jit(solution)/shard_map/ppermute | solution.py:41
  138.4 1.0 convert_element_type.117
  139.4 1.8 fusion.39
  141.2 3.5 %collective-permute-start.10 = (bf16[48,1152]{1,0:T(8,128)(2,1)S(1)}, bf16[48,1152]{1,0:T(8,128)(2,1)S(1)}, u32[]{:S(2)}, u32[]{:S(2)}) collective-permute-start(bf16[48,1152]{1,0:T(8,128)(2,1)S(1)} %pad_maximum_fusion.4), channel_id=1, source_target_pairs={{0,320},{8,200},{32,352},{40,232},{64,384},{72,264},{96,416},{104,... | collective-permute-start | bytes 331784 | tf_op jit(solution)/shard_map/ppermute | solution.py:41
  144.7 4.0 %collective-permute-start.9 = (bf16[48,1152]{1,0:T(8,128)(2,1)}, bf16[48,1152]{1,0:T(8,128)(2,1)}, u32[]{:S(2)}, u32[]{:S(2)}) collective-permute-start(bf16[48,1152]{1,0:T(8,128)(2,1)} %get-tuple-element.15), channel_id=1, source_target_pairs={{0,416},{8,104},{32,448},{40,136},{64,480},{72,168},{96,0},{104,20... | collective-permute-start | bytes 331784 | tf_op jit(solution)/shard_map/ppermute | solution.py:41
  148.7 2.0 %fusion.16 = (f32[192]{0:T(256)S(1)}, f32[192]{0:T(256)S(1)}, bf16[192,538]{1,0:T(8,128)(2,1)S(1)}) fusion(f32[538]{0:T(1024)S(1)} %multiply_reduce_fusion, f32[192,538]{1,0:T(8,128)} %copy-done.18, bf16[192,1152]{1,0:T(8,128)(2,1)} %bitcast.4, bf16[538,1152]{1,0:T(8,128)(2,1)S(1)} %copy-done), kind=kOutput, calls=%fused_computation.37 | convolution fusion | flops 240576000 | bytes 2305384 | tf_op jit(solution)/shard_map/dot_general | solution.py:138
  150.8 1.3 convolution_convert_fusion.2
  152.1 3.1 %collective-permute-done.10 = bf16[48,1152]{1,0:T(8,128)(2,1)S(1)} collective-permute-done((bf16[48,1152]{1,0:T(8,128)(2,1)S(1)}, bf16[48,1152]{1,0:T(8,128)(2,1)S(1)}, u32[]{:S(2)}, u32[]{:S(2)}) %collective-permute-start.10) | collective-permute-done | bytes 110624 | tf_op jit(solution)/shard_map/ppermute | solution.py:41
  155.9 3.6 %collective-permute-done.9 = bf16[48,1152]{1,0:T(8,128)(2,1)} collective-permute-done((bf16[48,1152]{1,0:T(8,128)(2,1)}, bf16[48,1152]{1,0:T(8,128)(2,1)}, u32[]{:S(2)}, u32[]{:S(2)}) %collective-permute-start.9) | collective-permute-done | bytes 110624 | tf_op jit(solution)/shard_map/ppermute | solution.py:41
  159.4 1.2 fusion.41
  160.7 5.7 %collective-permute-start.11 = (bf16[24,1152]{1,0:T(8,128)(2,1)S(1)}, bf16[24,1152]{1,0:T(8,128)(2,1)S(1)}, u32[]{:S(2)}, u32[]{:S(2)}) collective-permute-start(bf16[24,1152]{1,0:T(8,128)(2,1)S(1)} %slice.152), channel_id=1, source_target_pairs={{0,8},{8,0},{1,9},{9,1},{2,10},{10,2},{3,11},{11,3},{4,12},{12,4},... | collective-permute-start | bytes 165896 | tf_op jit(solution)/shard_map/ppermute | solution.py:26
  166.4 2.1 %copy.13 = bf16[192,1152]{0,1:T(8,128)(2,1)} copy(bf16[192,1152]{1,0:T(8,128)(2,1)} %convolution_convert_fusion.2) | data formatting | bytes 884736 | tf_op jit(solution)/shard_map/convert_element_type | solution.py:198
  169.2 0.7 fusion.49.text_ref
  170.0 2.3 %shard_map.95 = bf16[8,520,128]{2,1,0:T(8,128)(2,1)} custom-call(bf16[1152,192]{1,0:T(8,128)(2,1)} %bitcast.31, bf16[16,128]{1,0:T(8,128)(2,1)} %pad.9.sums_ref, bf16[24,1152]{1,0:T(8,128)(2,1)} %fusion.49.text_ref), custom_call_target="tpu_custom_call" | custom-call | tf_op jit(solution)/shard_map/pallas_call | solution.py:209
  172.3 4.0 %all-to-all-start.4 = ((bf16[8,520,128]{2,1,0:T(8,128)(2,1)}), bf16[8,520,128]{2,1,0:T(8,128)(2,1)S(1)}, u32[]{:S(2)}, u32[]{:S(2)}) async-start(bf16[8,520,128]{2,1,0:T(8,128)(2,1)} %shard_map.95), calls=%async_computation.4 | async-start | bytes 2129920 | tf_op jit(solution)/shard_map/all_to_all | solution.py:21
  176.4 0.7 copy.14.gain_ref
  177.1 1.0 fusion.9.centred_ref
  178.1 2.0 %fusion.15.direct_ref = f32[144,192]{1,0:T(8,128)} fusion(bf16[192,1152]{1,0:T(8,128)(2,1)} %bitcast.4, s32[1152]{0:T(1024)S(1)} %iota_subtract_fusion), kind=kOutput, calls=%fused_computation.34 | convolution fusion | flops 63866880 | bytes 557568 | tf_op jit(solution)/shard_map/dot_general | solution.py:138
  180.1 12.9 %all-to-all-done.4.packed_ref = bf16[8,520,128]{2,1,0:T(8,128)(2,1)S(1)} async-done(((bf16[8,520,128]{2,1,0:T(8,128)(2,1)}), bf16[8,520,128]{2,1,0:T(8,128)(2,1)S(1)}, u32[]{:S(2)}, u32[]{:S(2)}) %all-to-all-start.4) | async-done | bytes 1064992 | tf_op jit(solution)/shard_map/all_to_all | solution.py:21
  193.0 1.0 copy-done.3
  194.0 2.6 %shard_map.96 = (f32[144,192]{1,0:T(8,128)}, f32[144,192]{1,0:T(8,128)}, bf16[192,1152]{1,0:T(8,128)(2,1)}) custom-call(bf16[8,520,128]{2,1,0:T(8,128)(2,1)} %copy-done.3, f32[144,192]{1,0:T(8,128)} %fusion.15.direct_ref, f32[144,192]{1,0:T(8,128)} %fusion.9.centred_ref, f32[1,192]{1,0:T(1,128)} %bitcast.35, f32[144,1]{1,0:T(8,128)} %copy.14.gain_ref, ...), custom_call_target="tpu_custom_call" | custom-call | tf_op jit(solution)/shard_map/pallas_call | solution.py:220
  (70 shorter events, 4.9 us)
Async XLA Ops:
  0.6 5.5 %copy-start = (bf16[538,1152]{1,0:T(8,128)(2,1)S(1)}, bf16[538,1152]{1,0:T(8,128)(2,1)}, u32[]{:S(2)}) copy-start(bf16[538,1152]{1,0:T(8,128)(2,1)} %param.12) | copy-start | bytes 3718660
  0.6 4.0 %copy-start.4 = (bf16[192,1152]{1,0:T(8,128)(2,1)S(1)}, bf16[192,1152]{1,0:T(8,128)(2,1)}, u32[]{:S(2)}) copy-start(bf16[192,1152]{1,0:T(8,128)(2,1)} %param.8) | copy-start | bytes 1327108
  0.7 4.0 %copy-start.2 = (bf16[1152,538]{0,1:T(8,128)(2,1)S(1)}, bf16[1152,538]{0,1:T(8,128)(2,1)}, u32[]{:S(2)}) copy-start(bf16[1152,538]{0,1:T(8,128)(2,1)} %param.11) | copy-start | bytes 3718660
  0.7 4.0 %copy-start.15 = (f32[1152]{0:T(1024)S(1)}, f32[1152]{0:T(1024)}, u32[]{:S(2)}) copy-start(f32[1152]{0:T(1024)} %param.10) | copy-start | bytes 13828
  3.3 173.8 %copy-start.16 = (f32[192]{0:T(256)}, f32[192]{0:T(256)S(1)}, u32[]{:S(2)}) copy-start(f32[192]{0:T(256)S(1)} %add_rsqrt_fusion) | copy-start | bytes 2308
  5.4 0.8 copy-start.18
  7.7 18.6 %all-to-all-start = ((bf16[8,48,1152]{2,1,0:T(8,128)(2,1)}), bf16[8,48,1152]{2,1,0:T(8,128)(2,1)S(1)}, u32[]{:S(2)}, u32[]{:S(2)}) async-start(bf16[8,48,1152]{2,1,0:T(8,128)(2,1)} %pad_maximum_fusion), calls=%async_computation | async-start | bytes 1769472 | tf_op jit(solution)/shard_map/all_to_all | solution.py:21
  26.4 1.0 copy-start.7
  28.1 7.7 %collective-permute-start = (bf16[24,1152]{1,0:T(8,128)(2,1)S(1)}, bf16[24,1152]{1,0:T(8,128)(2,1)S(1)}, u32[]{:S(2)}, u32[]{:S(2)}) collective-permute-start(bf16[24,1152]{1,0:T(8,128)(2,1)S(1)} %get-tuple-element.14), channel_id=1, source_target_pairs={{0,8},{8,0},{1,9},{9,1},{2,10},{10,2},{3,11},{11,3},{4,12},{12,4},... | collective-permute-start | bytes 165896 | tf_op jit(solution)/shard_map/ppermute | solution.py:26
  35.9 38.5 %copy-start.13 = (bf16[24,1152]{1,0:T(8,128)(2,1)}, bf16[24,1152]{1,0:T(8,128)(2,1)S(1)}, u32[]{:S(2)}) copy-start(bf16[24,1152]{1,0:T(8,128)(2,1)S(1)} %collective-permute-done) | copy-start | bytes 165892
  35.9 20.8 %collective-permute-start.2 = (bf16[48,1152]{1,0:T(8,128)(2,1)S(1)}, bf16[48,1152]{1,0:T(8,128)(2,1)S(1)}, u32[]{:S(2)}, u32[]{:S(2)}) collective-permute-start(bf16[48,1152]{1,0:T(8,128)(2,1)S(1)} %pad_maximum_fusion.3), channel_id=1, source_target_pairs={{0,192},{8,328},{32,224},{40,360},{64,256},{72,392},{96,288},{104,... | collective-permute-start | bytes 331784 | tf_op jit(solution)/shard_map/ppermute | solution.py:41
  50.0 10.8 %collective-permute-start.1 = (bf16[48,1152]{1,0:T(8,128)(2,1)S(1)}, bf16[48,1152]{1,0:T(8,128)(2,1)S(1)}, u32[]{:S(2)}, u32[]{:S(2)}) collective-permute-start(bf16[48,1152]{1,0:T(8,128)(2,1)S(1)} %pad_maximum_fusion.3), channel_id=1, source_target_pairs={{0,96},{8,424},{32,128},{40,456},{64,160},{72,488},{96,192},{104,8... | collective-permute-start | bytes 331784 | tf_op jit(solution)/shard_map/ppermute | solution.py:41
  56.7 4.2 %copy-start.8 = (bf16[48,1152]{1,0:T(8,128)(2,1)}, bf16[48,1152]{1,0:T(8,128)(2,1)S(1)}, u32[]{:S(2)}) copy-start(bf16[48,1152]{1,0:T(8,128)(2,1)S(1)} %collective-permute-done.2) | copy-start | bytes 331780
  60.8 0.8 copy-start.10
  63.3 16.4 %collective-permute-start.3 = (bf16[144,1152]{1,0:T(8,128)(2,1)}, bf16[144,1152]{1,0:T(8,128)(2,1)}, u32[]{:S(2)}, u32[]{:S(2)}) collective-permute-start(bf16[144,1152]{1,0:T(8,128)(2,1)} %pad_maximum_fusion.2), channel_id=1, source_target_pairs={{0,32},{8,488},{32,64},{40,8},{64,96},{72,40},{96,128},{104,72},{1... | collective-permute-start | bytes 995336 | tf_op jit(solution)/shard_map/ppermute | solution.py:41
  65.2 14.5 %collective-permute-start.4 = (bf16[120,1152]{1,0:T(8,128)(2,1)}, bf16[120,1152]{1,0:T(8,128)(2,1)}, u32[]{:S(2)}, u32[]{:S(2)}) collective-permute-start(bf16[120,1152]{1,0:T(8,128)(2,1)} %slice.92), channel_id=1, source_target_pairs={{0,64},{8,456},{32,96},{40,488},{64,128},{72,8},{96,160},{104,40},... | collective-permute-start | bytes 829448 | tf_op jit(solution)/shard_map/ppermute | solution.py:41
  74.3 18.8 %all-to-all-start.1 = ((bf16[16,24,1152]{2,1,0:T(8,128)(2,1)}), bf16[16,24,1152]{2,1,0:T(8,128)(2,1)S(1)}, u32[]{:S(2)}, u32[]{:S(2)}) async-start(bf16[16,24,1152]{2,1,0:T(8,128)(2,1)} %broadcast_in_dim.16), calls=%async_computation.1 | async-start | bytes 1769472 | tf_op jit(solution)/shard_map/all_to_all | solution.py:21
  78.2 4.6 %copy-start.11 = (bf16[48,1152]{1,0:T(8,128)(2,1)S(1)}, bf16[48,1152]{1,0:T(8,128)(2,1)}, u32[]{:S(2)}) copy-start(bf16[48,1152]{1,0:T(8,128)(2,1)} %copy-done.10) | copy-start | bytes 331780
  78.2 5.3 %copy-start.9 = (bf16[48,1152]{1,0:T(8,128)(2,1)S(1)}, bf16[48,1152]{1,0:T(8,128)(2,1)}, u32[]{:S(2)}) copy-start(bf16[48,1152]{1,0:T(8,128)(2,1)} %copy-done.8) | copy-start | bytes 331780
  80.9 6.6 %collective-permute-start.5 = (bf16[360,1152]{1,0:T(8,128)(2,1)S(1)}, bf16[360,1152]{1,0:T(8,128)(2,1)S(1)}, u32[]{:S(2)}, u32[]{:S(2)}) collective-permute-start(bf16[360,1152]{1,0:T(8,128)(2,1)S(1)} %pad_maximum_fusion.1), channel_id=1, source_target_pairs={{0,8},{8,0},{1,9},{9,1},{2,10},{10,2},{3,11},{11,3},{4,12},{12,4},... | collective-permute-start | bytes 2488328 | tf_op jit(solution)/shard_map/ppermute | solution.py:26
  96.1 5.7 %copy-start.12 = (bf16[768,384]{1,0:T(8,128)(2,1)}, bf16[768,384]{1,0:T(8,128)(2,1)S(1)}, u32[]{:S(2)}) copy-start(bf16[768,384]{1,0:T(8,128)(2,1)S(1)} %fusion.7) | copy-start | bytes 1769476
  96.1 3.8 %copy-start.17 = (bf16[768,1152]{1,0:T(8,128)(2,1)S(1)}, bf16[768,1152]{1,0:T(8,128)(2,1)}, u32[]{:S(2)}) copy-start(bf16[768,1152]{1,0:T(8,128)(2,1)} %constant_dynamic-update-slice_fusion) | copy-start | bytes 5308420
  97.7 10.2 %collective-permute-start.6 = (bf16[360,1152]{1,0:T(8,128)(2,1)}, bf16[360,1152]{1,0:T(8,128)(2,1)}, u32[]{:S(2)}, u32[]{:S(2)}) collective-permute-start(bf16[360,1152]{1,0:T(8,128)(2,1)} %convolution_convert_fusion.1), channel_id=1, source_target_pairs={{0,8},{8,0},{1,9},{9,1},{2,10},{10,2},{3,11},{11,3},{4,12},{12,4},... | collective-permute-start | bytes 2488328 | tf_op jit(solution)/shard_map/ppermute | solution.py:26
  101.8 19.0 %all-to-all-start.2 = ((bf16[16,24,1152]{2,1,0:T(8,128)(2,1)}), bf16[16,24,1152]{2,1,0:T(8,128)(2,1)}, u32[]{:S(2)}, u32[]{:S(2)}) async-start(bf16[16,24,1152]{2,1,0:T(8,128)(2,1)} %bitcast.33), calls=%async_computation.2 | async-start | bytes 1769472 | tf_op jit(solution)/shard_map/all_to_all | solution.py:21
  107.8 3.2 %copy-start.1 = (f32[408,1152]{1,0:T(8,128)}, f32[408,1152]{1,0:T(8,128)S(1)}, u32[]{:S(2)}) copy-start(f32[408,1152]{1,0:T(8,128)S(1)} %fusion.32) | copy-start | bytes 5640196
  122.2 12.3 %collective-permute-start.8 = (bf16[120,1152]{1,0:T(8,128)(2,1)}, bf16[120,1152]{1,0:T(8,128)(2,1)S(1)}, u32[]{:S(2)}, u32[]{:S(2)}) collective-permute-start(bf16[120,1152]{1,0:T(8,128)(2,1)} %slice.99), channel_id=1, source_target_pairs={{0,448},{8,72},{32,480},{40,104},{64,0},{72,136},{96,32},{104,168}... | collective-permute-start | bytes 829448 | tf_op jit(solution)/shard_map/ppermute | solution.py:41
  124.7 13.7 %collective-permute-start.7 = (bf16[144,1152]{1,0:T(8,128)(2,1)S(1)}, bf16[144,1152]{1,0:T(8,128)(2,1)}, u32[]{:S(2)}, u32[]{:S(2)}) collective-permute-start(bf16[144,1152]{1,0:T(8,128)(2,1)S(1)} %slice.97), channel_id=1, source_target_pairs={{0,480},{8,40},{32,0},{40,72},{64,32},{72,104},{96,64},{104,136},{... | collective-permute-start | bytes 995336 | tf_op jit(solution)/shard_map/ppermute | solution.py:41
  128.9 19.9 %all-to-all-start.3 = ((bf16[8,24,1152]{2,1,0:T(8,128)(2,1)}), bf16[8,24,1152]{2,1,0:T(8,128)(2,1)}, u32[]{:S(2)}, u32[]{:S(2)}) async-start(bf16[8,24,1152]{2,1,0:T(8,128)(2,1)} %broadcast_in_dim.17), calls=%async_computation.3 | async-start | bytes 884736 | tf_op jit(solution)/shard_map/all_to_all | solution.py:21
  134.6 6.6 %copy-start.6 = (f32[120,1152]{1,0:T(8,128)}, f32[120,1152]{1,0:T(8,128)S(1)}, u32[]{:S(2)}) copy-start(f32[120,1152]{1,0:T(8,128)S(1)} %convert_element_type.118) | copy-start | bytes 1658884
  141.2 14.0 %collective-permute-start.10 = (bf16[48,1152]{1,0:T(8,128)(2,1)S(1)}, bf16[48,1152]{1,0:T(8,128)(2,1)S(1)}, u32[]{:S(2)}, u32[]{:S(2)}) collective-permute-start(bf16[48,1152]{1,0:T(8,128)(2,1)S(1)} %pad_maximum_fusion.4), channel_id=1, source_target_pairs={{0,320},{8,200},{32,352},{40,232},{64,384},{72,264},{96,416},{104,... | collective-permute-start | bytes 331784 | tf_op jit(solution)/shard_map/ppermute | solution.py:41
  144.7 14.7 %collective-permute-start.9 = (bf16[48,1152]{1,0:T(8,128)(2,1)}, bf16[48,1152]{1,0:T(8,128)(2,1)}, u32[]{:S(2)}, u32[]{:S(2)}) collective-permute-start(bf16[48,1152]{1,0:T(8,128)(2,1)} %get-tuple-element.15), channel_id=1, source_target_pairs={{0,416},{8,104},{32,448},{40,136},{64,480},{72,168},{96,0},{104,20... | collective-permute-start | bytes 331784 | tf_op jit(solution)/shard_map/ppermute | solution.py:41
  155.2 0.6 copy-start.14
  160.7 8.4 %collective-permute-start.11 = (bf16[24,1152]{1,0:T(8,128)(2,1)S(1)}, bf16[24,1152]{1,0:T(8,128)(2,1)S(1)}, u32[]{:S(2)}, u32[]{:S(2)}) collective-permute-start(bf16[24,1152]{1,0:T(8,128)(2,1)S(1)} %slice.152), channel_id=1, source_target_pairs={{0,8},{8,0},{1,9},{9,1},{2,10},{10,2},{3,11},{11,3},{4,12},{12,4},... | collective-permute-start | bytes 165896 | tf_op jit(solution)/shard_map/ppermute | solution.py:26
  170.0 7.2 %copy-start.5 = (bf16[192,1152]{1,0:T(8,128)(2,1)S(1)}, bf16[192,1152]{1,0:T(8,128)(2,1)}, u32[]{:S(2)}) copy-start(bf16[192,1152]{1,0:T(8,128)(2,1)} %param.8) | copy-start | bytes 1327108
  172.3 20.7 %all-to-all-start.4 = ((bf16[8,520,128]{2,1,0:T(8,128)(2,1)}), bf16[8,520,128]{2,1,0:T(8,128)(2,1)S(1)}, u32[]{:S(2)}, u32[]{:S(2)}) async-start(bf16[8,520,128]{2,1,0:T(8,128)(2,1)} %shard_map.95), calls=%async_computation.4 | async-start | bytes 2129920 | tf_op jit(solution)/shard_map/all_to_all | solution.py:21
  193.0 1.0 copy-start.3

commit v4 on v3

--- a/solution.py
+++ b/solution.py
@@ -1,7 +1,10 @@
+import functools
+
 import jax
 import jax.numpy as jnp
 from jax import lax
 from jax.experimental import pallas as pl
+from jax.experimental.pallas import tpu as pltpu
 from jax.sharding import Mesh
 from jax.sharding import PartitionSpec as P
 
@@ -48,26 +51,103 @@
     near = jnp.concatenate([pair, *far], axis=0)
     cut = near.shape[0] - share
     last = [along(near, -NEAR[0]), along(near[:cut], -NEAR[1])]
-    mine = jnp.concatenate([near, *last], axis=0)
-    other = exchange(mine[2 * share :], "c", 1)
-    return jnp.concatenate([mine, other], axis=0)
+    other = exchange(jnp.concatenate([*far, *last], axis=0), "c", 1)
+    return [pair, *far, *last, other]
+
+
+def shape(rows, width, dtype):
+    return jax.ShapeDtypeStruct((rows, width), dtype)
+
+
+def pairs_kernel(share, consts_ref, start_ref, *refs):
+    pieces, images_ref = refs[:6], refs[6]
+    sent_ref, kept_ref, image_ref, texts_ref, weights_ref = refs[7:]
+    at = 0
+    for piece in pieces:
+        texts_ref[at : at + piece.shape[0], :] = piece[...]
+        at += piece.shape[0]
+    scale = consts_ref[0]
+    step = at // 6
+    columns = images_ref.shape[0]
+    for first in range(0, at, step):
+        energies = scale * dot(
+            texts_ref[first : first + step, :], images_ref[...], ((1,), (1,))
+        ) + consts_ref[1]
+        if first:
+            weights = scale * jax.nn.sigmoid(energies)
+        else:
+            text_ids = lax.broadcasted_iota(jnp.int32, (step, columns), 0)
+            image_ids = lax.broadcasted_iota(jnp.int32, (step, columns), 1) - start_ref[0]
+            same = (text_ids == image_ids) & (text_ids < share)
+            polarity = jnp.where(same, 1.0, -1.0).astype(F32)
+            weights = scale * -polarity * jax.nn.sigmoid(-polarity * energies)
+        weights_ref[first : first + step, :] = weights.astype(BF16)
+    middle = kept_ref.shape[0]
+    sent_ref[...] = dot(weights_ref[middle:, :], images_ref[...], ((1,), (0,))).astype(BF16)
+    kept_ref[...] = dot(weights_ref[:middle, :], images_ref[...], ((1,), (0,)))
+    image_ref[...] = dot(weights_ref[...], texts_ref[...], ((0,), (0,))).astype(BF16)
+
+
+def near_kernel(kept_ref, swapped_ref, one_ref, two_ref):
+    long = one_ref.shape[0]
+    pair = long // 3
+    one_ref[...] = (
+        kept_ref[3 * pair : 6 * pair, :] + swapped_ref[2 * pair : 5 * pair, :].astype(F32)
+    ).astype(BF16)
+    two_ref[...] = (
+        kept_ref[6 * pair :, :] + swapped_ref[5 * pair :, :].astype(F32)
+    ).astype(BF16)
+
+
+def far_kernel(kept_ref, swapped_ref, one_ref, two_ref, here_ref, three_ref, six_ref):
+    pair = here_ref.shape[0]
+    share = pair // 2
+    here_ref[...] = (
+        kept_ref[:pair, :] + one_ref[:pair, :].astype(F32) + two_ref[:pair, :].astype(F32)
+    )
+    three_ref[...] = (
+        kept_ref[pair : 2 * pair, :]
+        + swapped_ref[:pair, :].astype(F32)
+        + one_ref[pair : 2 * pair, :].astype(F32)
+        + two_ref[pair : 2 * pair, :].astype(F32)
+    ).astype(BF16)
+    sixth = (
+        kept_ref[2 * pair : 3 * pair, :]
+        + swapped_ref[pair : 2 * pair, :].astype(F32)
+        + one_ref[2 * pair :, :].astype(F32)
+    )
+    own = sixth[:share, :] + two_ref[2 * pair :, :].astype(F32)
+    six_ref[:share, :] = own.astype(BF16)
+    six_ref[share:, :] = sixth[share:, :].astype(BF16)
+
+
+def last_kernel(here_ref, three_ref, six_ref, own_ref, partner_ref):
+    share = own_ref.shape[0]
+    total = here_ref[...] + three_ref[...].astype(F32) + six_ref[...].astype(F32)
+    own_ref[...] = total[:share, :]
+    partner_ref[...] = total[share:, :].astype(BF16)
 
 
 def summed_line(kept, swapped, share):
+    width = kept.shape[1]
     pair = 2 * share
-    rest = kept[pair:] + swapped.astype(F32)
-    cut = 5 * pair
-    one = along(rest[2 * pair : cut].astype(BF16), NEAR[0]).astype(F32)
-    two = along(rest[cut:].astype(BF16), NEAR[1]).astype(F32)
-    here = kept[:pair] + one[:pair] + two[:pair]
-    third = rest[:pair] + one[pair : 2 * pair] + two[pair : 2 * pair]
-    sixth = rest[pair : 2 * pair] + one[2 * pair :]
-    sixth = jnp.concatenate([sixth[:share] + two[2 * pair :], sixth[share:]], axis=0)
-    three = along(third.astype(BF16), FAR[0])
-    six = along(sixth.astype(BF16), FAR[1])
-    total = here + three.astype(F32) + six.astype(F32)
-    partner = exchange(total[share:].astype(BF16), "c", 1)
-    return total[:share] + partner.astype(F32)
+    one, two = pl.pallas_call(
+        near_kernel,
+        out_shape=(shape(3 * pair, width, BF16), shape(2 * pair + share, width, BF16)),
+    )(kept, swapped)
+    one = along(one, NEAR[0])
+    two = along(two, NEAR[1])
+    here, three, six = pl.pallas_call(
+        far_kernel,
+        out_shape=(shape(pair, width, F32), shape(pair, width, BF16), shape(pair, width, BF16)),
+    )(kept, swapped, one, two)
+    three = along(three, FAR[0])
+    six = along(six, FAR[1])
+    own, partner = pl.pallas_call(
+        last_kernel, out_shape=(shape(share, width, F32), shape(share, width, BF16))
+    )(here, three, six)
+    partner = exchange(partner, "c", 1)
+    return own + partner.astype(F32)
 
 
 LANES = 128
@@ -168,22 +248,30 @@
     inv_image = lax.rsqrt(jnp.sum(image_out * image_out, axis=-1, keepdims=True) + 1e-06)
     unit_image = (image_out * inv_image).astype(BF16)
 
-    texts = gathered_line(unit_text)
+    pieces = gathered_line(unit_text)
     images = spread(unit_image, XY)
 
-    own_start = lax.axis_index(XY) * share
-    text_ids = jnp.arange(texts.shape[0], dtype=jnp.int32)[:, None]
-    image_ids = jnp.arange(images.shape[0], dtype=jnp.int32)[None, :] - own_start
-    same = (text_ids == image_ids) & (text_ids < share)
-    energies = scale * dot(texts, images, ((1,), (1,))) + offset
-    polarity = jnp.where(same, 1.0, -1.0).astype(F32)
-    weighted = (scale * -polarity * jax.nn.sigmoid(-polarity * energies)).astype(BF16)
-    middle = weighted.shape[0] // 2 + share
-    text_sent = dot(weighted[middle:], images, ((1,), (0,))).astype(BF16)
-    text_kept = dot(weighted[:middle], images, ((1,), (0,)))
-    image_add = dot(weighted, texts, ((0,), (0,)))
-
-    image_parts = swap(image_add.astype(BF16).reshape(-1, share, width), XY)
+    own_start = (lax.axis_index(XY) * share).reshape(1)
+    consts = jnp.stack([scale, offset])
+    sent_rows = pieces[-1].shape[0]
+    kept_rows = sum(p.shape[0] for p in pieces) - sent_rows
+    scalars = pl.BlockSpec(memory_space=pltpu.SMEM)
+    whole = pl.BlockSpec(memory_space=pltpu.VMEM)
+    text_sent, text_kept, image_add = pl.pallas_call(
+        functools.partial(pairs_kernel, share),
+        in_specs=[scalars, scalars] + [whole] * 7,
+        out_shape=(
+            shape(sent_rows, width, BF16),
+            shape(kept_rows, width, F32),
+            shape(images.shape[0], width, BF16),
+        ),
+        scratch_shapes=[
+            pltpu.VMEM((sent_rows + kept_rows, width), BF16),
+            pltpu.VMEM((sent_rows + kept_rows, images.shape[0]), BF16),
+        ],
+    )(consts, own_start, *pieces, images)
+
+    image_parts = swap(image_add.reshape(-1, share, width), XY)
     image_dir = jnp.sum(image_parts.astype(F32), axis=0)
     grad_share = norm_back(image_dir, unit_image, inv_image).astype(BF16)
     grad_out_b = spread(grad_share, MP)

time: 198 us -> 206 us (1.040)
  the two profiles are of different devices: /device:TPU:1 before, /device:TPU:32 now
where the time goes in v4:
time: 206 us; the launch traced here: 205 us
  waiting for transfers between devices  84.3 us (41%)
  starting transfers between devices  71.7 us (35%)
  Pallas kernels  18.1 us (9%)
  local copies, waits for them, and re-layouts  10.5 us (5%)
  other arithmetic  9.68 us (5%)
  matrix products  8.59 us (4%)
  between operations  2.28 us (1%)
    all_to_all x5, waiting for transfers between devices, swap(): return lax.all_to_all(array, axes, 0, 0, tiled=True)  50.6 us
    ppermute x8, starting transfers between devices, along(): return lax.ppermute(array, LINE, moves)  36.3 us
    ppermute x8, waiting for transfers between devices, along(): return lax.ppermute(array, LINE, moves)  32.5 us
    all_to_all x5, starting transfers between devices, swap(): return lax.all_to_all(array, axes, 0, 0, tiled=True)  27.6 us
    dot_general x7, matrix products, dot(): return lax.dot_general(a, b, (dims, ((), ())), preferred_element_type=F32)  8.59 us
    ppermute x4, starting transfers between devices, exchange(): return lax.ppermute(array, axes, [(i, i ^ k) for i in range(n)])  7.79 us
    pallas_call x1, Pallas kernels, per_device(): pl.pallas_call(functools.partial(pairs_kernel, share), in_specs=[scalars,...  6.13 us
    unnamed x42, local copies, waits for them, and re-layouts  5.48 us
  transfers between devices with their start and end apart: 17, of which 11 were waited for; matrix products, arithmetic and copies ran while one was open for 6% of the time, Pallas kernels for 3%

profile of v4, /device:TPU:32, one launch (start us, length us, event | category | flops | bytes accessed | tf_op | source)
XLA Modules:
  0.0 205.2 jit_solution(339463057414122369)
XLA Ops:
  0.6 1.3 convert_reduce_fusion.2
  1.9 1.3 fusion.3
  3.2 2.1 %fusion.16 = f32[192,538]{1,0:T(8,128)S(1)} fusion(bf16[1152,538]{0,1:T(8,128)(2,1)} %param.11, bf16[192,1152]{1,0:T(8,128)(2,1)} %param.8, f32[1152]{0:T(1024)} %param.10, f32[192]{0:T(256)S(1)} %add_rsqrt_fusion, f32[192]{0:T(256)S(1)} %broadcast_multiply_fusion), kind=kOutput, calls=%fused_computation.33 | convolution fusion | flops 239099904 | bytes 2101248 | tf_op jit(solution)/shard_map/dot_general | solution.py:218
  5.3 0.8 copy-done.20
  6.1 0.6 convolution_convert_fusion.1
  6.7 0.4 copy-done.7
  7.1 0.3 convolution_convert_fusion.2
  7.4 1.0 pad_maximum_fusion
  8.4 6.9 %all-to-all-start = ((bf16[8,48,1152]{2,1,0:T(8,128)(2,1)}), bf16[8,48,1152]{2,1,0:T(8,128)(2,1)S(1)}, u32[]{:S(2)}, u32[]{:S(2)}) async-start(bf16[8,48,1152]{2,1,0:T(8,128)(2,1)} %pad_maximum_fusion), calls=%async_computation | async-start | bytes 1769472 | tf_op jit(solution)/shard_map/all_to_all | solution.py:24
  15.4 14.2 %all-to-all-done = bf16[8,48,1152]{2,1,0:T(8,128)(2,1)S(1)} async-done(((bf16[8,48,1152]{2,1,0:T(8,128)(2,1)}), bf16[8,48,1152]{2,1,0:T(8,128)(2,1)S(1)}, u32[]{:S(2)}, u32[]{:S(2)}) %all-to-all-start) | async-done | bytes 884768 | tf_op jit(solution)/shard_map/all_to_all | solution.py:24
  29.6 1.0 multiply_reduce_fusion.2
  30.6 0.9 multiply_convert_fusion.2
  31.5 1.9 collective-permute-start
  33.5 1.2 collective-permute-done
  34.7 7.7 %collective-permute-start.1 = (bf16[48,1152]{1,0:T(8,128)(2,1)S(1)}, bf16[48,1152]{1,0:T(8,128)(2,1)S(1)}, u32[]{:S(2)}, u32[]{:S(2)}) collective-permute-start(bf16[48,1152]{1,0:T(8,128)(2,1)S(1)} %pad_maximum_fusion.3.refs_0_), channel_id=1, source_target_pairs={{0,96},{8,424},{32,128},{40,456},{64,160},{72,488},{96,192},{104,8... | collective-permute-start | bytes 331784 | tf_op jit(solution)/shard_map/ppermute | solution.py:44
  42.4 10.0 %collective-permute-start.2 = (bf16[48,1152]{1,0:T(8,128)(2,1)S(1)}, bf16[48,1152]{1,0:T(8,128)(2,1)S(1)}, u32[]{:S(2)}, u32[]{:S(2)}) collective-permute-start(bf16[48,1152]{1,0:T(8,128)(2,1)S(1)} %pad_maximum_fusion.3.refs_0_), channel_id=1, source_target_pairs={{0,192},{8,328},{32,224},{40,360},{64,256},{72,392},{96,288},{104,... | collective-permute-start | bytes 331784 | tf_op jit(solution)/shard_map/ppermute | solution.py:44
  52.5 10.1 %collective-permute-done.2.refs_2_ = bf16[48,1152]{1,0:T(8,128)(2,1)S(1)} collective-permute-done((bf16[48,1152]{1,0:T(8,128)(2,1)S(1)}, bf16[48,1152]{1,0:T(8,128)(2,1)S(1)}, u32[]{:S(2)}, u32[]{:S(2)}) %collective-permute-start.2) | collective-permute-done | bytes 110624 | tf_op jit(solution)/shard_map/ppermute | solution.py:44
  62.6 1.9 collective-permute-start.3
  64.5 0.7 slice.14
  65.3 4.2 %collective-permute-start.4 = (bf16[120,1152]{1,0:T(8,128)(2,1)}, bf16[120,1152]{1,0:T(8,128)(2,1)S(1)}, u32[]{:S(2)}, u32[]{:S(2)}) collective-permute-start(bf16[120,1152]{1,0:T(8,128)(2,1)} %slice.14), channel_id=1, source_target_pairs={{0,64},{8,456},{32,96},{40,488},{64,128},{72,8},{96,160},{104,40},... | collective-permute-start | bytes 829448 | tf_op jit(solution)/shard_map/ppermute | solution.py:44
  69.5 1.0 broadcast_in_dim.6
  70.5 4.2 %all-to-all-start.1 = ((bf16[16,24,1152]{2,1,0:T(8,128)(2,1)}), bf16[16,24,1152]{2,1,0:T(8,128)(2,1)S(1)}, u32[]{:S(2)}, u32[]{:S(2)}) async-start(bf16[16,24,1152]{2,1,0:T(8,128)(2,1)} %broadcast_in_dim.6), calls=%async_computation.1 | async-start | bytes 1769472 | tf_op jit(solution)/shard_map/all_to_all | solution.py:24
  74.7 4.2 %collective-permute-done.4.refs_4_ = bf16[120,1152]{1,0:T(8,128)(2,1)S(1)} collective-permute-done((bf16[120,1152]{1,0:T(8,128)(2,1)}, bf16[120,1152]{1,0:T(8,128)(2,1)S(1)}, u32[]{:S(2)}, u32[]{:S(2)}) %collective-permute-start.4) | collective-permute-done | bytes 276512 | tf_op jit(solution)/shard_map/ppermute | solution.py:44
  78.9 1.1 pad_maximum_fusion.1
  80.0 1.9 collective-permute-start.5
  83.2 0.6 pad_maximum_fusion.5.consts_ref
  83.8 8.7 %all-to-all-done.1 = bf16[16,24,1152]{2,1,0:T(8,128)(2,1)S(1)} async-done(((bf16[16,24,1152]{2,1,0:T(8,128)(2,1)}), bf16[16,24,1152]{2,1,0:T(8,128)(2,1)S(1)}, u32[]{:S(2)}, u32[]{:S(2)}) %all-to-all-start.1) | async-done | bytes 884768 | tf_op jit(solution)/shard_map/all_to_all | solution.py:24
  92.6 0.9 copy-done.3
  93.5 6.1 %shard_map.95 = (bf16[360,1152]{1,0:T(8,128)(2,1)}, f32[408,1152]{1,0:T(8,128)}, bf16[384,1152]{1,0:T(8,128)(2,1)}) custom-call(f32[2]{0:T(128)} %pad_maximum_fusion.5.consts_ref, s32[1]{0:T(128)} %bitcast.4.start_ref, bf16[48,1152]{1,0:T(8,128)(2,1)} %copy-done.12, bf16[48,1152]{1,0:T(8,128)(2,1)} %copy-done.9, bf16[48,1152]{1,0:T(8,128)(2,1)} %copy-done.10, ...), custom_call_target="tpu_custom_call" | custom-call | tf_op jit(solution)/shard_map/pallas_call | solution.py:260
  99.6 5.0 %all-to-all-start.2 = ((bf16[16,24,1152]{2,1,0:T(8,128)(2,1)}), bf16[16,24,1152]{2,1,0:T(8,128)(2,1)S(1)}, u32[]{:S(2)}, u32[]{:S(2)}) async-start(bf16[16,24,1152]{2,1,0:T(8,128)(2,1)} %bitcast.30), calls=%async_computation.2 | async-start | bytes 1769472 | tf_op jit(solution)/shard_map/all_to_all | solution.py:24
  104.6 1.9 collective-permute-start.6
  106.6 14.0 %all-to-all-done.2 = bf16[16,24,1152]{2,1,0:T(8,128)(2,1)S(1)} async-done(((bf16[16,24,1152]{2,1,0:T(8,128)(2,1)}), bf16[16,24,1152]{2,1,0:T(8,128)(2,1)S(1)}, u32[]{:S(2)}, u32[]{:S(2)}) %all-to-all-start.2) | async-done | bytes 884768 | tf_op jit(solution)/shard_map/all_to_all | solution.py:24
  120.9 0.8 broadcast_in_dim.7
  121.7 4.1 %all-to-all-start.3 = ((bf16[8,24,1152]{2,1,0:T(8,128)(2,1)}), bf16[8,24,1152]{2,1,0:T(8,128)(2,1)}, u32[]{:S(2)}, u32[]{:S(2)}) async-start(bf16[8,24,1152]{2,1,0:T(8,128)(2,1)} %broadcast_in_dim.7), calls=%async_computation.3 | async-start | bytes 884736 | tf_op jit(solution)/shard_map/all_to_all | solution.py:24
  125.9 0.9 copy-done.4
  126.7 2.7 %shard_map.96 = (bf16[144,1152]{1,0:T(8,128)(2,1)}, bf16[120,1152]{1,0:T(8,128)(2,1)}) custom-call(f32[408,1152]{1,0:T(8,128)} %get-tuple-element.15.kept_ref, bf16[360,1152]{1,0:T(8,128)(2,1)} %copy-done.4), custom_call_target="tpu_custom_call" | custom-call | tf_op jit(solution)/shard_map/pallas_call | solution.py:134
  129.4 1.9 collective-permute-start.7
  131.4 1.9 collective-permute-start.8
  133.3 0.3 multiply_reduce_fusion
  133.6 7.3 %collective-permute-done.8.two_ref = bf16[120,1152]{1,0:T(8,128)(2,1)S(1)} collective-permute-done((bf16[120,1152]{1,0:T(8,128)(2,1)}, bf16[120,1152]{1,0:T(8,128)(2,1)S(1)}, u32[]{:S(2)}, u32[]{:S(2)}) %collective-permute-start.8) | collective-permute-done | bytes 276512 | tf_op jit(solution)/shard_map/ppermute | solution.py:44
  141.0 0.6 collective-permute-done.7.one_ref
  141.7 0.7 copy-done.13
  142.4 2.7 %shard_map.97 = (f32[48,1152]{1,0:T(8,128)}, bf16[48,1152]{1,0:T(8,128)(2,1)}, bf16[48,1152]{1,0:T(8,128)(2,1)}) custom-call(f32[408,1152]{1,0:T(8,128)} %get-tuple-element.15.kept_ref, bf16[360,1152]{1,0:T(8,128)(2,1)} %copy-done.4, bf16[144,1152]{1,0:T(8,128)(2,1)} %copy-done.13, bf16[120,1152]{1,0:T(8,128)(2,1)} %copy-done.14), custom_call_target="tpu_custom_call" | custom-call | tf_op jit(solution)/shard_map/pallas_call | solution.py:140
  145.1 4.2 %collective-permute-start.10 = (bf16[48,1152]{1,0:T(8,128)(2,1)}, bf16[48,1152]{1,0:T(8,128)(2,1)S(1)}, u32[]{:S(2)}, u32[]{:S(2)}) collective-permute-start(bf16[48,1152]{1,0:T(8,128)(2,1)} %get-tuple-element.21), channel_id=1, source_target_pairs={{0,320},{8,200},{32,352},{40,232},{64,384},{72,264},{96,416},{104,... | collective-permute-start | bytes 331784 | tf_op jit(solution)/shard_map/ppermute | solution.py:44
  149.3 4.3 %collective-permute-start.9 = (bf16[48,1152]{1,0:T(8,128)(2,1)}, bf16[48,1152]{1,0:T(8,128)(2,1)S(1)}, u32[]{:S(2)}, u32[]{:S(2)}) collective-permute-start(bf16[48,1152]{1,0:T(8,128)(2,1)} %get-tuple-element.20), channel_id=1, source_target_pairs={{0,416},{8,104},{32,448},{40,136},{64,480},{72,168},{96,0},{104,20... | collective-permute-start | bytes 331784 | tf_op jit(solution)/shard_map/ppermute | solution.py:44
  153.7 2.0 fusion.7
  155.7 0.5 convolution_convert_fusion
  156.3 3.8 %collective-permute-done.10.six_ref = bf16[48,1152]{1,0:T(8,128)(2,1)S(1)} collective-permute-done((bf16[48,1152]{1,0:T(8,128)(2,1)}, bf16[48,1152]{1,0:T(8,128)(2,1)S(1)}, u32[]{:S(2)}, u32[]{:S(2)}) %collective-permute-start.10) | collective-permute-done | bytes 110624 | tf_op jit(solution)/shard_map/ppermute | solution.py:44
  160.1 6.4 %collective-permute-done.9.three_ref = bf16[48,1152]{1,0:T(8,128)(2,1)S(1)} collective-permute-done((bf16[48,1152]{1,0:T(8,128)(2,1)}, bf16[48,1152]{1,0:T(8,128)(2,1)S(1)}, u32[]{:S(2)}, u32[]{:S(2)}) %collective-permute-start.9) | collective-permute-done | bytes 110624 | tf_op jit(solution)/shard_map/ppermute | solution.py:44
  166.5 0.6 copy-done.16
  167.1 1.7 shard_map.98
  168.9 2.0 collective-permute-start.11
  171.0 1.1 copy.13
  172.0 0.6 pad.9.sums_ref
  172.6 1.0 fusion.31
  173.7 0.7 fusion.34.text_ref
  174.4 2.2 %shard_map.99 = bf16[8,520,128]{2,1,0:T(8,128)(2,1)} custom-call(bf16[1152,192]{1,0:T(8,128)(2,1)} %bitcast.28, bf16[16,128]{1,0:T(8,128)(2,1)} %pad.9.sums_ref, bf16[24,1152]{1,0:T(8,128)(2,1)} %fusion.34.text_ref), custom_call_target="tpu_custom_call" | custom-call | tf_op jit(solution)/shard_map/pallas_call | solution.py:297
  176.6 7.4 %all-to-all-start.4 = ((bf16[8,520,128]{2,1,0:T(8,128)(2,1)}), bf16[8,520,128]{2,1,0:T(8,128)(2,1)S(1)}, u32[]{:S(2)}, u32[]{:S(2)}) async-start(bf16[8,520,128]{2,1,0:T(8,128)(2,1)} %shard_map.99), calls=%async_computation.4 | async-start | bytes 2129920 | tf_op jit(solution)/shard_map/all_to_all | solution.py:24
  184.1 0.7 copy.14.gain_ref
  184.8 1.0 fusion.centred_ref
  185.8 2.0 fusion.6.direct_ref
  187.8 13.7 %all-to-all-done.4.packed_ref = bf16[8,520,128]{2,1,0:T(8,128)(2,1)S(1)} async-done(((bf16[8,520,128]{2,1,0:T(8,128)(2,1)}), bf16[8,520,128]{2,1,0:T(8,128)(2,1)S(1)}, u32[]{:S(2)}, u32[]{:S(2)}) %all-to-all-start.4) | async-done | bytes 1064992 | tf_op jit(solution)/shard_map/all_to_all | solution.py:24
  201.6 1.0 copy-done.2
  202.6 2.6 %shard_map.100 = (f32[144,192]{1,0:T(8,128)}, f32[144,192]{1,0:T(8,128)}, bf16[192,1152]{1,0:T(8,128)(2,1)}) custom-call(bf16[8,520,128]{2,1,0:T(8,128)(2,1)} %copy-done.2, f32[144,192]{1,0:T(8,128)} %fusion.6.direct_ref, f32[144,192]{1,0:T(8,128)} %fusion.centred_ref, f32[1,192]{1,0:T(1,128)} %bitcast.32, f32[144,1]{1,0:T(8,128)} %copy.14.gain_ref, ...), custom_call_target="tpu_custom_call" | custom-call | tf_op jit(solution)/shard_map/pallas_call | solution.py:308
  (55 shorter events, 0.8 us)
Async XLA Ops:
  0.6 5.5 %copy-start = (bf16[538,1152]{1,0:T(8,128)(2,1)S(1)}, bf16[538,1152]{1,0:T(8,128)(2,1)}, u32[]{:S(2)}) copy-start(bf16[538,1152]{1,0:T(8,128)(2,1)} %param.12) | copy-start | bytes 3718660
  3.2 181.6 %copy-start.19 = (f32[192]{0:T(256)}, f32[192]{0:T(256)S(1)}, u32[]{:S(2)}) copy-start(f32[192]{0:T(256)S(1)} %add_rsqrt_fusion) | copy-start | bytes 2308
  5.3 0.8 copy-start.20
  6.1 1.0 copy-start.7
  6.1 1.0 copy-start.17
  8.4 21.1 %all-to-all-start = ((bf16[8,48,1152]{2,1,0:T(8,128)(2,1)}), bf16[8,48,1152]{2,1,0:T(8,128)(2,1)S(1)}, u32[]{:S(2)}, u32[]{:S(2)}) async-start(bf16[8,48,1152]{2,1,0:T(8,128)(2,1)} %pad_maximum_fusion), calls=%async_computation | async-start | bytes 1769472 | tf_op jit(solution)/shard_map/all_to_all | solution.py:24
  31.5 3.1 %collective-permute-start = (bf16[24,1152]{1,0:T(8,128)(2,1)S(1)}, bf16[24,1152]{1,0:T(8,128)(2,1)S(1)}, u32[]{:S(2)}, u32[]{:S(2)}) collective-permute-start(bf16[24,1152]{1,0:T(8,128)(2,1)S(1)} %get-tuple-element.32), channel_id=1, source_target_pairs={{0,8},{8,0},{1,9},{9,1},{2,10},{10,2},{3,11},{11,3},{4,12},{12,4},... | collective-permute-start | bytes 165896 | tf_op jit(solution)/shard_map/ppermute | solution.py:29
  34.7 17.8 %copy-start.12 = (bf16[48,1152]{1,0:T(8,128)(2,1)}, bf16[48,1152]{1,0:T(8,128)(2,1)S(1)}, u32[]{:S(2)}) copy-start(bf16[48,1152]{1,0:T(8,128)(2,1)S(1)} %pad_maximum_fusion.3.refs_0_) | copy-start | bytes 331780
  34.7 17.8 %collective-permute-start.1 = (bf16[48,1152]{1,0:T(8,128)(2,1)S(1)}, bf16[48,1152]{1,0:T(8,128)(2,1)S(1)}, u32[]{:S(2)}, u32[]{:S(2)}) collective-permute-start(bf16[48,1152]{1,0:T(8,128)(2,1)S(1)} %pad_maximum_fusion.3.refs_0_), channel_id=1, source_target_pairs={{0,96},{8,424},{32,128},{40,456},{64,160},{72,488},{96,192},{104,8... | collective-permute-start | bytes 331784 | tf_op jit(solution)/shard_map/ppermute | solution.py:44
  42.4 20.1 %collective-permute-start.2 = (bf16[48,1152]{1,0:T(8,128)(2,1)S(1)}, bf16[48,1152]{1,0:T(8,128)(2,1)S(1)}, u32[]{:S(2)}, u32[]{:S(2)}) collective-permute-start(bf16[48,1152]{1,0:T(8,128)(2,1)S(1)} %pad_maximum_fusion.3.refs_0_), channel_id=1, source_target_pairs={{0,192},{8,328},{32,224},{40,360},{64,256},{72,392},{96,288},{104,... | collective-permute-start | bytes 331784 | tf_op jit(solution)/shard_map/ppermute | solution.py:44
  52.5 26.4 %copy-start.9 = (bf16[48,1152]{1,0:T(8,128)(2,1)}, bf16[48,1152]{1,0:T(8,128)(2,1)S(1)}, u32[]{:S(2)}) copy-start(bf16[48,1152]{1,0:T(8,128)(2,1)S(1)} %collective-permute-done.1.refs_1_) | copy-start | bytes 331780
  62.6 16.4 %copy-start.10 = (bf16[48,1152]{1,0:T(8,128)(2,1)}, bf16[48,1152]{1,0:T(8,128)(2,1)S(1)}, u32[]{:S(2)}) copy-start(bf16[48,1152]{1,0:T(8,128)(2,1)S(1)} %collective-permute-done.2.refs_2_) | copy-start | bytes 331780
  62.6 16.3 %collective-permute-start.3 = (bf16[144,1152]{1,0:T(8,128)(2,1)S(1)}, bf16[144,1152]{1,0:T(8,128)(2,1)S(1)}, u32[]{:S(2)}, u32[]{:S(2)}) collective-permute-start(bf16[144,1152]{1,0:T(8,128)(2,1)S(1)} %pad_maximum_fusion.2), channel_id=1, source_target_pairs={{0,32},{8,488},{32,64},{40,8},{64,96},{72,40},{96,128},{104,72},{1... | collective-permute-start | bytes 995336 | tf_op jit(solution)/shard_map/ppermute | solution.py:44
  65.3 13.6 %collective-permute-start.4 = (bf16[120,1152]{1,0:T(8,128)(2,1)}, bf16[120,1152]{1,0:T(8,128)(2,1)S(1)}, u32[]{:S(2)}, u32[]{:S(2)}) collective-permute-start(bf16[120,1152]{1,0:T(8,128)(2,1)} %slice.14), channel_id=1, source_target_pairs={{0,64},{8,456},{32,96},{40,488},{64,128},{72,8},{96,160},{104,40},... | collective-permute-start | bytes 829448 | tf_op jit(solution)/shard_map/ppermute | solution.py:44
  70.5 22.1 %all-to-all-start.1 = ((bf16[16,24,1152]{2,1,0:T(8,128)(2,1)}), bf16[16,24,1152]{2,1,0:T(8,128)(2,1)S(1)}, u32[]{:S(2)}, u32[]{:S(2)}) async-start(bf16[16,24,1152]{2,1,0:T(8,128)(2,1)} %broadcast_in_dim.6), calls=%async_computation.1 | async-start | bytes 1769472 | tf_op jit(solution)/shard_map/all_to_all | solution.py:24
  78.9 13.7 %copy-start.8 = (bf16[120,1152]{1,0:T(8,128)(2,1)}, bf16[120,1152]{1,0:T(8,128)(2,1)S(1)}, u32[]{:S(2)}) copy-start(bf16[120,1152]{1,0:T(8,128)(2,1)S(1)} %collective-permute-done.4.refs_4_) | copy-start | bytes 829444
  78.9 13.6 %copy-start.6 = (bf16[144,1152]{1,0:T(8,128)(2,1)}, bf16[144,1152]{1,0:T(8,128)(2,1)S(1)}, u32[]{:S(2)}) copy-start(bf16[144,1152]{1,0:T(8,128)(2,1)S(1)} %collective-permute-done.3.refs_3_) | copy-start | bytes 995332
  80.0 12.6 %collective-permute-start.5 = (bf16[360,1152]{1,0:T(8,128)(2,1)}, bf16[360,1152]{1,0:T(8,128)(2,1)}, u32[]{:S(2)}, u32[]{:S(2)}) collective-permute-start(bf16[360,1152]{1,0:T(8,128)(2,1)} %pad_maximum_fusion.1), channel_id=1, source_target_pairs={{0,8},{8,0},{1,9},{9,1},{2,10},{10,2},{3,11},{11,3},{4,12},{12,4},... | collective-permute-start | bytes 2488328 | tf_op jit(solution)/shard_map/ppermute | solution.py:29
  92.5 0.9 copy-start.3
  99.6 21.0 %all-to-all-start.2 = ((bf16[16,24,1152]{2,1,0:T(8,128)(2,1)}), bf16[16,24,1152]{2,1,0:T(8,128)(2,1)S(1)}, u32[]{:S(2)}, u32[]{:S(2)}) async-start(bf16[16,24,1152]{2,1,0:T(8,128)(2,1)} %bitcast.30), calls=%async_computation.2 | async-start | bytes 1769472 | tf_op jit(solution)/shard_map/all_to_all | solution.py:24
  104.6 21.2 %collective-permute-start.6 = (bf16[360,1152]{1,0:T(8,128)(2,1)}, bf16[360,1152]{1,0:T(8,128)(2,1)S(1)}, u32[]{:S(2)}, u32[]{:S(2)}) collective-permute-start(bf16[360,1152]{1,0:T(8,128)(2,1)} %get-tuple-element.16), channel_id=1, source_target_pairs={{0,8},{8,0},{1,9},{9,1},{2,10},{10,2},{3,11},{11,3},{4,12},{12,4},... | collective-permute-start | bytes 2488328 | tf_op jit(solution)/shard_map/ppermute | solution.py:29
  121.7 32.0 %all-to-all-start.3 = ((bf16[8,24,1152]{2,1,0:T(8,128)(2,1)}), bf16[8,24,1152]{2,1,0:T(8,128)(2,1)}, u32[]{:S(2)}, u32[]{:S(2)}) async-start(bf16[8,24,1152]{2,1,0:T(8,128)(2,1)} %broadcast_in_dim.7), calls=%async_computation.3 | async-start | bytes 884736 | tf_op jit(solution)/shard_map/all_to_all | solution.py:24
  125.8 0.9 copy-start.4
  126.7 6.5 %copy-start.1 = (bf16[1152,538]{0,1:T(8,128)(2,1)S(1)}, bf16[1152,538]{0,1:T(8,128)(2,1)}, u32[]{:S(2)}) copy-start(bf16[1152,538]{0,1:T(8,128)(2,1)} %param.11) | copy-start | bytes 3718660
  126.7 6.6 %copy-start.18 = (f32[1152]{0:T(1024)S(1)}, f32[1152]{0:T(1024)}, u32[]{:S(2)}) copy-start(f32[1152]{0:T(1024)} %param.10) | copy-start | bytes 13828
  129.4 12.2 %collective-permute-start.7 = (bf16[144,1152]{1,0:T(8,128)(2,1)}, bf16[144,1152]{1,0:T(8,128)(2,1)S(1)}, u32[]{:S(2)}, u32[]{:S(2)}) collective-permute-start(bf16[144,1152]{1,0:T(8,128)(2,1)} %get-tuple-element.17), channel_id=1, source_target_pairs={{0,480},{8,40},{32,0},{40,72},{64,32},{72,104},{96,64},{104,136},{... | collective-permute-start | bytes 995336 | tf_op jit(solution)/shard_map/ppermute | solution.py:44
  131.4 9.6 %collective-permute-start.8 = (bf16[120,1152]{1,0:T(8,128)(2,1)}, bf16[120,1152]{1,0:T(8,128)(2,1)S(1)}, u32[]{:S(2)}, u32[]{:S(2)}) collective-permute-start(bf16[120,1152]{1,0:T(8,128)(2,1)} %get-tuple-element.18), channel_id=1, source_target_pairs={{0,448},{8,72},{32,480},{40,104},{64,0},{72,136},{96,32},{104,168}... | collective-permute-start | bytes 829448 | tf_op jit(solution)/shard_map/ppermute | solution.py:44
  141.0 0.7 copy-start.14
  141.7 0.7 copy-start.13
  145.1 15.0 %collective-permute-start.10 = (bf16[48,1152]{1,0:T(8,128)(2,1)}, bf16[48,1152]{1,0:T(8,128)(2,1)S(1)}, u32[]{:S(2)}, u32[]{:S(2)}) collective-permute-start(bf16[48,1152]{1,0:T(8,128)(2,1)} %get-tuple-element.21), channel_id=1, source_target_pairs={{0,320},{8,200},{32,352},{40,232},{64,384},{72,264},{96,416},{104,... | collective-permute-start | bytes 331784 | tf_op jit(solution)/shard_map/ppermute | solution.py:44
  149.3 17.2 %collective-permute-start.9 = (bf16[48,1152]{1,0:T(8,128)(2,1)}, bf16[48,1152]{1,0:T(8,128)(2,1)S(1)}, u32[]{:S(2)}, u32[]{:S(2)}) collective-permute-start(bf16[48,1152]{1,0:T(8,128)(2,1)} %get-tuple-element.20), channel_id=1, source_target_pairs={{0,416},{8,104},{32,448},{40,136},{64,480},{72,168},{96,0},{104,20... | collective-permute-start | bytes 331784 | tf_op jit(solution)/shard_map/ppermute | solution.py:44
  160.1 6.4 %copy-start.15 = (bf16[48,1152]{1,0:T(8,128)(2,1)}, bf16[48,1152]{1,0:T(8,128)(2,1)S(1)}, u32[]{:S(2)}) copy-start(bf16[48,1152]{1,0:T(8,128)(2,1)S(1)} %collective-permute-done.10.six_ref) | copy-start | bytes 331780
  166.5 0.6 copy-start.16
  168.9 4.8 %copy-start.11 = (f32[24,1152]{1,0:T(8,128)S(1)}, f32[24,1152]{1,0:T(8,128)}, u32[]{:S(2)}) copy-start(f32[24,1152]{1,0:T(8,128)} %get-tuple-element.22) | copy-start | bytes 331780
  168.9 3.8 %collective-permute-start.11 = (bf16[24,1152]{1,0:T(8,128)(2,1)}, bf16[24,1152]{1,0:T(8,128)(2,1)S(1)}, u32[]{:S(2)}, u32[]{:S(2)}) collective-permute-start(bf16[24,1152]{1,0:T(8,128)(2,1)} %get-tuple-element.23), channel_id=1, source_target_pairs={{0,8},{8,0},{1,9},{9,1},{2,10},{10,2},{3,11},{11,3},{4,12},{12,4},... | collective-permute-start | bytes 165896 | tf_op jit(solution)/shard_map/ppermute | solution.py:29
  176.6 8.2 %copy-start.5 = (bf16[192,1152]{1,0:T(8,128)(2,1)S(1)}, bf16[192,1152]{1,0:T(8,128)(2,1)}, u32[]{:S(2)}) copy-start(bf16[192,1152]{1,0:T(8,128)(2,1)} %param.8) | copy-start | bytes 1327108
  176.6 24.9 %all-to-all-start.4 = ((bf16[8,520,128]{2,1,0:T(8,128)(2,1)}), bf16[8,520,128]{2,1,0:T(8,128)(2,1)S(1)}, u32[]{:S(2)}, u32[]{:S(2)}) async-start(bf16[8,520,128]{2,1,0:T(8,128)(2,1)} %shard_map.99), calls=%async_computation.4 | async-start | bytes 2129920 | tf_op jit(solution)/shard_map/all_to_all | solution.py:24
  201.6 1.0 copy-start.2

commit v5 on v4

--- a/solution.py
+++ b/solution.py
@@ -47,7 +47,8 @@
 def gathered_line(array):
     share = array.shape[0]
     pair = jnp.concatenate([array, exchange(array, "c", 1)], axis=0)
-    far = [along(pair, -k) for k in FAR]
+    third = along(pair, -FAR[0])
+    far = [third, along(third, FAR[0] - FAR[1])]
     near = jnp.concatenate([pair, *far], axis=0)
     cut = near.shape[0] - share
     last = [along(near, -NEAR[0]), along(near[:cut], -NEAR[1])]
@@ -157,16 +158,17 @@
 def pack_kernel(back_ref, sums_ref, text_ref, out_ref):
     heads = out_ref.shape[0]
     cols = back_ref.shape[0] // heads
-    rows = back_ref.shape[1]
+    half = cols // 2
+    side = LANES // 2
     share, width = text_ref.shape
     for h in range(heads):
         block = back_ref[h * cols : (h + 1) * cols, :]
         out_ref[h, :cols, :] = block[:, :LANES]
-        out_ref[h, cols : 2 * cols, : rows - LANES] = block[:, LANES:]
-        out_ref[h, cols : 2 * cols, rows - LANES :] = jnp.zeros((cols, 2 * LANES - rows), BF16)
-        out_ref[h, 2 * cols : 2 * cols + SUM_ROWS, :] = sums_ref[...]
+        out_ref[h, cols : cols + half, :side] = block[:half, LANES:]
+        out_ref[h, cols : cols + half, side:] = block[half:, LANES:]
+        out_ref[h, cols + half : cols + half + SUM_ROWS, :] = sums_ref[...]
         for k in range(width // LANES):
-            first = 2 * cols + SUM_ROWS + k * share
+            first = cols + half + SUM_ROWS + k * share
             out_ref[h, first : first + share, :] = text_ref[:, k * LANES : (k + 1) * LANES]
 
 
@@ -175,33 +177,40 @@
 ):
     heads = packed_ref.shape[0]
     cols, rows = direct_ref.shape
+    half = cols // 2
+    side = LANES // 2
     width = mapping_ref.shape[1]
     share = rows // heads
-    sums = packed_ref[0, 2 * cols : 2 * cols + SUM_ROWS, :].astype(F32)
-    for h in range(1, heads):
-        sums = sums + packed_ref[h, 2 * cols : 2 * cols + SUM_ROWS, :].astype(F32)
-    for half, span in enumerate((LANES, rows - LANES)):
-        here = slice(half * LANES, half * LANES + span)
-        total = packed_ref[0, half * cols : (half + 1) * cols, :span].astype(F32)
+    tail = cols + half + SUM_ROWS
+
+    def added(first, last):
+        total = packed_ref[0, first:last, :].astype(F32)
         for h in range(1, heads):
-            total = total + packed_ref[h, half * cols : (half + 1) * cols, :span].astype(F32)
-        one = (sums[half : half + 1, :span] + sums[half + 4 : half + 5, :span]) / width
-        two = (sums[half + 2 : half + 3, :span] + sums[half + 6 : half + 7, :span]) / width
-        image_ref[:, here] = direct_ref[:, here] + inv_ref[:, here] * (
-            total * gain_ref[...] - one - centred_ref[:, here] * two
+            total = total + packed_ref[h, first:last, :].astype(F32)
+        return total
+
+    sums = added(cols + half, tail)
+    low = added(0, cols)
+    high = added(cols, cols + half)
+
+    def store(top, bottom, here, part, row):
+        span = part.shape[1]
+        one = (sums[row : row + 1, :span] + sums[row + 4 : row + 5, :span]) / width
+        two = (sums[row + 2 : row + 3, :span] + sums[row + 6 : row + 7, :span]) / width
+        image_ref[top:bottom, here] = direct_ref[top:bottom, here] + inv_ref[:, here] * (
+            part * gain_ref[top:bottom, :] - one - centred_ref[top:bottom, here] * two
         )
+
+    store(0, cols, slice(0, LANES), low, 0)
+    store(0, half, slice(LANES, rows), high[:, :side], 1)
+    store(half, cols, slice(LANES, rows), high[:, side:], 1)
     for h in range(heads):
         for k in range(width // LANES):
-            first = 2 * cols + SUM_ROWS + k * share
+            first = tail + k * share
             rows_ref[h * share : (h + 1) * share, k * LANES : (k + 1) * LANES] = packed_ref[
                 h, first : first + share, :
             ]
-    text_ref[...] = lax.dot_general(
-        mapping_ref[...],
-        rows_ref[...],
-        (((1,), (1,)), ((), ())),
-        preferred_element_type=F32,
-    )
+    text_ref[...] = dot(mapping_ref[...], rows_ref[...], ((1,), (1,)))
 
 
 def gelu_tanh(values):
@@ -293,7 +302,7 @@
     sums_both = jnp.concatenate([sums_high, sums_low], axis=0).astype(BF16)
     sums_both = jnp.pad(sums_both, ((0, 0), (0, 2 * LANES - rows))).reshape(-1, LANES)
     sums_both = jnp.pad(sums_both, ((0, SUM_ROWS - sums_both.shape[0]), (0, 0)))
-    length = 2 * cols + SUM_ROWS + share * width // LANES
+    length = cols + cols // 2 + SUM_ROWS + share * width // LANES
     packed = pl.pallas_call(
         pack_kernel, out_shape=jax.ShapeDtypeStruct((heads, length, LANES), BF16)
     )(back, sums_both, grad_text_share)

time: 206 us -> 204 us (level)
  starting transfers between devices: 71.7 us -> 64.2 us
  waiting for transfers between devices: 84.3 us -> 88.1 us
    ppermute x8, waiting for transfers between devices: 32.5 us -> 42.1 us  [along(): return lax.ppermute(array, LINE, moves)]
    ppermute x8, starting transfers between devices: 36.3 us -> 28.5 us  [along(): return lax.ppermute(array, LINE, moves)]
    all_to_all x5, waiting for transfers between devices: 50.6 us -> 44.8 us  [swap(): return lax.all_to_all(array, axes, 0, 0, tiled=True)]
    unnamed x42 -> x40, local copies, waits for them, and re-layouts: 5.48 us -> 6.03 us
where the time goes in v5:
time: 204 us; the launch traced here: 203 us
  waiting for transfers between devices  88.1 us (43%)
  starting transfers between devices  64.2 us (31%)
  Pallas kernels  17.9 us (9%)
  local copies, waits for them, and re-layouts  11.1 us (5%)
  other arithmetic  10.6 us (5%)
  matrix products  8.6 us (4%)
  between operations  2.27 us (1%)
    all_to_all x5, waiting for transfers between devices, swap(): return lax.all_to_all(array, axes, 0, 0, tiled=True)  44.8 us
    ppermute x8, waiting for transfers between devices, along(): return lax.ppermute(array, LINE, moves)  42.1 us
    ppermute x8, starting transfers between devices, along(): return lax.ppermute(array, LINE, moves)  28.5 us
    all_to_all x5, starting transfers between devices, swap(): return lax.all_to_all(array, axes, 0, 0, tiled=True)  28 us
    dot_general x7, matrix products, dot(): return lax.dot_general(a, b, (dims, ((), ())), preferred_element_type=F32)  8.6 us
    ppermute x4, starting transfers between devices, exchange(): return lax.ppermute(array, axes, [(i, i ^ k) for i in range(n)])  7.66 us
    pallas_call x1, Pallas kernels, per_device(): pl.pallas_call(functools.partial(pairs_kernel, share), in_specs=[scalars,...  6.14 us
    unnamed x40, local copies, waits for them, and re-layouts  6.03 us
  transfers between devices with their start and end apart: 17, of which 11 were waited for; matrix products, arithmetic and copies ran while one was open for 6% of the time, Pallas kernels for 3%

profile of v5, /device:TPU:32, one launch (start us, length us, event | category | flops | bytes accessed | tf_op | source)
XLA Modules:
  0.0 202.7 jit_solution(18147774104773381549)
XLA Ops:
  0.6 1.3 convert_reduce_fusion.2
  1.9 1.3 fusion.3
  3.2 2.1 %fusion.16 = f32[192,538]{1,0:T(8,128)S(1)} fusion(bf16[1152,538]{0,1:T(8,128)(2,1)} %param.11, bf16[192,1152]{1,0:T(8,128)(2,1)} %param.8, f32[1152]{0:T(1024)} %param.10, f32[192]{0:T(256)S(1)} %add_rsqrt_fusion, f32[192]{0:T(256)S(1)} %broadcast_multiply_fusion), kind=kOutput, calls=%fused_computation.33 | convolution fusion | flops 239099904 | bytes 2101248 | tf_op jit(solution)/shard_map/dot_general | solution.py:227
  5.3 0.8 copy-done.19
  6.1 0.6 convolution_convert_fusion.1
  6.7 0.4 copy-done.7
  7.1 0.3 convolution_convert_fusion.2
  7.4 1.0 pad_maximum_fusion
  8.4 6.9 %all-to-all-start = ((bf16[8,48,1152]{2,1,0:T(8,128)(2,1)}), bf16[8,48,1152]{2,1,0:T(8,128)(2,1)S(1)}, u32[]{:S(2)}, u32[]{:S(2)}) async-start(bf16[8,48,1152]{2,1,0:T(8,128)(2,1)} %pad_maximum_fusion), calls=%async_computation | async-start | bytes 1769472 | tf_op jit(solution)/shard_map/all_to_all | solution.py:24
  15.4 14.2 %all-to-all-done = bf16[8,48,1152]{2,1,0:T(8,128)(2,1)S(1)} async-done(((bf16[8,48,1152]{2,1,0:T(8,128)(2,1)}), bf16[8,48,1152]{2,1,0:T(8,128)(2,1)S(1)}, u32[]{:S(2)}, u32[]{:S(2)}) %all-to-all-start) | async-done | bytes 884768 | tf_op jit(solution)/shard_map/all_to_all | solution.py:24
  29.6 1.0 multiply_reduce_fusion.2
  30.6 0.9 multiply_convert_fusion.2
  31.5 1.9 collective-permute-start
  33.4 1.2 collective-permute-done
  34.7 7.7 %collective-permute-start.1 = (bf16[48,1152]{1,0:T(8,128)(2,1)S(1)}, bf16[48,1152]{1,0:T(8,128)(2,1)S(1)}, u32[]{:S(2)}, u32[]{:S(2)}) collective-permute-start(bf16[48,1152]{1,0:T(8,128)(2,1)S(1)} %pad_maximum_fusion.3.refs_0_), channel_id=1, source_target_pairs={{0,96},{8,424},{32,128},{40,456},{64,160},{72,488},{96,192},{104,8... | collective-permute-start | bytes 331784 | tf_op jit(solution)/shard_map/ppermute | solution.py:44
  42.4 7.6 %collective-permute-done.1.refs_1_ = bf16[48,1152]{1,0:T(8,128)(2,1)S(1)} collective-permute-done((bf16[48,1152]{1,0:T(8,128)(2,1)S(1)}, bf16[48,1152]{1,0:T(8,128)(2,1)S(1)}, u32[]{:S(2)}, u32[]{:S(2)}) %collective-permute-start.1) | collective-permute-done | bytes 110624 | tf_op jit(solution)/shard_map/ppermute | solution.py:44
  50.1 2.1 %collective-permute-start.2 = (bf16[48,1152]{1,0:T(8,128)(2,1)S(1)}, bf16[48,1152]{1,0:T(8,128)(2,1)S(1)}, u32[]{:S(2)}, u32[]{:S(2)}) collective-permute-start(bf16[48,1152]{1,0:T(8,128)(2,1)S(1)} %collective-permute-done.1.refs_1_), channel_id=1, source_target_pairs={{0,96},{8,424},{32,128},{40,456},{64,160},{72,488},{96,192},{104,8... | collective-permute-start | bytes 331784 | tf_op jit(solution)/shard_map/ppermute | solution.py:44
  52.2 7.6 %collective-permute-done.2.refs_2_ = bf16[48,1152]{1,0:T(8,128)(2,1)S(1)} collective-permute-done((bf16[48,1152]{1,0:T(8,128)(2,1)S(1)}, bf16[48,1152]{1,0:T(8,128)(2,1)S(1)}, u32[]{:S(2)}, u32[]{:S(2)}) %collective-permute-start.2) | collective-permute-done | bytes 110624 | tf_op jit(solution)/shard_map/ppermute | solution.py:44
  59.8 4.6 %collective-permute-start.3 = (bf16[144,1152]{1,0:T(8,128)(2,1)S(1)}, bf16[144,1152]{1,0:T(8,128)(2,1)S(1)}, u32[]{:S(2)}, u32[]{:S(2)}) collective-permute-start(bf16[144,1152]{1,0:T(8,128)(2,1)S(1)} %pad_maximum_fusion.2), channel_id=1, source_target_pairs={{0,32},{8,488},{32,64},{40,8},{64,96},{72,40},{96,128},{104,72},{1... | collective-permute-start | bytes 995336 | tf_op jit(solution)/shard_map/ppermute | solution.py:44
  64.4 0.7 slice.14
  65.1 1.9 collective-permute-start.4
  67.1 1.0 broadcast_in_dim.6
  68.0 4.2 %all-to-all-start.1 = ((bf16[16,24,1152]{2,1,0:T(8,128)(2,1)}), bf16[16,24,1152]{2,1,0:T(8,128)(2,1)S(1)}, u32[]{:S(2)}, u32[]{:S(2)}) async-start(bf16[16,24,1152]{2,1,0:T(8,128)(2,1)} %broadcast_in_dim.6), calls=%async_computation.1 | async-start | bytes 1769472 | tf_op jit(solution)/shard_map/all_to_all | solution.py:24
  72.2 6.5 %collective-permute-done.4.refs_4_ = bf16[120,1152]{1,0:T(8,128)(2,1)S(1)} collective-permute-done((bf16[120,1152]{1,0:T(8,128)(2,1)}, bf16[120,1152]{1,0:T(8,128)(2,1)S(1)}, u32[]{:S(2)}, u32[]{:S(2)}) %collective-permute-start.4) | collective-permute-done | bytes 276512 | tf_op jit(solution)/shard_map/ppermute | solution.py:44
  78.8 1.0 pad_maximum_fusion.1
  79.8 1.9 collective-permute-start.5
  83.0 0.6 pad_maximum_fusion.5.consts_ref
  83.7 4.3 %all-to-all-done.1 = bf16[16,24,1152]{2,1,0:T(8,128)(2,1)S(1)} async-done(((bf16[16,24,1152]{2,1,0:T(8,128)(2,1)}), bf16[16,24,1152]{2,1,0:T(8,128)(2,1)S(1)}, u32[]{:S(2)}, u32[]{:S(2)}) %all-to-all-start.1) | async-done | bytes 884768 | tf_op jit(solution)/shard_map/all_to_all | solution.py:24
  88.0 0.9 copy-done.3
  88.9 6.1 %shard_map.95 = (bf16[360,1152]{1,0:T(8,128)(2,1)}, f32[408,1152]{1,0:T(8,128)}, bf16[384,1152]{1,0:T(8,128)(2,1)}) custom-call(f32[2]{0:T(128)} %pad_maximum_fusion.5.consts_ref, s32[1]{0:T(128)} %bitcast.4.start_ref, bf16[48,1152]{1,0:T(8,128)(2,1)} %copy-done.11, bf16[48,1152]{1,0:T(8,128)(2,1)} %copy-done.9, bf16[48,1152]{1,0:T(8,128)(2,1)} %copy-done.10, ...), custom_call_target="tpu_custom_call" | custom-call | tf_op jit(solution)/shard_map/pallas_call | solution.py:269
  95.1 5.6 %all-to-all-start.2 = ((bf16[16,24,1152]{2,1,0:T(8,128)(2,1)}), bf16[16,24,1152]{2,1,0:T(8,128)(2,1)S(1)}, u32[]{:S(2)}, u32[]{:S(2)}) async-start(bf16[16,24,1152]{2,1,0:T(8,128)(2,1)} %bitcast.30), calls=%async_computation.2 | async-start | bytes 1769472 | tf_op jit(solution)/shard_map/all_to_all | solution.py:24
  100.6 1.9 collective-permute-start.6
  102.6 14.7 %all-to-all-done.2 = bf16[16,24,1152]{2,1,0:T(8,128)(2,1)S(1)} async-done(((bf16[16,24,1152]{2,1,0:T(8,128)(2,1)}), bf16[16,24,1152]{2,1,0:T(8,128)(2,1)S(1)}, u32[]{:S(2)}, u32[]{:S(2)}) %all-to-all-start.2) | async-done | bytes 884768 | tf_op jit(solution)/shard_map/all_to_all | solution.py:24
  117.6 0.8 broadcast_in_dim.7
  118.4 4.2 %all-to-all-start.3 = ((bf16[8,24,1152]{2,1,0:T(8,128)(2,1)}), bf16[8,24,1152]{2,1,0:T(8,128)(2,1)}, u32[]{:S(2)}, u32[]{:S(2)}) async-start(bf16[8,24,1152]{2,1,0:T(8,128)(2,1)} %broadcast_in_dim.7), calls=%async_computation.3 | async-start | bytes 884736 | tf_op jit(solution)/shard_map/all_to_all | solution.py:24
  122.7 0.9 copy-done.4
  123.6 2.6 %shard_map.96 = (bf16[144,1152]{1,0:T(8,128)(2,1)}, bf16[120,1152]{1,0:T(8,128)(2,1)}) custom-call(f32[408,1152]{1,0:T(8,128)} %get-tuple-element.15.kept_ref, bf16[360,1152]{1,0:T(8,128)(2,1)} %copy-done.4), custom_call_target="tpu_custom_call" | custom-call | tf_op jit(solution)/shard_map/pallas_call | solution.py:135
  126.2 3.3 %collective-permute-start.7 = (bf16[144,1152]{1,0:T(8,128)(2,1)}, bf16[144,1152]{1,0:T(8,128)(2,1)S(1)}, u32[]{:S(2)}, u32[]{:S(2)}) collective-permute-start(bf16[144,1152]{1,0:T(8,128)(2,1)} %get-tuple-element.17), channel_id=1, source_target_pairs={{0,480},{8,40},{32,0},{40,72},{64,32},{72,104},{96,64},{104,136},{... | collective-permute-start | bytes 995336 | tf_op jit(solution)/shard_map/ppermute | solution.py:44
  129.5 2.6 %collective-permute-start.8 = (bf16[120,1152]{1,0:T(8,128)(2,1)}, bf16[120,1152]{1,0:T(8,128)(2,1)S(1)}, u32[]{:S(2)}, u32[]{:S(2)}) collective-permute-start(bf16[120,1152]{1,0:T(8,128)(2,1)} %get-tuple-element.18), channel_id=1, source_target_pairs={{0,448},{8,72},{32,480},{40,104},{64,0},{72,136},{96,32},{104,168}... | collective-permute-start | bytes 829448 | tf_op jit(solution)/shard_map/ppermute | solution.py:44
  132.5 9.6 %collective-permute-done.8.two_ref = bf16[120,1152]{1,0:T(8,128)(2,1)S(1)} collective-permute-done((bf16[120,1152]{1,0:T(8,128)(2,1)}, bf16[120,1152]{1,0:T(8,128)(2,1)S(1)}, u32[]{:S(2)}, u32[]{:S(2)}) %collective-permute-start.8) | collective-permute-done | bytes 276512 | tf_op jit(solution)/shard_map/ppermute | solution.py:44
  142.0 0.7 copy-done.13
  142.7 0.7 copy-done.12
  143.5 2.7 %shard_map.97 = (f32[48,1152]{1,0:T(8,128)}, bf16[48,1152]{1,0:T(8,128)(2,1)}, bf16[48,1152]{1,0:T(8,128)(2,1)}) custom-call(f32[408,1152]{1,0:T(8,128)} %get-tuple-element.15.kept_ref, bf16[360,1152]{1,0:T(8,128)(2,1)} %copy-done.4, bf16[144,1152]{1,0:T(8,128)(2,1)} %copy-done.12, bf16[120,1152]{1,0:T(8,128)(2,1)} %copy-done.13), custom_call_target="tpu_custom_call" | custom-call | tf_op jit(solution)/shard_map/pallas_call | solution.py:141
  146.1 2.3 %collective-permute-start.10 = (bf16[48,1152]{1,0:T(8,128)(2,1)}, bf16[48,1152]{1,0:T(8,128)(2,1)S(1)}, u32[]{:S(2)}, u32[]{:S(2)}) collective-permute-start(bf16[48,1152]{1,0:T(8,128)(2,1)} %get-tuple-element.21), channel_id=1, source_target_pairs={{0,320},{8,200},{32,352},{40,232},{64,384},{72,264},{96,416},{104,... | collective-permute-start | bytes 331784 | tf_op jit(solution)/shard_map/ppermute | solution.py:44
  148.5 4.0 %collective-permute-start.9 = (bf16[48,1152]{1,0:T(8,128)(2,1)}, bf16[48,1152]{1,0:T(8,128)(2,1)S(1)}, u32[]{:S(2)}, u32[]{:S(2)}) collective-permute-start(bf16[48,1152]{1,0:T(8,128)(2,1)} %get-tuple-element.20), channel_id=1, source_target_pairs={{0,416},{8,104},{32,448},{40,136},{64,480},{72,168},{96,0},{104,20... | collective-permute-start | bytes 331784 | tf_op jit(solution)/shard_map/ppermute | solution.py:44
  152.5 2.0 %fusion.7 = (f32[192]{0:T(256)S(1)}, f32[192]{0:T(256)S(1)}, bf16[192,538]{1,0:T(8,128)(2,1)S(1)}) fusion(f32[538]{0:T(1024)S(1)} %multiply_reduce_fusion, f32[192,538]{1,0:T(8,128)} %copy-done.19, bf16[192,1152]{1,0:T(8,128)(2,1)} %bitcast.7, bf16[538,1152]{1,0:T(8,128)(2,1)S(1)} %copy-done), kind=kOutput, calls=%fused_computation.23 | convolution fusion | flops 240576000 | bytes 2305384 | tf_op jit(solution)/shard_map/dot_general | solution.py:227
  154.5 0.5 convolution_convert_fusion
  155.1 6.0 %collective-permute-done.10.six_ref = bf16[48,1152]{1,0:T(8,128)(2,1)S(1)} collective-permute-done((bf16[48,1152]{1,0:T(8,128)(2,1)}, bf16[48,1152]{1,0:T(8,128)(2,1)S(1)}, u32[]{:S(2)}, u32[]{:S(2)}) %collective-permute-start.10) | collective-permute-done | bytes 110624 | tf_op jit(solution)/shard_map/ppermute | solution.py:44
  161.0 4.8 %collective-permute-done.9.three_ref = bf16[48,1152]{1,0:T(8,128)(2,1)S(1)} collective-permute-done((bf16[48,1152]{1,0:T(8,128)(2,1)}, bf16[48,1152]{1,0:T(8,128)(2,1)S(1)}, u32[]{:S(2)}, u32[]{:S(2)}) %collective-permute-start.9) | collective-permute-done | bytes 110624 | tf_op jit(solution)/shard_map/ppermute | solution.py:44
  165.8 0.6 copy-done.15
  166.5 1.7 shard_map.98
  168.2 1.9 collective-permute-start.11
  170.2 1.1 copy.13
  171.3 0.6 pad.9.sums_ref
  171.9 1.0 fusion.31
  172.9 1.6 fusion.34.text_ref
  174.5 2.2 %shard_map.99 = bf16[8,448,128]{2,1,0:T(8,128)(2,1)} custom-call(bf16[1152,192]{1,0:T(8,128)(2,1)} %bitcast.28, bf16[16,128]{1,0:T(8,128)(2,1)} %pad.9.sums_ref, bf16[24,1152]{1,0:T(8,128)(2,1)} %fusion.34.text_ref), custom_call_target="tpu_custom_call" | custom-call | tf_op jit(solution)/shard_map/pallas_call | solution.py:306
  176.7 7.1 %all-to-all-start.4 = ((bf16[8,448,128]{2,1,0:T(8,128)(2,1)}), bf16[8,448,128]{2,1,0:T(8,128)(2,1)S(1)}, u32[]{:S(2)}, u32[]{:S(2)}) async-start(bf16[8,448,128]{2,1,0:T(8,128)(2,1)} %shard_map.99), calls=%async_computation.4 | async-start | bytes 1835008 | tf_op jit(solution)/shard_map/all_to_all | solution.py:24
  183.9 0.7 copy.14.gain_ref
  184.6 1.0 fusion.centred_ref
  185.6 2.0 fusion.6.direct_ref
  187.7 11.6 %all-to-all-done.4.packed_ref = bf16[8,448,128]{2,1,0:T(8,128)(2,1)S(1)} async-done(((bf16[8,448,128]{2,1,0:T(8,128)(2,1)}), bf16[8,448,128]{2,1,0:T(8,128)(2,1)S(1)}, u32[]{:S(2)}, u32[]{:S(2)}) %all-to-all-start.4) | async-done | bytes 917536 | tf_op jit(solution)/shard_map/all_to_all | solution.py:24
  199.2 0.9 copy-done.2
  200.1 2.6 %shard_map.100 = (f32[144,192]{1,0:T(8,128)}, f32[144,192]{1,0:T(8,128)}, bf16[192,1152]{1,0:T(8,128)(2,1)}) custom-call(bf16[8,448,128]{2,1,0:T(8,128)(2,1)} %copy-done.2, f32[144,192]{1,0:T(8,128)} %fusion.6.direct_ref, f32[144,192]{1,0:T(8,128)} %fusion.centred_ref, f32[1,192]{1,0:T(1,128)} %bitcast.33, f32[144,1]{1,0:T(8,128)} %copy.14.gain_ref, ...), custom_call_target="tpu_custom_call" | custom-call | tf_op jit(solution)/shard_map/pallas_call | solution.py:317
  (53 shorter events, 1.1 us)
Async XLA Ops:
  0.6 5.5 %copy-start = (bf16[538,1152]{1,0:T(8,128)(2,1)S(1)}, bf16[538,1152]{1,0:T(8,128)(2,1)}, u32[]{:S(2)}) copy-start(bf16[538,1152]{1,0:T(8,128)(2,1)} %param.12) | copy-start | bytes 3718660
  3.2 181.5 %copy-start.18 = (f32[192]{0:T(256)}, f32[192]{0:T(256)S(1)}, u32[]{:S(2)}) copy-start(f32[192]{0:T(256)S(1)} %add_rsqrt_fusion) | copy-start | bytes 2308
  5.3 0.8 copy-start.19
  6.1 1.0 copy-start.7
  6.1 1.0 copy-start.16
  8.4 21.1 %all-to-all-start = ((bf16[8,48,1152]{2,1,0:T(8,128)(2,1)}), bf16[8,48,1152]{2,1,0:T(8,128)(2,1)S(1)}, u32[]{:S(2)}, u32[]{:S(2)}) async-start(bf16[8,48,1152]{2,1,0:T(8,128)(2,1)} %pad_maximum_fusion), calls=%async_computation | async-start | bytes 1769472 | tf_op jit(solution)/shard_map/all_to_all | solution.py:24
  31.5 3.1 %collective-permute-start = (bf16[24,1152]{1,0:T(8,128)(2,1)S(1)}, bf16[24,1152]{1,0:T(8,128)(2,1)S(1)}, u32[]{:S(2)}, u32[]{:S(2)}) collective-permute-start(bf16[24,1152]{1,0:T(8,128)(2,1)S(1)} %get-tuple-element.32), channel_id=1, source_target_pairs={{0,8},{8,0},{1,9},{9,1},{2,10},{10,2},{3,11},{11,3},{4,12},{12,4},... | collective-permute-start | bytes 165896 | tf_op jit(solution)/shard_map/ppermute | solution.py:29
  34.7 7.8 %copy-start.11 = (bf16[48,1152]{1,0:T(8,128)(2,1)}, bf16[48,1152]{1,0:T(8,128)(2,1)S(1)}, u32[]{:S(2)}) copy-start(bf16[48,1152]{1,0:T(8,128)(2,1)S(1)} %pad_maximum_fusion.3.refs_0_) | copy-start | bytes 331780
  34.7 15.4 %collective-permute-start.1 = (bf16[48,1152]{1,0:T(8,128)(2,1)S(1)}, bf16[48,1152]{1,0:T(8,128)(2,1)S(1)}, u32[]{:S(2)}, u32[]{:S(2)}) collective-permute-start(bf16[48,1152]{1,0:T(8,128)(2,1)S(1)} %pad_maximum_fusion.3.refs_0_), channel_id=1, source_target_pairs={{0,96},{8,424},{32,128},{40,456},{64,160},{72,488},{96,192},{104,8... | collective-permute-start | bytes 331784 | tf_op jit(solution)/shard_map/ppermute | solution.py:44
  50.1 28.7 %copy-start.9 = (bf16[48,1152]{1,0:T(8,128)(2,1)}, bf16[48,1152]{1,0:T(8,128)(2,1)S(1)}, u32[]{:S(2)}) copy-start(bf16[48,1152]{1,0:T(8,128)(2,1)S(1)} %collective-permute-done.1.refs_1_) | copy-start | bytes 331780
  50.1 9.7 %collective-permute-start.2 = (bf16[48,1152]{1,0:T(8,128)(2,1)S(1)}, bf16[48,1152]{1,0:T(8,128)(2,1)S(1)}, u32[]{:S(2)}, u32[]{:S(2)}) collective-permute-start(bf16[48,1152]{1,0:T(8,128)(2,1)S(1)} %collective-permute-done.1.refs_1_), channel_id=1, source_target_pairs={{0,96},{8,424},{32,128},{40,456},{64,160},{72,488},{96,192},{104,8... | collective-permute-start | bytes 331784 | tf_op jit(solution)/shard_map/ppermute | solution.py:44
  59.8 19.0 %copy-start.10 = (bf16[48,1152]{1,0:T(8,128)(2,1)}, bf16[48,1152]{1,0:T(8,128)(2,1)S(1)}, u32[]{:S(2)}) copy-start(bf16[48,1152]{1,0:T(8,128)(2,1)S(1)} %collective-permute-done.2.refs_2_) | copy-start | bytes 331780
  59.8 18.9 %collective-permute-start.3 = (bf16[144,1152]{1,0:T(8,128)(2,1)S(1)}, bf16[144,1152]{1,0:T(8,128)(2,1)S(1)}, u32[]{:S(2)}, u32[]{:S(2)}) collective-permute-start(bf16[144,1152]{1,0:T(8,128)(2,1)S(1)} %pad_maximum_fusion.2), channel_id=1, source_target_pairs={{0,32},{8,488},{32,64},{40,8},{64,96},{72,40},{96,128},{104,72},{1... | collective-permute-start | bytes 995336 | tf_op jit(solution)/shard_map/ppermute | solution.py:44
  65.1 13.6 %collective-permute-start.4 = (bf16[120,1152]{1,0:T(8,128)(2,1)}, bf16[120,1152]{1,0:T(8,128)(2,1)S(1)}, u32[]{:S(2)}, u32[]{:S(2)}) collective-permute-start(bf16[120,1152]{1,0:T(8,128)(2,1)} %slice.14), channel_id=1, source_target_pairs={{0,64},{8,456},{32,96},{40,488},{64,128},{72,8},{96,160},{104,40},... | collective-permute-start | bytes 829448 | tf_op jit(solution)/shard_map/ppermute | solution.py:44
  68.0 20.0 %all-to-all-start.1 = ((bf16[16,24,1152]{2,1,0:T(8,128)(2,1)}), bf16[16,24,1152]{2,1,0:T(8,128)(2,1)S(1)}, u32[]{:S(2)}, u32[]{:S(2)}) async-start(bf16[16,24,1152]{2,1,0:T(8,128)(2,1)} %broadcast_in_dim.6), calls=%async_computation.1 | async-start | bytes 1769472 | tf_op jit(solution)/shard_map/all_to_all | solution.py:24
  78.7 9.3 %copy-start.8 = (bf16[120,1152]{1,0:T(8,128)(2,1)}, bf16[120,1152]{1,0:T(8,128)(2,1)S(1)}, u32[]{:S(2)}) copy-start(bf16[120,1152]{1,0:T(8,128)(2,1)S(1)} %collective-permute-done.4.refs_4_) | copy-start | bytes 829444
  78.7 9.3 %copy-start.6 = (bf16[144,1152]{1,0:T(8,128)(2,1)}, bf16[144,1152]{1,0:T(8,128)(2,1)S(1)}, u32[]{:S(2)}) copy-start(bf16[144,1152]{1,0:T(8,128)(2,1)S(1)} %collective-permute-done.3.refs_3_) | copy-start | bytes 995332
  79.8 8.2 %collective-permute-start.5 = (bf16[360,1152]{1,0:T(8,128)(2,1)}, bf16[360,1152]{1,0:T(8,128)(2,1)}, u32[]{:S(2)}, u32[]{:S(2)}) collective-permute-start(bf16[360,1152]{1,0:T(8,128)(2,1)} %pad_maximum_fusion.1), channel_id=1, source_target_pairs={{0,8},{8,0},{1,9},{9,1},{2,10},{10,2},{3,11},{11,3},{4,12},{12,4},... | collective-permute-start | bytes 2488328 | tf_op jit(solution)/shard_map/ppermute | solution.py:29
  88.0 0.9 copy-start.3
  95.1 22.2 %all-to-all-start.2 = ((bf16[16,24,1152]{2,1,0:T(8,128)(2,1)}), bf16[16,24,1152]{2,1,0:T(8,128)(2,1)S(1)}, u32[]{:S(2)}, u32[]{:S(2)}) async-start(bf16[16,24,1152]{2,1,0:T(8,128)(2,1)} %bitcast.30), calls=%async_computation.2 | async-start | bytes 1769472 | tf_op jit(solution)/shard_map/all_to_all | solution.py:24
  100.6 22.1 %collective-permute-start.6 = (bf16[360,1152]{1,0:T(8,128)(2,1)}, bf16[360,1152]{1,0:T(8,128)(2,1)S(1)}, u32[]{:S(2)}, u32[]{:S(2)}) collective-permute-start(bf16[360,1152]{1,0:T(8,128)(2,1)} %get-tuple-element.16), channel_id=1, source_target_pairs={{0,8},{8,0},{1,9},{9,1},{2,10},{10,2},{3,11},{11,3},{4,12},{12,4},... | collective-permute-start | bytes 2488328 | tf_op jit(solution)/shard_map/ppermute | solution.py:29
  118.4 13.7 %copy-start.1 = (bf16[1152,538]{0,1:T(8,128)(2,1)S(1)}, bf16[1152,538]{0,1:T(8,128)(2,1)}, u32[]{:S(2)}) copy-start(bf16[1152,538]{0,1:T(8,128)(2,1)} %param.11) | copy-start | bytes 3718660
  118.4 13.7 %copy-start.17 = (f32[1152]{0:T(1024)S(1)}, f32[1152]{0:T(1024)}, u32[]{:S(2)}) copy-start(f32[1152]{0:T(1024)} %param.10) | copy-start | bytes 13828
  118.4 34.0 %all-to-all-start.3 = ((bf16[8,24,1152]{2,1,0:T(8,128)(2,1)}), bf16[8,24,1152]{2,1,0:T(8,128)(2,1)}, u32[]{:S(2)}, u32[]{:S(2)}) async-start(bf16[8,24,1152]{2,1,0:T(8,128)(2,1)} %broadcast_in_dim.7), calls=%async_computation.3 | async-start | bytes 884736 | tf_op jit(solution)/shard_map/all_to_all | solution.py:24
  122.7 0.9 copy-start.4
  126.2 15.8 %collective-permute-start.7 = (bf16[144,1152]{1,0:T(8,128)(2,1)}, bf16[144,1152]{1,0:T(8,128)(2,1)S(1)}, u32[]{:S(2)}, u32[]{:S(2)}) collective-permute-start(bf16[144,1152]{1,0:T(8,128)(2,1)} %get-tuple-element.17), channel_id=1, source_target_pairs={{0,480},{8,40},{32,0},{40,72},{64,32},{72,104},{96,64},{104,136},{... | collective-permute-start | bytes 995336 | tf_op jit(solution)/shard_map/ppermute | solution.py:44
  129.5 12.5 %collective-permute-start.8 = (bf16[120,1152]{1,0:T(8,128)(2,1)}, bf16[120,1152]{1,0:T(8,128)(2,1)S(1)}, u32[]{:S(2)}, u32[]{:S(2)}) collective-permute-start(bf16[120,1152]{1,0:T(8,128)(2,1)} %get-tuple-element.18), channel_id=1, source_target_pairs={{0,448},{8,72},{32,480},{40,104},{64,0},{72,136},{96,32},{104,168}... | collective-permute-start | bytes 829448 | tf_op jit(solution)/shard_map/ppermute | solution.py:44
  142.0 0.7 copy-start.13
  142.7 0.7 copy-start.12
  146.1 14.9 %collective-permute-start.10 = (bf16[48,1152]{1,0:T(8,128)(2,1)}, bf16[48,1152]{1,0:T(8,128)(2,1)S(1)}, u32[]{:S(2)}, u32[]{:S(2)}) collective-permute-start(bf16[48,1152]{1,0:T(8,128)(2,1)} %get-tuple-element.21), channel_id=1, source_target_pairs={{0,320},{8,200},{32,352},{40,232},{64,384},{72,264},{96,416},{104,... | collective-permute-start | bytes 331784 | tf_op jit(solution)/shard_map/ppermute | solution.py:44
  148.5 17.3 %collective-permute-start.9 = (bf16[48,1152]{1,0:T(8,128)(2,1)}, bf16[48,1152]{1,0:T(8,128)(2,1)S(1)}, u32[]{:S(2)}, u32[]{:S(2)}) collective-permute-start(bf16[48,1152]{1,0:T(8,128)(2,1)} %get-tuple-element.20), channel_id=1, source_target_pairs={{0,416},{8,104},{32,448},{40,136},{64,480},{72,168},{96,0},{104,20... | collective-permute-start | bytes 331784 | tf_op jit(solution)/shard_map/ppermute | solution.py:44
  161.0 4.8 %copy-start.14 = (bf16[48,1152]{1,0:T(8,128)(2,1)}, bf16[48,1152]{1,0:T(8,128)(2,1)S(1)}, u32[]{:S(2)}) copy-start(bf16[48,1152]{1,0:T(8,128)(2,1)S(1)} %collective-permute-done.10.six_ref) | copy-start | bytes 331780
  165.8 0.6 copy-start.15
  168.2 3.6 %collective-permute-start.11 = (bf16[24,1152]{1,0:T(8,128)(2,1)}, bf16[24,1152]{1,0:T(8,128)(2,1)S(1)}, u32[]{:S(2)}, u32[]{:S(2)}) collective-permute-start(bf16[24,1152]{1,0:T(8,128)(2,1)} %get-tuple-element.23), channel_id=1, source_target_pairs={{0,8},{8,0},{1,9},{9,1},{2,10},{10,2},{3,11},{11,3},{4,12},{12,4},... | collective-permute-start | bytes 165896 | tf_op jit(solution)/shard_map/ppermute | solution.py:29
  174.5 10.1 %copy-start.5 = (bf16[192,1152]{1,0:T(8,128)(2,1)S(1)}, bf16[192,1152]{1,0:T(8,128)(2,1)}, u32[]{:S(2)}) copy-start(bf16[192,1152]{1,0:T(8,128)(2,1)} %param.8) | copy-start | bytes 1327108
  176.7 22.5 %all-to-all-start.4 = ((bf16[8,448,128]{2,1,0:T(8,128)(2,1)}), bf16[8,448,128]{2,1,0:T(8,128)(2,1)S(1)}, u32[]{:S(2)}, u32[]{:S(2)}) async-start(bf16[8,448,128]{2,1,0:T(8,128)(2,1)} %shard_map.99), calls=%async_computation.4 | async-start | bytes 1835008 | tf_op jit(solution)/shard_map/all_to_all | solution.py:24
  199.2 0.9 copy-start.2

commit v6 on v5

--- a/solution.py
+++ b/solution.py
@@ -85,7 +85,7 @@
         weights_ref[first : first + step, :] = weights.astype(BF16)
     middle = kept_ref.shape[0]
     sent_ref[...] = dot(weights_ref[middle:, :], images_ref[...], ((1,), (0,))).astype(BF16)
-    kept_ref[...] = dot(weights_ref[:middle, :], images_ref[...], ((1,), (0,)))
+    kept_ref[...] = dot(weights_ref[:middle, :], images_ref[...], ((1,), (0,))).astype(BF16)
     image_ref[...] = dot(weights_ref[...], texts_ref[...], ((0,), (0,))).astype(BF16)
 
 
@@ -93,10 +93,11 @@
     long = one_ref.shape[0]
     pair = long // 3
     one_ref[...] = (
-        kept_ref[3 * pair : 6 * pair, :] + swapped_ref[2 * pair : 5 * pair, :].astype(F32)
+        kept_ref[3 * pair : 6 * pair, :].astype(F32)
+        + swapped_ref[2 * pair : 5 * pair, :].astype(F32)
     ).astype(BF16)
     two_ref[...] = (
-        kept_ref[6 * pair :, :] + swapped_ref[5 * pair :, :].astype(F32)
+        kept_ref[6 * pair :, :].astype(F32) + swapped_ref[5 * pair :, :].astype(F32)
     ).astype(BF16)
 
 
@@ -104,16 +105,18 @@
     pair = here_ref.shape[0]
     share = pair // 2
     here_ref[...] = (
-        kept_ref[:pair, :] + one_ref[:pair, :].astype(F32) + two_ref[:pair, :].astype(F32)
+        kept_ref[:pair, :].astype(F32)
+        + one_ref[:pair, :].astype(F32)
+        + two_ref[:pair, :].astype(F32)
     )
     three_ref[...] = (
-        kept_ref[pair : 2 * pair, :]
+        kept_ref[pair : 2 * pair, :].astype(F32)
         + swapped_ref[:pair, :].astype(F32)
         + one_ref[pair : 2 * pair, :].astype(F32)
         + two_ref[pair : 2 * pair, :].astype(F32)
     ).astype(BF16)
     sixth = (
-        kept_ref[2 * pair : 3 * pair, :]
+        kept_ref[2 * pair : 3 * pair, :].astype(F32)
         + swapped_ref[pair : 2 * pair, :].astype(F32)
         + one_ref[2 * pair :, :].astype(F32)
     )
@@ -271,7 +274,7 @@
         in_specs=[scalars, scalars] + [whole] * 7,
         out_shape=(
             shape(sent_rows, width, BF16),
-            shape(kept_rows, width, F32),
+            shape(kept_rows, width, BF16),
             shape(images.shape[0], width, BF16),
         ),
         scratch_shapes=[

time: 204 us -> 203 us (level)
    unnamed x40 -> x42, local copies, waits for them, and re-layouts: 6.03 us -> 6.15 us
  transfers between devices with their start and end apart: 17 -> 17, of which waited for: 11 -> 11; matrix products, arithmetic and copies ran while one was open for 6% -> 6% of each run, Pallas kernels for 3% -> 2%
where the time goes in v6:
time: 203 us; the launch traced here: 202 us
  waiting for transfers between devices  88.2 us (43%)
  starting transfers between devices  64.4 us (32%)
  Pallas kernels  17.3 us (9%)
  local copies, waits for them, and re-layouts  11.2 us (6%)
  other arithmetic  9.65 us (5%)
  matrix products  8.6 us (4%)
  between operations  2.27 us (1%)
    all_to_all x5, waiting for transfers between devices, swap(): return lax.all_to_all(array, axes, 0, 0, tiled=True)  44.8 us
    ppermute x8, waiting for transfers between devices, along(): return lax.ppermute(array, LINE, moves)  42.1 us
    ppermute x8, starting transfers between devices, along(): return lax.ppermute(array, LINE, moves)  28.5 us
    all_to_all x5, starting transfers between devices, swap(): return lax.all_to_all(array, axes, 0, 0, tiled=True)  28.1 us
    dot_general x7, matrix products, dot(): return lax.dot_general(a, b, (dims, ((), ())), preferred_element_type=F32)  8.6 us
    ppermute x4, starting transfers between devices, exchange(): return lax.ppermute(array, axes, [(i, i ^ k) for i in range(n)])  7.79 us
    unnamed x42, local copies, waits for them, and re-layouts  6.15 us
    pallas_call x1, Pallas kernels, per_device(): pl.pallas_call(functools.partial(pairs_kernel, share), in_specs=[scalars,...  6.14 us
  transfers between devices with their start and end apart: 17, of which 11 were waited for; matrix products, arithmetic and copies ran while one was open for 6% of the time, Pallas kernels for 2%

profile of v6, /device:TPU:32, one launch (start us, length us, event | category | flops | bytes accessed | tf_op | source)
XLA Modules:
  0.0 201.7 jit_solution(6940717939013372575)
XLA Ops:
  0.6 1.3 convert_reduce_fusion.2
  1.9 1.3 fusion.3
  3.2 2.1 %fusion.16 = f32[192,538]{1,0:T(8,128)S(1)} fusion(bf16[1152,538]{0,1:T(8,128)(2,1)} %param.11, bf16[192,1152]{1,0:T(8,128)(2,1)} %param.8, f32[1152]{0:T(1024)} %param.10, f32[192]{0:T(256)S(1)} %add_rsqrt_fusion, f32[192]{0:T(256)S(1)} %broadcast_multiply_fusion), kind=kOutput, calls=%fused_computation.33 | convolution fusion | flops 239099904 | bytes 2101248 | tf_op jit(solution)/shard_map/dot_general | solution.py:230
  5.3 0.8 copy-done.20
  6.2 0.6 convolution_convert_fusion.1
  6.7 0.4 copy-done.7
  7.1 0.3 convolution_convert_fusion.2
  7.5 1.0 pad_maximum_fusion
  8.5 6.9 %all-to-all-start = ((bf16[8,48,1152]{2,1,0:T(8,128)(2,1)}), bf16[8,48,1152]{2,1,0:T(8,128)(2,1)S(1)}, u32[]{:S(2)}, u32[]{:S(2)}) async-start(bf16[8,48,1152]{2,1,0:T(8,128)(2,1)} %pad_maximum_fusion), calls=%async_computation | async-start | bytes 1769472 | tf_op jit(solution)/shard_map/all_to_all | solution.py:24
  15.4 14.2 %all-to-all-done = bf16[8,48,1152]{2,1,0:T(8,128)(2,1)S(1)} async-done(((bf16[8,48,1152]{2,1,0:T(8,128)(2,1)}), bf16[8,48,1152]{2,1,0:T(8,128)(2,1)S(1)}, u32[]{:S(2)}, u32[]{:S(2)}) %all-to-all-start) | async-done | bytes 884768 | tf_op jit(solution)/shard_map/all_to_all | solution.py:24
  29.7 1.0 multiply_reduce_fusion.2
  30.6 0.9 multiply_convert_fusion.2
  31.6 1.9 collective-permute-start
  33.5 1.2 collective-permute-done
  34.7 7.7 %collective-permute-start.1 = (bf16[48,1152]{1,0:T(8,128)(2,1)S(1)}, bf16[48,1152]{1,0:T(8,128)(2,1)S(1)}, u32[]{:S(2)}, u32[]{:S(2)}) collective-permute-start(bf16[48,1152]{1,0:T(8,128)(2,1)S(1)} %pad_maximum_fusion.3.refs_0_), channel_id=1, source_target_pairs={{0,96},{8,424},{32,128},{40,456},{64,160},{72,488},{96,192},{104,8... | collective-permute-start | bytes 331784 | tf_op jit(solution)/shard_map/ppermute | solution.py:44
  42.5 7.6 %collective-permute-done.1.refs_1_ = bf16[48,1152]{1,0:T(8,128)(2,1)S(1)} collective-permute-done((bf16[48,1152]{1,0:T(8,128)(2,1)S(1)}, bf16[48,1152]{1,0:T(8,128)(2,1)S(1)}, u32[]{:S(2)}, u32[]{:S(2)}) %collective-permute-start.1) | collective-permute-done | bytes 110624 | tf_op jit(solution)/shard_map/ppermute | solution.py:44
  50.1 2.1 %collective-permute-start.2 = (bf16[48,1152]{1,0:T(8,128)(2,1)S(1)}, bf16[48,1152]{1,0:T(8,128)(2,1)S(1)}, u32[]{:S(2)}, u32[]{:S(2)}) collective-permute-start(bf16[48,1152]{1,0:T(8,128)(2,1)S(1)} %collective-permute-done.1.refs_1_), channel_id=1, source_target_pairs={{0,96},{8,424},{32,128},{40,456},{64,160},{72,488},{96,192},{104,8... | collective-permute-start | bytes 331784 | tf_op jit(solution)/shard_map/ppermute | solution.py:44
  52.2 7.6 %collective-permute-done.2.refs_2_ = bf16[48,1152]{1,0:T(8,128)(2,1)S(1)} collective-permute-done((bf16[48,1152]{1,0:T(8,128)(2,1)S(1)}, bf16[48,1152]{1,0:T(8,128)(2,1)S(1)}, u32[]{:S(2)}, u32[]{:S(2)}) %collective-permute-start.2) | collective-permute-done | bytes 110624 | tf_op jit(solution)/shard_map/ppermute | solution.py:44
  59.9 4.6 %collective-permute-start.3 = (bf16[144,1152]{1,0:T(8,128)(2,1)S(1)}, bf16[144,1152]{1,0:T(8,128)(2,1)S(1)}, u32[]{:S(2)}, u32[]{:S(2)}) collective-permute-start(bf16[144,1152]{1,0:T(8,128)(2,1)S(1)} %pad_maximum_fusion.2), channel_id=1, source_target_pairs={{0,32},{8,488},{32,64},{40,8},{64,96},{72,40},{96,128},{104,72},{1... | collective-permute-start | bytes 995336 | tf_op jit(solution)/shard_map/ppermute | solution.py:44
  64.4 0.7 slice.14
  65.2 1.9 collective-permute-start.4
  67.1 1.0 broadcast_in_dim.6
  68.1 4.2 %all-to-all-start.1 = ((bf16[16,24,1152]{2,1,0:T(8,128)(2,1)}), bf16[16,24,1152]{2,1,0:T(8,128)(2,1)S(1)}, u32[]{:S(2)}, u32[]{:S(2)}) async-start(bf16[16,24,1152]{2,1,0:T(8,128)(2,1)} %broadcast_in_dim.6), calls=%async_computation.1 | async-start | bytes 1769472 | tf_op jit(solution)/shard_map/all_to_all | solution.py:24
  72.3 6.5 %collective-permute-done.4.refs_4_ = bf16[120,1152]{1,0:T(8,128)(2,1)S(1)} collective-permute-done((bf16[120,1152]{1,0:T(8,128)(2,1)}, bf16[120,1152]{1,0:T(8,128)(2,1)S(1)}, u32[]{:S(2)}, u32[]{:S(2)}) %collective-permute-start.4) | collective-permute-done | bytes 276512 | tf_op jit(solution)/shard_map/ppermute | solution.py:44
  78.8 1.0 pad_maximum_fusion.1
  79.9 1.9 collective-permute-start.5
  83.1 0.6 pad_maximum_fusion.5.consts_ref
  83.7 4.4 %all-to-all-done.1 = bf16[16,24,1152]{2,1,0:T(8,128)(2,1)S(1)} async-done(((bf16[16,24,1152]{2,1,0:T(8,128)(2,1)}), bf16[16,24,1152]{2,1,0:T(8,128)(2,1)S(1)}, u32[]{:S(2)}, u32[]{:S(2)}) %all-to-all-start.1) | async-done | bytes 884768 | tf_op jit(solution)/shard_map/all_to_all | solution.py:24
  88.1 0.9 copy-done.3
  89.0 6.1 %shard_map.95 = (bf16[360,1152]{1,0:T(8,128)(2,1)}, bf16[408,1152]{1,0:T(8,128)(2,1)}, bf16[384,1152]{1,0:T(8,128)(2,1)}) custom-call(f32[2]{0:T(128)} %pad_maximum_fusion.5.consts_ref, s32[1]{0:T(128)} %bitcast.4.start_ref, bf16[48,1152]{1,0:T(8,128)(2,1)} %copy-done.12, bf16[48,1152]{1,0:T(8,128)(2,1)} %copy-done.9, bf16[48,1152]{1,0:T(8,128)(2,1)} %copy-done.10, ...), custom_call_target="tpu_custom_call" | custom-call | tf_op jit(solution)/shard_map/pallas_call | solution.py:272
  95.1 5.6 %all-to-all-start.2 = ((bf16[16,24,1152]{2,1,0:T(8,128)(2,1)}), bf16[16,24,1152]{2,1,0:T(8,128)(2,1)S(1)}, u32[]{:S(2)}, u32[]{:S(2)}) async-start(bf16[16,24,1152]{2,1,0:T(8,128)(2,1)} %bitcast.30), calls=%async_computation.2 | async-start | bytes 1769472 | tf_op jit(solution)/shard_map/all_to_all | solution.py:24
  100.7 1.9 collective-permute-start.6
  102.6 14.7 %all-to-all-done.2 = bf16[16,24,1152]{2,1,0:T(8,128)(2,1)S(1)} async-done(((bf16[16,24,1152]{2,1,0:T(8,128)(2,1)}), bf16[16,24,1152]{2,1,0:T(8,128)(2,1)S(1)}, u32[]{:S(2)}, u32[]{:S(2)}) %all-to-all-start.2) | async-done | bytes 884768 | tf_op jit(solution)/shard_map/all_to_all | solution.py:24
  117.7 0.8 broadcast_in_dim.7
  118.5 4.3 %all-to-all-start.3 = ((bf16[8,24,1152]{2,1,0:T(8,128)(2,1)}), bf16[8,24,1152]{2,1,0:T(8,128)(2,1)}, u32[]{:S(2)}, u32[]{:S(2)}) async-start(bf16[8,24,1152]{2,1,0:T(8,128)(2,1)} %broadcast_in_dim.7), calls=%async_computation.3 | async-start | bytes 884736 | tf_op jit(solution)/shard_map/all_to_all | solution.py:24
  122.8 0.9 copy-done.4
  123.7 2.3 %shard_map.96 = (bf16[144,1152]{1,0:T(8,128)(2,1)}, bf16[120,1152]{1,0:T(8,128)(2,1)}) custom-call(bf16[408,1152]{1,0:T(8,128)(2,1)} %get-tuple-element.15.kept_ref, bf16[360,1152]{1,0:T(8,128)(2,1)} %copy-done.4), custom_call_target="tpu_custom_call" | custom-call | tf_op jit(solution)/shard_map/pallas_call | solution.py:138
  126.0 3.3 %collective-permute-start.7 = (bf16[144,1152]{1,0:T(8,128)(2,1)}, bf16[144,1152]{1,0:T(8,128)(2,1)S(1)}, u32[]{:S(2)}, u32[]{:S(2)}) collective-permute-start(bf16[144,1152]{1,0:T(8,128)(2,1)} %get-tuple-element.17), channel_id=1, source_target_pairs={{0,480},{8,40},{32,0},{40,72},{64,32},{72,104},{96,64},{104,136},{... | collective-permute-start | bytes 995336 | tf_op jit(solution)/shard_map/ppermute | solution.py:44
  129.4 2.6 %collective-permute-start.8 = (bf16[120,1152]{1,0:T(8,128)(2,1)}, bf16[120,1152]{1,0:T(8,128)(2,1)S(1)}, u32[]{:S(2)}, u32[]{:S(2)}) collective-permute-start(bf16[120,1152]{1,0:T(8,128)(2,1)} %get-tuple-element.18), channel_id=1, source_target_pairs={{0,448},{8,72},{32,480},{40,104},{64,0},{72,136},{96,32},{104,168}... | collective-permute-start | bytes 829448 | tf_op jit(solution)/shard_map/ppermute | solution.py:44
  132.3 9.6 %collective-permute-done.8.two_ref = bf16[120,1152]{1,0:T(8,128)(2,1)S(1)} collective-permute-done((bf16[120,1152]{1,0:T(8,128)(2,1)}, bf16[120,1152]{1,0:T(8,128)(2,1)S(1)}, u32[]{:S(2)}, u32[]{:S(2)}) %collective-permute-start.8) | collective-permute-done | bytes 276512 | tf_op jit(solution)/shard_map/ppermute | solution.py:44
  141.9 0.7 copy-done.14
  142.6 0.7 copy-done.13
  143.3 2.4 %shard_map.97 = (f32[48,1152]{1,0:T(8,128)}, bf16[48,1152]{1,0:T(8,128)(2,1)}, bf16[48,1152]{1,0:T(8,128)(2,1)}) custom-call(bf16[408,1152]{1,0:T(8,128)(2,1)} %get-tuple-element.15.kept_ref, bf16[360,1152]{1,0:T(8,128)(2,1)} %copy-done.4, bf16[144,1152]{1,0:T(8,128)(2,1)} %copy-done.13, bf16[120,1152]{1,0:T(8,128)(2,1)} %copy-done.14), custom_call_target="tpu_custom_call" | custom-call | tf_op jit(solution)/shard_map/pallas_call | solution.py:144
  145.7 2.4 %collective-permute-start.10 = (bf16[48,1152]{1,0:T(8,128)(2,1)}, bf16[48,1152]{1,0:T(8,128)(2,1)S(1)}, u32[]{:S(2)}, u32[]{:S(2)}) collective-permute-start(bf16[48,1152]{1,0:T(8,128)(2,1)} %get-tuple-element.21), channel_id=1, source_target_pairs={{0,320},{8,200},{32,352},{40,232},{64,384},{72,264},{96,416},{104,... | collective-permute-start | bytes 331784 | tf_op jit(solution)/shard_map/ppermute | solution.py:44
  148.1 3.9 %collective-permute-start.9 = (bf16[48,1152]{1,0:T(8,128)(2,1)}, bf16[48,1152]{1,0:T(8,128)(2,1)S(1)}, u32[]{:S(2)}, u32[]{:S(2)}) collective-permute-start(bf16[48,1152]{1,0:T(8,128)(2,1)} %get-tuple-element.20), channel_id=1, source_target_pairs={{0,416},{8,104},{32,448},{40,136},{64,480},{72,168},{96,0},{104,20... | collective-permute-start | bytes 331784 | tf_op jit(solution)/shard_map/ppermute | solution.py:44
  152.0 2.0 %fusion.7 = (f32[192]{0:T(256)S(1)}, f32[192]{0:T(256)S(1)}, bf16[192,538]{1,0:T(8,128)(2,1)S(1)}) fusion(f32[538]{0:T(1024)S(1)} %multiply_reduce_fusion, f32[192,538]{1,0:T(8,128)} %copy-done.20, bf16[192,1152]{1,0:T(8,128)(2,1)} %bitcast.7, bf16[538,1152]{1,0:T(8,128)(2,1)S(1)} %copy-done), kind=kOutput, calls=%fused_computation.23 | convolution fusion | flops 240576000 | bytes 2305384 | tf_op jit(solution)/shard_map/dot_general | solution.py:230
  154.0 0.5 convolution_convert_fusion
  154.6 6.0 %collective-permute-done.10.six_ref = bf16[48,1152]{1,0:T(8,128)(2,1)S(1)} collective-permute-done((bf16[48,1152]{1,0:T(8,128)(2,1)}, bf16[48,1152]{1,0:T(8,128)(2,1)S(1)}, u32[]{:S(2)}, u32[]{:S(2)}) %collective-permute-start.10) | collective-permute-done | bytes 110624 | tf_op jit(solution)/shard_map/ppermute | solution.py:44
  160.6 4.8 %collective-permute-done.9.three_ref = bf16[48,1152]{1,0:T(8,128)(2,1)S(1)} collective-permute-done((bf16[48,1152]{1,0:T(8,128)(2,1)}, bf16[48,1152]{1,0:T(8,128)(2,1)S(1)}, u32[]{:S(2)}, u32[]{:S(2)}) %collective-permute-start.9) | collective-permute-done | bytes 110624 | tf_op jit(solution)/shard_map/ppermute | solution.py:44
  165.4 0.6 copy-done.16
  166.1 1.7 shard_map.98
  167.8 2.0 %collective-permute-start.11 = (bf16[24,1152]{1,0:T(8,128)(2,1)}, bf16[24,1152]{1,0:T(8,128)(2,1)S(1)}, u32[]{:S(2)}, u32[]{:S(2)}) collective-permute-start(bf16[24,1152]{1,0:T(8,128)(2,1)} %get-tuple-element.23), channel_id=1, source_target_pairs={{0,8},{8,0},{1,9},{9,1},{2,10},{10,2},{3,11},{11,3},{4,12},{12,4},... | collective-permute-start | bytes 165896 | tf_op jit(solution)/shard_map/ppermute | solution.py:29
  169.9 1.1 copy.13
  171.0 0.6 pad.9.sums_ref
  171.6 1.0 fusion.31
  172.6 0.7 fusion.34.text_ref
  173.4 2.2 %shard_map.99 = bf16[8,448,128]{2,1,0:T(8,128)(2,1)} custom-call(bf16[1152,192]{1,0:T(8,128)(2,1)} %bitcast.28, bf16[16,128]{1,0:T(8,128)(2,1)} %pad.9.sums_ref, bf16[24,1152]{1,0:T(8,128)(2,1)} %fusion.34.text_ref), custom_call_target="tpu_custom_call" | custom-call | tf_op jit(solution)/shard_map/pallas_call | solution.py:309
  175.5 7.2 %all-to-all-start.4 = ((bf16[8,448,128]{2,1,0:T(8,128)(2,1)}), bf16[8,448,128]{2,1,0:T(8,128)(2,1)S(1)}, u32[]{:S(2)}, u32[]{:S(2)}) async-start(bf16[8,448,128]{2,1,0:T(8,128)(2,1)} %shard_map.99), calls=%async_computation.4 | async-start | bytes 1835008 | tf_op jit(solution)/shard_map/all_to_all | solution.py:24
  182.8 0.8 copy.14.gain_ref
  183.6 1.0 fusion.centred_ref
  184.6 2.0 fusion.6.direct_ref
  186.6 11.5 %all-to-all-done.4.packed_ref = bf16[8,448,128]{2,1,0:T(8,128)(2,1)S(1)} async-done(((bf16[8,448,128]{2,1,0:T(8,128)(2,1)}), bf16[8,448,128]{2,1,0:T(8,128)(2,1)S(1)}, u32[]{:S(2)}, u32[]{:S(2)}) %all-to-all-start.4) | async-done | bytes 917536 | tf_op jit(solution)/shard_map/all_to_all | solution.py:24
  198.1 0.9 copy-done.2
  199.1 2.6 %shard_map.100 = (f32[144,192]{1,0:T(8,128)}, f32[144,192]{1,0:T(8,128)}, bf16[192,1152]{1,0:T(8,128)(2,1)}) custom-call(bf16[8,448,128]{2,1,0:T(8,128)(2,1)} %copy-done.2, f32[144,192]{1,0:T(8,128)} %fusion.6.direct_ref, f32[144,192]{1,0:T(8,128)} %fusion.centred_ref, f32[1,192]{1,0:T(1,128)} %bitcast.33, f32[144,1]{1,0:T(8,128)} %copy.14.gain_ref, ...), custom_call_target="tpu_custom_call" | custom-call | tf_op jit(solution)/shard_map/pallas_call | solution.py:320
  (55 shorter events, 1.1 us)
Async XLA Ops:
  0.6 5.5 %copy-start = (bf16[538,1152]{1,0:T(8,128)(2,1)S(1)}, bf16[538,1152]{1,0:T(8,128)(2,1)}, u32[]{:S(2)}) copy-start(bf16[538,1152]{1,0:T(8,128)(2,1)} %param.12) | copy-start | bytes 3718660
  3.2 180.4 %copy-start.19 = (f32[192]{0:T(256)}, f32[192]{0:T(256)S(1)}, u32[]{:S(2)}) copy-start(f32[192]{0:T(256)S(1)} %add_rsqrt_fusion) | copy-start | bytes 2308
  5.3 0.8 copy-start.20
  6.1 1.0 copy-start.7
  6.1 1.0 copy-start.17
  8.5 21.1 %all-to-all-start = ((bf16[8,48,1152]{2,1,0:T(8,128)(2,1)}), bf16[8,48,1152]{2,1,0:T(8,128)(2,1)S(1)}, u32[]{:S(2)}, u32[]{:S(2)}) async-start(bf16[8,48,1152]{2,1,0:T(8,128)(2,1)} %pad_maximum_fusion), calls=%async_computation | async-start | bytes 1769472 | tf_op jit(solution)/shard_map/all_to_all | solution.py:24
  31.6 3.1 %collective-permute-start = (bf16[24,1152]{1,0:T(8,128)(2,1)S(1)}, bf16[24,1152]{1,0:T(8,128)(2,1)S(1)}, u32[]{:S(2)}, u32[]{:S(2)}) collective-permute-start(bf16[24,1152]{1,0:T(8,128)(2,1)S(1)} %get-tuple-element.32), channel_id=1, source_target_pairs={{0,8},{8,0},{1,9},{9,1},{2,10},{10,2},{3,11},{11,3},{4,12},{12,4},... | collective-permute-start | bytes 165896 | tf_op jit(solution)/shard_map/ppermute | solution.py:29
  34.7 7.8 %copy-start.12 = (bf16[48,1152]{1,0:T(8,128)(2,1)}, bf16[48,1152]{1,0:T(8,128)(2,1)S(1)}, u32[]{:S(2)}) copy-start(bf16[48,1152]{1,0:T(8,128)(2,1)S(1)} %pad_maximum_fusion.3.refs_0_) | copy-start | bytes 331780
  34.7 15.4 %collective-permute-start.1 = (bf16[48,1152]{1,0:T(8,128)(2,1)S(1)}, bf16[48,1152]{1,0:T(8,128)(2,1)S(1)}, u32[]{:S(2)}, u32[]{:S(2)}) collective-permute-start(bf16[48,1152]{1,0:T(8,128)(2,1)S(1)} %pad_maximum_fusion.3.refs_0_), channel_id=1, source_target_pairs={{0,96},{8,424},{32,128},{40,456},{64,160},{72,488},{96,192},{104,8... | collective-permute-start | bytes 331784 | tf_op jit(solution)/shard_map/ppermute | solution.py:44
  50.1 28.7 %copy-start.9 = (bf16[48,1152]{1,0:T(8,128)(2,1)}, bf16[48,1152]{1,0:T(8,128)(2,1)S(1)}, u32[]{:S(2)}) copy-start(bf16[48,1152]{1,0:T(8,128)(2,1)S(1)} %collective-permute-done.1.refs_1_) | copy-start | bytes 331780
  50.1 9.7 %collective-permute-start.2 = (bf16[48,1152]{1,0:T(8,128)(2,1)S(1)}, bf16[48,1152]{1,0:T(8,128)(2,1)S(1)}, u32[]{:S(2)}, u32[]{:S(2)}) collective-permute-start(bf16[48,1152]{1,0:T(8,128)(2,1)S(1)} %collective-permute-done.1.refs_1_), channel_id=1, source_target_pairs={{0,96},{8,424},{32,128},{40,456},{64,160},{72,488},{96,192},{104,8... | collective-permute-start | bytes 331784 | tf_op jit(solution)/shard_map/ppermute | solution.py:44
  59.8 19.0 %copy-start.10 = (bf16[48,1152]{1,0:T(8,128)(2,1)}, bf16[48,1152]{1,0:T(8,128)(2,1)S(1)}, u32[]{:S(2)}) copy-start(bf16[48,1152]{1,0:T(8,128)(2,1)S(1)} %collective-permute-done.2.refs_2_) | copy-start | bytes 331780
  59.9 18.9 %collective-permute-start.3 = (bf16[144,1152]{1,0:T(8,128)(2,1)S(1)}, bf16[144,1152]{1,0:T(8,128)(2,1)S(1)}, u32[]{:S(2)}, u32[]{:S(2)}) collective-permute-start(bf16[144,1152]{1,0:T(8,128)(2,1)S(1)} %pad_maximum_fusion.2), channel_id=1, source_target_pairs={{0,32},{8,488},{32,64},{40,8},{64,96},{72,40},{96,128},{104,72},{1... | collective-permute-start | bytes 995336 | tf_op jit(solution)/shard_map/ppermute | solution.py:44
  65.2 13.6 %collective-permute-start.4 = (bf16[120,1152]{1,0:T(8,128)(2,1)}, bf16[120,1152]{1,0:T(8,128)(2,1)S(1)}, u32[]{:S(2)}, u32[]{:S(2)}) collective-permute-start(bf16[120,1152]{1,0:T(8,128)(2,1)} %slice.14), channel_id=1, source_target_pairs={{0,64},{8,456},{32,96},{40,488},{64,128},{72,8},{96,160},{104,40},... | collective-permute-start | bytes 829448 | tf_op jit(solution)/shard_map/ppermute | solution.py:44
  68.1 20.0 %all-to-all-start.1 = ((bf16[16,24,1152]{2,1,0:T(8,128)(2,1)}), bf16[16,24,1152]{2,1,0:T(8,128)(2,1)S(1)}, u32[]{:S(2)}, u32[]{:S(2)}) async-start(bf16[16,24,1152]{2,1,0:T(8,128)(2,1)} %broadcast_in_dim.6), calls=%async_computation.1 | async-start | bytes 1769472 | tf_op jit(solution)/shard_map/all_to_all | solution.py:24
  78.8 9.3 %copy-start.8 = (bf16[120,1152]{1,0:T(8,128)(2,1)}, bf16[120,1152]{1,0:T(8,128)(2,1)S(1)}, u32[]{:S(2)}) copy-start(bf16[120,1152]{1,0:T(8,128)(2,1)S(1)} %collective-permute-done.4.refs_4_) | copy-start | bytes 829444
  78.8 9.3 %copy-start.6 = (bf16[144,1152]{1,0:T(8,128)(2,1)}, bf16[144,1152]{1,0:T(8,128)(2,1)S(1)}, u32[]{:S(2)}) copy-start(bf16[144,1152]{1,0:T(8,128)(2,1)S(1)} %collective-permute-done.3.refs_3_) | copy-start | bytes 995332
  79.9 8.2 %collective-permute-start.5 = (bf16[360,1152]{1,0:T(8,128)(2,1)}, bf16[360,1152]{1,0:T(8,128)(2,1)}, u32[]{:S(2)}, u32[]{:S(2)}) collective-permute-start(bf16[360,1152]{1,0:T(8,128)(2,1)} %pad_maximum_fusion.1), channel_id=1, source_target_pairs={{0,8},{8,0},{1,9},{9,1},{2,10},{10,2},{3,11},{11,3},{4,12},{12,4},... | collective-permute-start | bytes 2488328 | tf_op jit(solution)/shard_map/ppermute | solution.py:29
  88.1 0.9 copy-start.3
  95.1 22.2 %all-to-all-start.2 = ((bf16[16,24,1152]{2,1,0:T(8,128)(2,1)}), bf16[16,24,1152]{2,1,0:T(8,128)(2,1)S(1)}, u32[]{:S(2)}, u32[]{:S(2)}) async-start(bf16[16,24,1152]{2,1,0:T(8,128)(2,1)} %bitcast.30), calls=%async_computation.2 | async-start | bytes 1769472 | tf_op jit(solution)/shard_map/all_to_all | solution.py:24
  100.7 22.1 %collective-permute-start.6 = (bf16[360,1152]{1,0:T(8,128)(2,1)}, bf16[360,1152]{1,0:T(8,128)(2,1)S(1)}, u32[]{:S(2)}, u32[]{:S(2)}) collective-permute-start(bf16[360,1152]{1,0:T(8,128)(2,1)} %get-tuple-element.16), channel_id=1, source_target_pairs={{0,8},{8,0},{1,9},{9,1},{2,10},{10,2},{3,11},{11,3},{4,12},{12,4},... | collective-permute-start | bytes 2488328 | tf_op jit(solution)/shard_map/ppermute | solution.py:29
  118.5 13.5 %copy-start.1 = (bf16[1152,538]{0,1:T(8,128)(2,1)S(1)}, bf16[1152,538]{0,1:T(8,128)(2,1)}, u32[]{:S(2)}) copy-start(bf16[1152,538]{0,1:T(8,128)(2,1)} %param.11) | copy-start | bytes 3718660
  118.5 13.5 %copy-start.18 = (f32[1152]{0:T(1024)S(1)}, f32[1152]{0:T(1024)}, u32[]{:S(2)}) copy-start(f32[1152]{0:T(1024)} %param.10) | copy-start | bytes 13828
  118.5 33.5 %all-to-all-start.3 = ((bf16[8,24,1152]{2,1,0:T(8,128)(2,1)}), bf16[8,24,1152]{2,1,0:T(8,128)(2,1)}, u32[]{:S(2)}, u32[]{:S(2)}) async-start(bf16[8,24,1152]{2,1,0:T(8,128)(2,1)} %broadcast_in_dim.7), calls=%async_computation.3 | async-start | bytes 884736 | tf_op jit(solution)/shard_map/all_to_all | solution.py:24
  122.8 0.9 copy-start.4
  126.0 15.8 %collective-permute-start.7 = (bf16[144,1152]{1,0:T(8,128)(2,1)}, bf16[144,1152]{1,0:T(8,128)(2,1)S(1)}, u32[]{:S(2)}, u32[]{:S(2)}) collective-permute-start(bf16[144,1152]{1,0:T(8,128)(2,1)} %get-tuple-element.17), channel_id=1, source_target_pairs={{0,480},{8,40},{32,0},{40,72},{64,32},{72,104},{96,64},{104,136},{... | collective-permute-start | bytes 995336 | tf_op jit(solution)/shard_map/ppermute | solution.py:44
  129.4 12.5 %collective-permute-start.8 = (bf16[120,1152]{1,0:T(8,128)(2,1)}, bf16[120,1152]{1,0:T(8,128)(2,1)S(1)}, u32[]{:S(2)}, u32[]{:S(2)}) collective-permute-start(bf16[120,1152]{1,0:T(8,128)(2,1)} %get-tuple-element.18), channel_id=1, source_target_pairs={{0,448},{8,72},{32,480},{40,104},{64,0},{72,136},{96,32},{104,168}... | collective-permute-start | bytes 829448 | tf_op jit(solution)/shard_map/ppermute | solution.py:44
  141.9 0.7 copy-start.14
  142.6 0.7 copy-start.13
  145.7 14.9 %collective-permute-start.10 = (bf16[48,1152]{1,0:T(8,128)(2,1)}, bf16[48,1152]{1,0:T(8,128)(2,1)S(1)}, u32[]{:S(2)}, u32[]{:S(2)}) collective-permute-start(bf16[48,1152]{1,0:T(8,128)(2,1)} %get-tuple-element.21), channel_id=1, source_target_pairs={{0,320},{8,200},{32,352},{40,232},{64,384},{72,264},{96,416},{104,... | collective-permute-start | bytes 331784 | tf_op jit(solution)/shard_map/ppermute | solution.py:44
  148.1 17.3 %collective-permute-start.9 = (bf16[48,1152]{1,0:T(8,128)(2,1)}, bf16[48,1152]{1,0:T(8,128)(2,1)S(1)}, u32[]{:S(2)}, u32[]{:S(2)}) collective-permute-start(bf16[48,1152]{1,0:T(8,128)(2,1)} %get-tuple-element.20), channel_id=1, source_target_pairs={{0,416},{8,104},{32,448},{40,136},{64,480},{72,168},{96,0},{104,20... | collective-permute-start | bytes 331784 | tf_op jit(solution)/shard_map/ppermute | solution.py:44
  160.6 4.8 %copy-start.15 = (bf16[48,1152]{1,0:T(8,128)(2,1)}, bf16[48,1152]{1,0:T(8,128)(2,1)S(1)}, u32[]{:S(2)}) copy-start(bf16[48,1152]{1,0:T(8,128)(2,1)S(1)} %collective-permute-done.10.six_ref) | copy-start | bytes 331780
  165.4 0.6 copy-start.16
  167.8 4.8 %copy-start.11 = (f32[24,1152]{1,0:T(8,128)S(1)}, f32[24,1152]{1,0:T(8,128)}, u32[]{:S(2)}) copy-start(f32[24,1152]{1,0:T(8,128)} %get-tuple-element.22) | copy-start | bytes 331780
  167.8 3.8 %collective-permute-start.11 = (bf16[24,1152]{1,0:T(8,128)(2,1)}, bf16[24,1152]{1,0:T(8,128)(2,1)S(1)}, u32[]{:S(2)}, u32[]{:S(2)}) collective-permute-start(bf16[24,1152]{1,0:T(8,128)(2,1)} %get-tuple-element.23), channel_id=1, source_target_pairs={{0,8},{8,0},{1,9},{9,1},{2,10},{10,2},{3,11},{11,3},{4,12},{12,4},... | collective-permute-start | bytes 165896 | tf_op jit(solution)/shard_map/ppermute | solution.py:29
  175.5 8.1 %copy-start.5 = (bf16[192,1152]{1,0:T(8,128)(2,1)S(1)}, bf16[192,1152]{1,0:T(8,128)(2,1)}, u32[]{:S(2)}) copy-start(bf16[192,1152]{1,0:T(8,128)(2,1)} %param.8) | copy-start | bytes 1327108
  175.5 22.6 %all-to-all-start.4 = ((bf16[8,448,128]{2,1,0:T(8,128)(2,1)}), bf16[8,448,128]{2,1,0:T(8,128)(2,1)S(1)}, u32[]{:S(2)}, u32[]{:S(2)}) async-start(bf16[8,448,128]{2,1,0:T(8,128)(2,1)} %shard_map.99), calls=%async_computation.4 | async-start | bytes 1835008 | tf_op jit(solution)/shard_map/all_to_all | solution.py:24
  198.1 0.9 copy-start.2

commit v7 on v6

--- a/solution.py
+++ b/solution.py
@@ -54,6 +54,19 @@
     last = [along(near, -NEAR[0]), along(near[:cut], -NEAR[1])]
     other = exchange(jnp.concatenate([*far, *last], axis=0), "c", 1)
     return [pair, *far, *last, other]
+
+
+LIMIT = pltpu.CompilerParams(vmem_limit_bytes=32 << 20)
+
+
+def near_core(array):
+    return pltpu.with_memory_space_constraint(array, pltpu.VMEM)
+
+
+def in_fast_memory(kernel, out_shape):
+    kept = jax.tree.map(lambda s: pltpu.VMEM(s.shape, s.dtype), out_shape)
+    run = pl.pallas_call(kernel, out_shape=kept, compiler_params=LIMIT)
+    return lambda *operands: run(*(near_core(x) for x in operands))
 
 
 def shape(rows, width, dtype):
@@ -135,20 +148,20 @@
 def summed_line(kept, swapped, share):
     width = kept.shape[1]
     pair = 2 * share
-    one, two = pl.pallas_call(
+    one, two = in_fast_memory(
         near_kernel,
-        out_shape=(shape(3 * pair, width, BF16), shape(2 * pair + share, width, BF16)),
+        (shape(3 * pair, width, BF16), shape(2 * pair + share, width, BF16)),
     )(kept, swapped)
     one = along(one, NEAR[0])
     two = along(two, NEAR[1])
-    here, three, six = pl.pallas_call(
+    here, three, six = in_fast_memory(
         far_kernel,
-        out_shape=(shape(pair, width, F32), shape(pair, width, BF16), shape(pair, width, BF16)),
+        (shape(pair, width, F32), shape(pair, width, BF16), shape(pair, width, BF16)),
     )(kept, swapped, one, two)
     three = along(three, FAR[0])
     six = along(six, FAR[1])
-    own, partner = pl.pallas_call(
-        last_kernel, out_shape=(shape(share, width, F32), shape(share, width, BF16))
+    own, partner = in_fast_memory(
+        last_kernel, (shape(share, width, F32), shape(share, width, BF16))
     )(here, three, six)
     partner = exchange(partner, "c", 1)
     return own + partner.astype(F32)
@@ -272,16 +285,18 @@
     text_sent, text_kept, image_add = pl.pallas_call(
         functools.partial(pairs_kernel, share),
         in_specs=[scalars, scalars] + [whole] * 7,
+        out_specs=(whole, whole, whole),
         out_shape=(
-            shape(sent_rows, width, BF16),
-            shape(kept_rows, width, BF16),
-            shape(images.shape[0], width, BF16),
+            pltpu.VMEM((sent_rows, width), BF16),
+            pltpu.VMEM((kept_rows, width), BF16),
+            pltpu.VMEM((images.shape[0], width), BF16),
         ),
+        compiler_params=LIMIT,
         scratch_shapes=[
             pltpu.VMEM((sent_rows + kept_rows, width), BF16),
             pltpu.VMEM((sent_rows + kept_rows, images.shape[0]), BF16),
         ],
-    )(consts, own_start, *pieces, images)
+    )(consts, own_start, *(near_core(x) for x in (*pieces, images)))
 
     image_parts = swap(image_add.reshape(-1, share, width), XY)
     image_dir = jnp.sum(image_parts.astype(F32), axis=0)
@@ -306,8 +321,8 @@
     sums_both = jnp.pad(sums_both, ((0, 0), (0, 2 * LANES - rows))).reshape(-1, LANES)
     sums_both = jnp.pad(sums_both, ((0, SUM_ROWS - sums_both.shape[0]), (0, 0)))
     length = cols + cols // 2 + SUM_ROWS + share * width // LANES
-    packed = pl.pallas_call(
-        pack_kernel, out_shape=jax.ShapeDtypeStruct((heads, length, LANES), BF16)
+    packed = in_fast_memory(
+        pack_kernel, jax.ShapeDtypeStruct((heads, length, LANES), BF16)
     )(back, sums_both, grad_text_share)
     arrived = swap(packed, MP)
     gain_here = lax.dynamic_slice_in_dim(gain, first_col, cols, 0)

time: 203 us -> 195 us (0.961)
  Pallas kernels: 17.3 us -> 9.26 us
    pallas_call x4, Pallas kernels: 8.64 us -> 2.04 us  [in_fast_memory(): return lambda *operands: run(*(near_core(x) for x in operands))]
    unnamed x42 -> x44, local copies, waits for them, and re-layouts: 6.15 us -> 7.39 us
  transfers between devices with their start and end apart: 17 -> 17, of which waited for: 11 -> 12; matrix products, arithmetic and copies ran while one was open for 6% -> 6% of each run, Pallas kernels for 2% -> 0%
where the time goes in v7:
time: 195 us; the launch traced here: 194 us
  waiting for transfers between devices  89.9 us (46%)
  starting transfers between devices  64.1 us (33%)
  local copies, waits for them, and re-layouts  11 us (6%)
  Pallas kernels  9.26 us (5%)
  other arithmetic  8.74 us (4%)
  matrix products  8.71 us (4%)
  between operations  2.33 us (1%)
    all_to_all x5, waiting for transfers between devices, swap(): return lax.all_to_all(array, axes, 0, 0, tiled=True)  45.4 us
    ppermute x8, waiting for transfers between devices, along(): return lax.ppermute(array, LINE, moves)  42.4 us
    all_to_all x5, starting transfers between devices, swap(): return lax.all_to_all(array, axes, 0, 0, tiled=True)  28.2 us
    ppermute x8, starting transfers between devices, along(): return lax.ppermute(array, LINE, moves)  27.8 us
    dot_general x7, matrix products, dot(): return lax.dot_general(a, b, (dims, ((), ())), preferred_element_type=F32)  8.71 us
    ppermute x4, starting transfers between devices, exchange(): return lax.ppermute(array, axes, [(i, i ^ k) for i in range(n)])  8.17 us
    unnamed x44, local copies, waits for them, and re-layouts  7.39 us
    pallas_call x1, Pallas kernels, per_device(): pl.pallas_call(functools.partial(pairs_kernel, share), in_specs=[scalars,...  4.64 us
  transfers between devices with their start and end apart: 17, of which 12 were waited for; matrix products, arithmetic and copies ran while one was open for 6% of the time, Pallas kernels for 0%

profile of v7, /device:TPU:32, one launch (start us, length us, event | category | flops | bytes accessed | tf_op | source)
XLA Modules:
  0.0 194.1 jit_solution(951021956727196214)
XLA Ops:
  0.6 1.3 convert_reduce_fusion.2
  1.9 1.3 fusion.3
  3.2 2.1 %fusion.16 = f32[192,538]{1,0:T(8,128)S(1)} fusion(bf16[1152,538]{0,1:T(8,128)(2,1)} %param.11, bf16[192,1152]{1,0:T(8,128)(2,1)} %param.8, f32[1152]{0:T(1024)} %param.10, f32[192]{0:T(256)S(1)} %add_rsqrt_fusion, f32[192]{0:T(256)S(1)} %broadcast_multiply_fusion), kind=kOutput, calls=%fused_computation.33 | convolution fusion | flops 239099904 | bytes 2101248 | tf_op jit(solution)/shard_map/dot_general | solution.py:243
  5.3 0.8 copy-done.21
  6.1 0.6 convolution_convert_fusion.1
  6.7 0.4 copy-done.15
  7.1 0.3 convolution_convert_fusion.2
  7.5 1.0 pad_maximum_fusion
  8.4 6.9 %all-to-all-start = ((bf16[8,48,1152]{2,1,0:T(8,128)(2,1)}), bf16[8,48,1152]{2,1,0:T(8,128)(2,1)S(1)}, u32[]{:S(2)}, u32[]{:S(2)}) async-start(bf16[8,48,1152]{2,1,0:T(8,128)(2,1)} %pad_maximum_fusion), calls=%async_computation | async-start | bytes 1769472 | tf_op jit(solution)/shard_map/all_to_all | solution.py:24
  15.4 14.2 %all-to-all-done = bf16[8,48,1152]{2,1,0:T(8,128)(2,1)S(1)} async-done(((bf16[8,48,1152]{2,1,0:T(8,128)(2,1)}), bf16[8,48,1152]{2,1,0:T(8,128)(2,1)S(1)}, u32[]{:S(2)}, u32[]{:S(2)}) %all-to-all-start) | async-done | bytes 884768 | tf_op jit(solution)/shard_map/all_to_all | solution.py:24
  29.7 1.0 multiply_reduce_fusion.2
  30.6 0.9 multiply_convert_fusion.2
  31.5 1.9 collective-permute-start
  33.5 1.2 collective-permute-done
  34.7 7.7 %collective-permute-start.1 = (bf16[48,1152]{1,0:T(8,128)(2,1)S(1)}, bf16[48,1152]{1,0:T(8,128)(2,1)S(1)}, u32[]{:S(2)}, u32[]{:S(2)}) collective-permute-start(bf16[48,1152]{1,0:T(8,128)(2,1)S(1)} %pad_maximum_fusion.3.refs_0_), channel_id=1, source_target_pairs={{0,96},{8,424},{32,128},{40,456},{64,160},{72,488},{96,192},{104,8... | collective-permute-start | bytes 331784 | tf_op jit(solution)/shard_map/ppermute | solution.py:44
  42.5 0.6 copy-done.6
  43.1 7.0 %collective-permute-done.1.refs_1_ = bf16[48,1152]{1,0:T(8,128)(2,1)S(1)} collective-permute-done((bf16[48,1152]{1,0:T(8,128)(2,1)S(1)}, bf16[48,1152]{1,0:T(8,128)(2,1)S(1)}, u32[]{:S(2)}, u32[]{:S(2)}) %collective-permute-start.1) | collective-permute-done | bytes 110624 | tf_op jit(solution)/shard_map/ppermute | solution.py:44
  50.1 2.1 %collective-permute-start.2 = (bf16[48,1152]{1,0:T(8,128)(2,1)S(1)}, bf16[48,1152]{1,0:T(8,128)(2,1)S(1)}, u32[]{:S(2)}, u32[]{:S(2)}) collective-permute-start(bf16[48,1152]{1,0:T(8,128)(2,1)S(1)} %collective-permute-done.1.refs_1_), channel_id=1, source_target_pairs={{0,96},{8,424},{32,128},{40,456},{64,160},{72,488},{96,192},{104,8... | collective-permute-start | bytes 331784 | tf_op jit(solution)/shard_map/ppermute | solution.py:44
  52.2 7.6 %collective-permute-done.2.refs_2_ = bf16[48,1152]{1,0:T(8,128)(2,1)S(1)} collective-permute-done((bf16[48,1152]{1,0:T(8,128)(2,1)S(1)}, bf16[48,1152]{1,0:T(8,128)(2,1)S(1)}, u32[]{:S(2)}, u32[]{:S(2)}) %collective-permute-start.2) | collective-permute-done | bytes 110624 | tf_op jit(solution)/shard_map/ppermute | solution.py:44
  59.8 4.6 %collective-permute-start.3 = (bf16[144,1152]{1,0:T(8,128)(2,1)S(1)}, bf16[144,1152]{1,0:T(8,128)(2,1)S(1)}, u32[]{:S(2)}, u32[]{:S(2)}) collective-permute-start(bf16[144,1152]{1,0:T(8,128)(2,1)S(1)} %pad_maximum_fusion.2), channel_id=1, source_target_pairs={{0,32},{8,488},{32,64},{40,8},{64,96},{72,40},{96,128},{104,72},{1... | collective-permute-start | bytes 995336 | tf_op jit(solution)/shard_map/ppermute | solution.py:44
  64.4 0.7 slice.14
  65.2 1.9 collective-permute-start.4
  67.1 1.0 broadcast_in_dim.6
  68.1 4.2 %all-to-all-start.1 = ((bf16[16,24,1152]{2,1,0:T(8,128)(2,1)}), bf16[16,24,1152]{2,1,0:T(8,128)(2,1)S(1)}, u32[]{:S(2)}, u32[]{:S(2)}) async-start(bf16[16,24,1152]{2,1,0:T(8,128)(2,1)} %broadcast_in_dim.6), calls=%async_computation.1 | async-start | bytes 1769472 | tf_op jit(solution)/shard_map/all_to_all | solution.py:24
  72.2 6.5 %collective-permute-done.4.refs_4_ = bf16[120,1152]{1,0:T(8,128)(2,1)S(1)} collective-permute-done((bf16[120,1152]{1,0:T(8,128)(2,1)}, bf16[120,1152]{1,0:T(8,128)(2,1)S(1)}, u32[]{:S(2)}, u32[]{:S(2)}) %collective-permute-start.4) | collective-permute-done | bytes 276512 | tf_op jit(solution)/shard_map/ppermute | solution.py:44
  78.8 1.0 pad_maximum_fusion.1
  79.8 1.9 collective-permute-start.5
  83.1 5.0 %all-to-all-done.1 = bf16[16,24,1152]{2,1,0:T(8,128)(2,1)S(1)} async-done(((bf16[16,24,1152]{2,1,0:T(8,128)(2,1)}), bf16[16,24,1152]{2,1,0:T(8,128)(2,1)S(1)}, u32[]{:S(2)}, u32[]{:S(2)}) %all-to-all-start.1) | async-done | bytes 884768 | tf_op jit(solution)/shard_map/all_to_all | solution.py:24
  88.1 1.0 copy-done.2
  89.0 0.9 copy-done.4
  89.9 0.9 copy-done.7
  90.8 4.6 %shard_map.95 = (bf16[360,1152]{1,0:T(8,128)(2,1)S(1)}, bf16[408,1152]{1,0:T(8,128)(2,1)S(1)}, bf16[384,1152]{1,0:T(8,128)(2,1)S(1)}) custom-call(f32[2]{0:T(128)S(1)} %pad_maximum_fusion.5.consts_ref, s32[1]{0:T(128)} %bitcast.4.start_ref, bf16[48,1152]{1,0:T(8,128)(2,1)S(1)} %copy-done.7, bf16[48,1152]{1,0:T(8,128)(2,1)S(1)} %collective-permute-done.1.refs_1_, ...), custom_call_target="tpu_custom_call" | custom-call | tf_op jit(solution)/shard_map/pallas_call | solution.py:285
  95.5 0.9 copy-done.5
  96.4 0.9 copy-done.8
  97.3 5.7 %all-to-all-start.2 = ((bf16[16,24,1152]{2,1,0:T(8,128)(2,1)}), bf16[16,24,1152]{2,1,0:T(8,128)(2,1)}, u32[]{:S(2)}, u32[]{:S(2)}) async-start(bf16[16,24,1152]{2,1,0:T(8,128)(2,1)} %bitcast.29), calls=%async_computation.2 | async-start | bytes 1769472 | tf_op jit(solution)/shard_map/all_to_all | solution.py:24
  103.0 2.4 %collective-permute-start.6 = (bf16[360,1152]{1,0:T(8,128)(2,1)}, bf16[360,1152]{1,0:T(8,128)(2,1)S(1)}, u32[]{:S(2)}, u32[]{:S(2)}) collective-permute-start(bf16[360,1152]{1,0:T(8,128)(2,1)} %copy-done.8), channel_id=1, source_target_pairs={{0,8},{8,0},{1,9},{9,1},{2,10},{10,2},{3,11},{11,3},{4,12},{12,4},... | collective-permute-start | bytes 2488328 | tf_op jit(solution)/shard_map/ppermute | solution.py:29
  105.4 15.3 %all-to-all-done.2 = bf16[16,24,1152]{2,1,0:T(8,128)(2,1)} async-done(((bf16[16,24,1152]{2,1,0:T(8,128)(2,1)}), bf16[16,24,1152]{2,1,0:T(8,128)(2,1)}, u32[]{:S(2)}, u32[]{:S(2)}) %all-to-all-start.2) | async-done | bytes 884768 | tf_op jit(solution)/shard_map/all_to_all | solution.py:24
  120.7 1.3 convert_reduce_fusion
  122.3 0.8 broadcast_in_dim.7
  123.1 4.3 %all-to-all-start.3 = ((bf16[8,24,1152]{2,1,0:T(8,128)(2,1)}), bf16[8,24,1152]{2,1,0:T(8,128)(2,1)}, u32[]{:S(2)}, u32[]{:S(2)}) async-start(bf16[8,24,1152]{2,1,0:T(8,128)(2,1)} %broadcast_in_dim.7), calls=%async_computation.3 | async-start | bytes 884736 | tf_op jit(solution)/shard_map/all_to_all | solution.py:24
  127.4 0.1 shard_map.96
  127.5 2.9 %collective-permute-start.7 = (bf16[144,1152]{1,0:T(8,128)(2,1)S(1)}, bf16[144,1152]{1,0:T(8,128)(2,1)S(1)}, u32[]{:S(2)}, u32[]{:S(2)}) collective-permute-start(bf16[144,1152]{1,0:T(8,128)(2,1)S(1)} %get-tuple-element.17), channel_id=1, source_target_pairs={{0,480},{8,40},{32,0},{40,72},{64,32},{72,104},{96,64},{104,136},{... | collective-permute-start | bytes 995336 | tf_op jit(solution)/shard_map/ppermute | solution.py:44
  130.4 2.2 %collective-permute-start.8 = (bf16[120,1152]{1,0:T(8,128)(2,1)S(1)}, bf16[120,1152]{1,0:T(8,128)(2,1)S(1)}, u32[]{:S(2)}, u32[]{:S(2)}) collective-permute-start(bf16[120,1152]{1,0:T(8,128)(2,1)S(1)} %get-tuple-element.18), channel_id=1, source_target_pairs={{0,448},{8,72},{32,480},{40,104},{64,0},{72,136},{96,32},{104,168}... | collective-permute-start | bytes 829448 | tf_op jit(solution)/shard_map/ppermute | solution.py:44
  132.6 0.3 multiply_reduce_fusion
  133.0 9.8 %collective-permute-done.8.two_ref = bf16[120,1152]{1,0:T(8,128)(2,1)S(1)} collective-permute-done((bf16[120,1152]{1,0:T(8,128)(2,1)S(1)}, bf16[120,1152]{1,0:T(8,128)(2,1)S(1)}, u32[]{:S(2)}, u32[]{:S(2)}) %collective-permute-start.8) | collective-permute-done | bytes 276512 | tf_op jit(solution)/shard_map/ppermute | solution.py:44
  142.7 0.8 shard_map.97
  143.5 1.9 collective-permute-start.10
  145.4 4.4 %collective-permute-start.9 = (bf16[48,1152]{1,0:T(8,128)(2,1)}, bf16[48,1152]{1,0:T(8,128)(2,1)S(1)}, u32[]{:S(2)}, u32[]{:S(2)}) collective-permute-start(bf16[48,1152]{1,0:T(8,128)(2,1)} %get-tuple-element.20), channel_id=1, source_target_pairs={{0,416},{8,104},{32,448},{40,136},{64,480},{72,168},{96,0},{104,20... | collective-permute-start | bytes 331784 | tf_op jit(solution)/shard_map/ppermute | solution.py:44
  149.9 2.2 %fusion.7 = (f32[192]{0:T(256)S(1)}, f32[192]{0:T(256)S(1)}, bf16[192,538]{1,0:T(8,128)(2,1)S(1)}) fusion(f32[538]{0:T(1024)S(1)} %multiply_reduce_fusion, f32[192,538]{1,0:T(8,128)} %copy-done.21, bf16[192,1152]{1,0:T(8,128)(2,1)} %bitcast.7, bf16[538,1152]{1,0:T(8,128)(2,1)S(1)} %copy-done), kind=kOutput, calls=%fused_computation.23 | convolution fusion | flops 240576000 | bytes 2305384 | tf_op jit(solution)/shard_map/dot_general | solution.py:243
  152.1 0.5 convolution_convert_fusion
  152.7 6.2 %collective-permute-done.10.six_ref = bf16[48,1152]{1,0:T(8,128)(2,1)S(1)} collective-permute-done((bf16[48,1152]{1,0:T(8,128)(2,1)}, bf16[48,1152]{1,0:T(8,128)(2,1)S(1)}, u32[]{:S(2)}, u32[]{:S(2)}) %collective-permute-start.10) | collective-permute-done | bytes 110624 | tf_op jit(solution)/shard_map/ppermute | solution.py:44
  158.8 5.3 %collective-permute-done.9.three_ref = bf16[48,1152]{1,0:T(8,128)(2,1)S(1)} collective-permute-done((bf16[48,1152]{1,0:T(8,128)(2,1)}, bf16[48,1152]{1,0:T(8,128)(2,1)S(1)}, u32[]{:S(2)}, u32[]{:S(2)}) %collective-permute-start.9) | collective-permute-done | bytes 110624 | tf_op jit(solution)/shard_map/ppermute | solution.py:44
  164.2 1.9 collective-permute-start.11
  166.2 0.2 copy.13
  166.4 0.9 collective-permute-done.11
  167.3 0.1 fusion.31
  167.6 1.1 shard_map.99
  168.7 7.1 %all-to-all-start.4 = ((bf16[8,448,128]{2,1,0:T(8,128)(2,1)}), bf16[8,448,128]{2,1,0:T(8,128)(2,1)S(1)}, u32[]{:S(2)}, u32[]{:S(2)}) async-start(bf16[8,448,128]{2,1,0:T(8,128)(2,1)} %shard_map.99), calls=%async_computation.4 | async-start | bytes 1835008 | tf_op jit(solution)/shard_map/all_to_all | solution.py:24
  175.8 0.8 copy.14.gain_ref
  176.6 1.0 fusion.centred_ref
  177.6 2.0 %fusion.6.direct_ref = f32[144,192]{1,0:T(8,128)} fusion(bf16[192,1152]{1,0:T(8,128)(2,1)} %bitcast.7, s32[1152]{0:T(1024)S(1)} %iota_subtract_fusion), kind=kOutput, calls=%fused_computation.20 | convolution fusion | flops 63866880 | bytes 557568 | tf_op jit(solution)/shard_map/dot_general | solution.py:243
  179.6 11.0 %all-to-all-done.4.packed_ref = bf16[8,448,128]{2,1,0:T(8,128)(2,1)S(1)} async-done(((bf16[8,448,128]{2,1,0:T(8,128)(2,1)}), bf16[8,448,128]{2,1,0:T(8,128)(2,1)S(1)}, u32[]{:S(2)}, u32[]{:S(2)}) %all-to-all-start.4) | async-done | bytes 917536 | tf_op jit(solution)/shard_map/all_to_all | solution.py:24
  190.6 0.9 copy-done.11
  191.5 2.6 %shard_map.100 = (f32[144,192]{1,0:T(8,128)}, f32[144,192]{1,0:T(8,128)}, bf16[192,1152]{1,0:T(8,128)(2,1)}) custom-call(bf16[8,448,128]{2,1,0:T(8,128)(2,1)} %copy-done.11, f32[144,192]{1,0:T(8,128)} %fusion.6.direct_ref, f32[144,192]{1,0:T(8,128)} %fusion.centred_ref, f32[1,192]{1,0:T(1,128)} %bitcast.33, f32[144,1]{1,0:T(8,128)} %copy.14.gain_ref, ...), custom_call_target="tpu_custom_call" | custom-call | tf_op jit(solution)/shard_map/pallas_call | solution.py:335
  (57 shorter events, 0.8 us)
Async XLA Ops:
  0.6 5.5 %copy-start = (bf16[538,1152]{1,0:T(8,128)(2,1)S(1)}, bf16[538,1152]{1,0:T(8,128)(2,1)}, u32[]{:S(2)}) copy-start(bf16[538,1152]{1,0:T(8,128)(2,1)} %param.12) | copy-start | bytes 3718660
  3.2 173.4 %copy-start.20 = (f32[192]{0:T(256)}, f32[192]{0:T(256)S(1)}, u32[]{:S(2)}) copy-start(f32[192]{0:T(256)S(1)} %add_rsqrt_fusion) | copy-start | bytes 2308
  5.3 0.8 copy-start.21
  6.1 1.0 copy-start.15
  6.1 1.0 copy-start.18
  8.4 21.1 %all-to-all-start = ((bf16[8,48,1152]{2,1,0:T(8,128)(2,1)}), bf16[8,48,1152]{2,1,0:T(8,128)(2,1)S(1)}, u32[]{:S(2)}, u32[]{:S(2)}) async-start(bf16[8,48,1152]{2,1,0:T(8,128)(2,1)} %pad_maximum_fusion), calls=%async_computation | async-start | bytes 1769472 | tf_op jit(solution)/shard_map/all_to_all | solution.py:24
  31.5 28.3 %copy-start.13 = (bf16[24,1152]{1,0:T(8,128)(2,1)}, bf16[24,1152]{1,0:T(8,128)(2,1)S(1)}, u32[]{:S(2)}) copy-start(bf16[24,1152]{1,0:T(8,128)(2,1)S(1)} %get-tuple-element.32) | copy-start | bytes 165892
  31.5 35.5 %copy-start.16 = (bf16[24,1152]{1,0:T(8,128)(2,1)}, bf16[24,1152]{1,0:T(8,128)(2,1)S(1)}, u32[]{:S(2)}) copy-start(bf16[24,1152]{1,0:T(8,128)(2,1)S(1)} %get-tuple-element.31) | copy-start | bytes 165892
  31.5 3.1 %collective-permute-start = (bf16[24,1152]{1,0:T(8,128)(2,1)S(1)}, bf16[24,1152]{1,0:T(8,128)(2,1)S(1)}, u32[]{:S(2)}, u32[]{:S(2)}) collective-permute-start(bf16[24,1152]{1,0:T(8,128)(2,1)S(1)} %get-tuple-element.32), channel_id=1, source_target_pairs={{0,8},{8,0},{1,9},{9,1},{2,10},{10,2},{3,11},{11,3},{4,12},{12,4},... | collective-permute-start | bytes 165896 | tf_op jit(solution)/shard_map/ppermute | solution.py:29
  34.7 15.4 %collective-permute-start.1 = (bf16[48,1152]{1,0:T(8,128)(2,1)S(1)}, bf16[48,1152]{1,0:T(8,128)(2,1)S(1)}, u32[]{:S(2)}, u32[]{:S(2)}) collective-permute-start(bf16[48,1152]{1,0:T(8,128)(2,1)S(1)} %pad_maximum_fusion.3.refs_0_), channel_id=1, source_target_pairs={{0,96},{8,424},{32,128},{40,456},{64,160},{72,488},{96,192},{104,8... | collective-permute-start | bytes 331784 | tf_op jit(solution)/shard_map/ppermute | solution.py:44
  42.4 0.6 copy-start.6
  50.1 9.7 %collective-permute-start.2 = (bf16[48,1152]{1,0:T(8,128)(2,1)S(1)}, bf16[48,1152]{1,0:T(8,128)(2,1)S(1)}, u32[]{:S(2)}, u32[]{:S(2)}) collective-permute-start(bf16[48,1152]{1,0:T(8,128)(2,1)S(1)} %collective-permute-done.1.refs_1_), channel_id=1, source_target_pairs={{0,96},{8,424},{32,128},{40,456},{64,160},{72,488},{96,192},{104,8... | collective-permute-start | bytes 331784 | tf_op jit(solution)/shard_map/ppermute | solution.py:44
  59.8 19.0 %copy-start.3 = (bf16[48,1152]{1,0:T(8,128)(2,1)}, bf16[48,1152]{1,0:T(8,128)(2,1)S(1)}, u32[]{:S(2)}) copy-start(bf16[48,1152]{1,0:T(8,128)(2,1)S(1)} %collective-permute-done.2.refs_2_) | copy-start | bytes 331780
  59.8 18.9 %collective-permute-start.3 = (bf16[144,1152]{1,0:T(8,128)(2,1)S(1)}, bf16[144,1152]{1,0:T(8,128)(2,1)S(1)}, u32[]{:S(2)}, u32[]{:S(2)}) collective-permute-start(bf16[144,1152]{1,0:T(8,128)(2,1)S(1)} %pad_maximum_fusion.2), channel_id=1, source_target_pairs={{0,32},{8,488},{32,64},{40,8},{64,96},{72,40},{96,128},{104,72},{1... | collective-permute-start | bytes 995336 | tf_op jit(solution)/shard_map/ppermute | solution.py:44
  65.2 13.6 %collective-permute-start.4 = (bf16[120,1152]{1,0:T(8,128)(2,1)}, bf16[120,1152]{1,0:T(8,128)(2,1)S(1)}, u32[]{:S(2)}, u32[]{:S(2)}) collective-permute-start(bf16[120,1152]{1,0:T(8,128)(2,1)} %slice.14), channel_id=1, source_target_pairs={{0,64},{8,456},{32,96},{40,488},{64,128},{72,8},{96,160},{104,40},... | collective-permute-start | bytes 829448 | tf_op jit(solution)/shard_map/ppermute | solution.py:44
  68.1 20.0 %all-to-all-start.1 = ((bf16[16,24,1152]{2,1,0:T(8,128)(2,1)}), bf16[16,24,1152]{2,1,0:T(8,128)(2,1)S(1)}, u32[]{:S(2)}, u32[]{:S(2)}) async-start(bf16[16,24,1152]{2,1,0:T(8,128)(2,1)} %broadcast_in_dim.6), calls=%async_computation.1 | async-start | bytes 1769472 | tf_op jit(solution)/shard_map/all_to_all | solution.py:24
  78.8 9.3 %copy-start.1 = (bf16[120,1152]{1,0:T(8,128)(2,1)}, bf16[120,1152]{1,0:T(8,128)(2,1)S(1)}, u32[]{:S(2)}) copy-start(bf16[120,1152]{1,0:T(8,128)(2,1)S(1)} %collective-permute-done.4.refs_4_) | copy-start | bytes 829444
  79.8 8.3 %collective-permute-start.5 = (bf16[360,1152]{1,0:T(8,128)(2,1)}, bf16[360,1152]{1,0:T(8,128)(2,1)}, u32[]{:S(2)}, u32[]{:S(2)}) collective-permute-start(bf16[360,1152]{1,0:T(8,128)(2,1)} %pad_maximum_fusion.1), channel_id=1, source_target_pairs={{0,8},{8,0},{1,9},{9,1},{2,10},{10,2},{3,11},{11,3},{4,12},{12,4},... | collective-permute-start | bytes 2488328 | tf_op jit(solution)/shard_map/ppermute | solution.py:29
  88.0 1.0 copy-start.2
  89.0 0.9 copy-start.4
  89.9 0.9 copy-start.7
  95.4 0.9 copy-start.5
  96.4 0.9 copy-start.8
  97.3 24.8 %copy-start.17 = (bf16[24,1152]{1,0:T(8,128)(2,1)S(1)}, bf16[24,1152]{1,0:T(8,128)(2,1)}, u32[]{:S(2)}) copy-start(bf16[24,1152]{1,0:T(8,128)(2,1)} %copy-done.16) | copy-start | bytes 165892
  97.3 23.5 %all-to-all-start.2 = ((bf16[16,24,1152]{2,1,0:T(8,128)(2,1)}), bf16[16,24,1152]{2,1,0:T(8,128)(2,1)}, u32[]{:S(2)}, u32[]{:S(2)}) async-start(bf16[16,24,1152]{2,1,0:T(8,128)(2,1)} %bitcast.29), calls=%async_computation.2 | async-start | bytes 1769472 | tf_op jit(solution)/shard_map/all_to_all | solution.py:24
  103.0 24.3 %collective-permute-start.6 = (bf16[360,1152]{1,0:T(8,128)(2,1)}, bf16[360,1152]{1,0:T(8,128)(2,1)S(1)}, u32[]{:S(2)}, u32[]{:S(2)}) collective-permute-start(bf16[360,1152]{1,0:T(8,128)(2,1)} %copy-done.8), channel_id=1, source_target_pairs={{0,8},{8,0},{1,9},{9,1},{2,10},{10,2},{3,11},{11,3},{4,12},{12,4},... | collective-permute-start | bytes 2488328 | tf_op jit(solution)/shard_map/ppermute | solution.py:29
  123.1 9.5 %copy-start.19 = (f32[1152]{0:T(1024)S(1)}, f32[1152]{0:T(1024)}, u32[]{:S(2)}) copy-start(f32[1152]{0:T(1024)} %param.10) | copy-start | bytes 13828
  123.1 26.8 %all-to-all-start.3 = ((bf16[8,24,1152]{2,1,0:T(8,128)(2,1)}), bf16[8,24,1152]{2,1,0:T(8,128)(2,1)}, u32[]{:S(2)}, u32[]{:S(2)}) async-start(bf16[8,24,1152]{2,1,0:T(8,128)(2,1)} %broadcast_in_dim.7), calls=%async_computation.3 | async-start | bytes 884736 | tf_op jit(solution)/shard_map/all_to_all | solution.py:24
  127.3 5.3 %copy-start.9 = (bf16[1152,538]{0,1:T(8,128)(2,1)S(1)}, bf16[1152,538]{0,1:T(8,128)(2,1)}, u32[]{:S(2)}) copy-start(bf16[1152,538]{0,1:T(8,128)(2,1)} %param.11) | copy-start | bytes 3718660
  127.5 15.2 %collective-permute-start.7 = (bf16[144,1152]{1,0:T(8,128)(2,1)S(1)}, bf16[144,1152]{1,0:T(8,128)(2,1)S(1)}, u32[]{:S(2)}, u32[]{:S(2)}) collective-permute-start(bf16[144,1152]{1,0:T(8,128)(2,1)S(1)} %get-tuple-element.17), channel_id=1, source_target_pairs={{0,480},{8,40},{32,0},{40,72},{64,32},{72,104},{96,64},{104,136},{... | collective-permute-start | bytes 995336 | tf_op jit(solution)/shard_map/ppermute | solution.py:44
  130.4 12.3 %collective-permute-start.8 = (bf16[120,1152]{1,0:T(8,128)(2,1)S(1)}, bf16[120,1152]{1,0:T(8,128)(2,1)S(1)}, u32[]{:S(2)}, u32[]{:S(2)}) collective-permute-start(bf16[120,1152]{1,0:T(8,128)(2,1)S(1)} %get-tuple-element.18), channel_id=1, source_target_pairs={{0,448},{8,72},{32,480},{40,104},{64,0},{72,136},{96,32},{104,168}... | collective-permute-start | bytes 829448 | tf_op jit(solution)/shard_map/ppermute | solution.py:44
  143.5 15.3 %collective-permute-start.10 = (bf16[48,1152]{1,0:T(8,128)(2,1)}, bf16[48,1152]{1,0:T(8,128)(2,1)S(1)}, u32[]{:S(2)}, u32[]{:S(2)}) collective-permute-start(bf16[48,1152]{1,0:T(8,128)(2,1)} %get-tuple-element.21), channel_id=1, source_target_pairs={{0,320},{8,200},{32,352},{40,232},{64,384},{72,264},{96,416},{104,... | collective-permute-start | bytes 331784 | tf_op jit(solution)/shard_map/ppermute | solution.py:44
  145.4 18.7 %collective-permute-start.9 = (bf16[48,1152]{1,0:T(8,128)(2,1)}, bf16[48,1152]{1,0:T(8,128)(2,1)S(1)}, u32[]{:S(2)}, u32[]{:S(2)}) collective-permute-start(bf16[48,1152]{1,0:T(8,128)(2,1)} %get-tuple-element.20), channel_id=1, source_target_pairs={{0,416},{8,104},{32,448},{40,136},{64,480},{72,168},{96,0},{104,20... | collective-permute-start | bytes 331784 | tf_op jit(solution)/shard_map/ppermute | solution.py:44
  149.9 2.2 %copy-start.10 = (bf16[1152,538]{0,1:T(8,128)(2,1)S(1)}, bf16[1152,538]{0,1:T(8,128)(2,1)}, u32[]{:S(2)}) copy-start(bf16[1152,538]{0,1:T(8,128)(2,1)} %param.11) | copy-start | bytes 3718660
  152.1 15.2 %copy-start.14 = (bf16[24,1152]{1,0:T(8,128)(2,1)S(1)}, bf16[24,1152]{1,0:T(8,128)(2,1)}, u32[]{:S(2)}) copy-start(bf16[24,1152]{1,0:T(8,128)(2,1)} %copy-done.13) | copy-start | bytes 165892
  164.2 3.1 %collective-permute-start.11 = (bf16[24,1152]{1,0:T(8,128)(2,1)S(1)}, bf16[24,1152]{1,0:T(8,128)(2,1)S(1)}, u32[]{:S(2)}, u32[]{:S(2)}) collective-permute-start(bf16[24,1152]{1,0:T(8,128)(2,1)S(1)} %get-tuple-element.23), channel_id=1, source_target_pairs={{0,8},{8,0},{1,9},{9,1},{2,10},{10,2},{3,11},{11,3},{4,12},{12,4},... | collective-permute-start | bytes 165896 | tf_op jit(solution)/shard_map/ppermute | solution.py:29
  168.7 8.0 %copy-start.12 = (bf16[192,1152]{1,0:T(8,128)(2,1)S(1)}, bf16[192,1152]{1,0:T(8,128)(2,1)}, u32[]{:S(2)}) copy-start(bf16[192,1152]{1,0:T(8,128)(2,1)} %param.8) | copy-start | bytes 1327108
  168.7 21.9 %all-to-all-start.4 = ((bf16[8,448,128]{2,1,0:T(8,128)(2,1)}), bf16[8,448,128]{2,1,0:T(8,128)(2,1)S(1)}, u32[]{:S(2)}, u32[]{:S(2)}) async-start(bf16[8,448,128]{2,1,0:T(8,128)(2,1)} %shard_map.99), calls=%async_computation.4 | async-start | bytes 1835008 | tf_op jit(solution)/shard_map/all_to_all | solution.py:24
  190.6 0.9 copy-start.11
